TPU v7x, 512 devices: a whole 4x4x16 slice. The times are simulated.
512 devices in a mesh: seq: 64 (over z, x), head: 8 (over y, core).
Axes of the slice: x: 4, y: 4, z: 16, core: 2. Of those that a mesh axis runs over, the one named last changes fastest.
Arguments:
- x_proj: bfloat16 [16384, 8192], P(('seq', 'head')), may hold values from -6 to 6
- z_proj: bfloat16 [16384, 8192], P(('seq', 'head')), may hold values from -6 to 6
- b_proj: bfloat16 [16384, 1024], P(('seq', 'head')), may hold values from -6 to 6
- c_proj: bfloat16 [16384, 1024], P(('seq', 'head')), may hold values from -6 to 6
- dt_raw: bfloat16 [16384, 128], P(('seq', 'head')), may hold values from -3.2 to 3.2, as said below
- dt_bias: float32 [128], P('head'), may hold values from -6.3 to -1.2, as said below
- a_log: float32 [128], P('head'), as said below
- d_skip: float32 [128], P('head'), may hold values from 0.5 to 2
- conv_x: float32 [4, 8192], P(None, 'head'), may hold values from -3 to 3
- conv_bias_x: float32 [8192], P('head'), may hold values from -3 to 3
- conv_bc: float32 [4, 2, 1024], P(None, None, 'head'), may hold values from -3 to 3
- conv_bias_bc: float32 [2, 1024], P(None, 'head'), may hold values from -3 to 3
- norm_weight: float32 [8192], P('head'), may hold values from 0.25 to 1.75
- out_weight: bfloat16 [8192, 4096], P('head', 'seq'), may hold values from -0.0625 to 0.0625
Outputs:
- mixed: bfloat16 [16384, 4096], P(('seq', 'head'))
Inputs may be any that keep to these rules, and one draw needn't show every extreme that they name: `dt_raw`: A normal draw times 0.7 plus an offset common to each head and each aligned run of 256 tokens. `dt_bias`: the inverse softplus of a per-head step size between 0.002 and 0.25. Finite; exp(a_log) lies above 0.0 and at most 0.3.
All inputs are finite; a program needn't handle non-finite values.
Results may differ from a plain program's by a relative error of at most 0.014.
Values may be sent and summed in bfloat16 or wider, within the bound.
No kernel may reach another device: no remote copies, remote signals or barrier semaphores. Data moves between devices by JAX's collectives and lax.ppermute only.
A program may use at most 128 MiB of HBM per device.

v0:
```python
import jax
import jax.numpy as jnp
from jax import lax
from jax.sharding import Mesh
from jax.sharding import PartitionSpec as P

HEAD_DIM = 64
STATE = 128
GROUPS = 8
SPAN = 128
DI = 8192
SEQ = ("seq_0", "seq_1")
SEQ_HEAD = ("seq_0", "seq_1", "head")


def from_behind(array, axis, by):
    count = lax.axis_size(axis)
    pairs = [(i, i + by) for i in range(count) if 0 <= i + by < count]
    return lax.ppermute(array, axis, pairs)


def filled_with(array, identity):
    return jax.tree.map(
        lambda a, e: jnp.broadcast_to(jnp.asarray(e, a.dtype), a.shape), array, identity
    )


def entering(array, axes, combine, identity):
    before = start = filled_with(array, identity)
    total = array
    for axis in reversed(axes):
        count, mine = (lax.axis_size(axis), lax.axis_index(axis))
        pieces = jax.tree.map(lambda part: lax.all_gather(part, axis), total)
        inside, total = (start, start)
        for k in range(count):
            passed = k < mine
            total = combine(total, jax.tree.map(lambda part: part[k], pieces))
            inside = jax.tree.map(lambda new, old: jnp.where(passed, new, old), total, inside)
        before = combine(inside, before)
    return before


def split_up(array, dim, count):
    shape = array.shape
    pieces = array.reshape(*shape[:dim], count, shape[dim] // count, *shape[dim + 1 :])
    return jnp.moveaxis(pieces, dim, 0)


def sent_and_summed(array, axis, dim):
    count = lax.axis_size(axis)
    pieces = lax.all_to_all(split_up(array, dim, count), axis, 0, 0, tiled=True)
    return jnp.sum(pieces.astype(jnp.float32), axis=0)


def depthwise(current, previous, weight, bias_row):
    padded = jnp.concatenate([previous, current], axis=0).astype(jnp.float32)
    token_count = current.shape[0]
    summed = jnp.broadcast_to(bias_row, current.shape)
    for offset in range(weight.shape[0]):
        summed = summed + weight[offset] * padded[offset : offset + token_count]
    return jax.nn.silu(summed).astype(jnp.bfloat16)


def block_weights(c_blocks, b_blocks, cumulative, step_size, per_group):
    scores = jnp.einsum("ktgn,ksgn->kgts", c_blocks, b_blocks, preferred_element_type=jnp.float32)
    by_head = jnp.transpose(cumulative, (0, 2, 1))
    spread = by_head[:, :, :, None] - by_head[:, :, None, :]
    length = cumulative.shape[1]
    causal = jnp.arange(length)[:, None] >= jnp.arange(length)[None, :]
    decays = jnp.exp(jnp.where(causal, spread, -jnp.inf))
    scaled = decays * jnp.transpose(step_size, (0, 2, 1))[:, :, None, :]
    block_count = cumulative.shape[0]
    head_count = cumulative.shape[2]
    grouped = scaled.reshape(block_count, -1, per_group, length, length) * scores[:, :, None]
    return grouped.reshape(block_count, head_count, length, length).astype(jnp.bfloat16)


def combine_states(earlier, later):
    return (earlier[0] + later[0], jnp.exp(later[0])[:, None, None] * earlier[1] + later[1])


def per_device(
    x_proj,
    z_proj,
    b_proj,
    c_proj,
    dt_raw,
    dt_bias,
    a_log,
    d_skip,
    conv_x,
    conv_bias_x,
    conv_bc,
    conv_bias_bc,
    norm_weight,
    out_weight,
):
    x_heads, z_heads, b_heads, c_heads, dt_heads = (
        lax.all_to_all(x_proj, "head", split_axis=1, concat_axis=0, tiled=True),
        lax.all_to_all(z_proj, "head", split_axis=1, concat_axis=0, tiled=True),
        lax.all_to_all(b_proj, "head", split_axis=1, concat_axis=0, tiled=True),
        lax.all_to_all(c_proj, "head", split_axis=1, concat_axis=0, tiled=True),
        lax.all_to_all(dt_raw, "head", split_axis=1, concat_axis=0, tiled=True),
    )
    kernel_len = conv_x.shape[0]
    x_cols = x_heads.shape[1]
    bc_cols = b_heads.shape[1]
    last_rows = jnp.concatenate(
        [x_heads[-(kernel_len - 1) :], b_heads[-(kernel_len - 1) :], c_heads[-(kernel_len - 1) :]],
        axis=1,
    )
    before = from_behind(last_rows, SEQ, 1)
    x_conv = depthwise(x_heads, before[:, :x_cols], conv_x, conv_bias_x)
    b_conv = depthwise(
        b_heads, before[:, x_cols : x_cols + bc_cols], conv_bc[:, 0], conv_bias_bc[0]
    )
    c_conv = depthwise(c_heads, before[:, x_cols + bc_cols :], conv_bc[:, 1], conv_bias_bc[1])
    token_count = x_conv.shape[0]
    local_heads = dt_bias.shape[0]
    local_groups = bc_cols // STATE
    per_group = local_heads // local_groups
    blocks = token_count // SPAN
    x_blocks = x_conv.reshape(blocks, SPAN, local_heads, HEAD_DIM)
    b_blocks = b_conv.reshape(blocks, SPAN, local_groups, STATE)
    c_blocks = c_conv.reshape(blocks, SPAN, local_groups, STATE)
    step_size = jax.nn.softplus(dt_heads.astype(jnp.float32) + dt_bias).reshape(
        blocks, SPAN, local_heads
    )
    cumulative = jnp.cumsum(-jnp.exp(a_log) * step_size, axis=1)
    mix_weights = block_weights(c_blocks, b_blocks, cumulative, step_size, per_group)
    y_local = jnp.einsum(
        "khts,kshp->kthp", mix_weights, x_blocks, preferred_element_type=jnp.float32
    )
    state_scale = step_size * jnp.exp(cumulative[:, -1:, :] - cumulative)
    x_weighted = (x_blocks.astype(jnp.float32) * state_scale[:, :, :, None]).astype(jnp.bfloat16)
    x_grouped = x_weighted.reshape(blocks, SPAN, local_groups, per_group, HEAD_DIM)
    pieces = jnp.einsum(
        "ksgqp,ksgn->kgqpn", x_grouped, b_blocks, preferred_element_type=jnp.float32
    )
    pieces = pieces.reshape(blocks, local_heads, HEAD_DIM, STATE)
    totals = cumulative[:, -1, :]
    final_state = jnp.zeros((local_heads, HEAD_DIM, STATE), jnp.float32)
    for block_idx in range(blocks):
        final_state = jnp.exp(totals[block_idx])[:, None, None] * final_state + pieces[block_idx]
    log_total = jnp.sum(totals, axis=0)
    carried = entering(
        (log_total, final_state),
        SEQ,
        combine_states,
        (jnp.zeros_like(log_total), jnp.zeros_like(final_state)),
    )
    running = carried[1]
    start_list = []
    for block_idx in range(blocks):
        start_list.append(running.astype(jnp.bfloat16))
        running = jnp.exp(totals[block_idx])[:, None, None] * running + pieces[block_idx]
    start_states = jnp.stack(start_list).reshape(blocks, local_groups, per_group, HEAD_DIM, STATE)
    y_carry = jnp.einsum(
        "ktgn,kgqpn->ktgqp", c_blocks, start_states, preferred_element_type=jnp.float32
    )
    y_carry = (
        y_carry.reshape(blocks, SPAN, local_heads, HEAD_DIM) * jnp.exp(cumulative)[:, :, :, None]
    )
    outputs = y_local + y_carry + d_skip[:, None] * x_blocks.astype(jnp.float32)
    outputs = outputs.reshape(token_count, local_heads * HEAD_DIM)
    gated = outputs * jax.nn.silu(z_heads.astype(jnp.float32))
    grouped = gated.reshape(token_count, -1, DI // GROUPS)
    normed = grouped / jnp.sqrt(jnp.mean(grouped * grouped, axis=-1, keepdims=True) + 1.0)
    normed = (normed.reshape(token_count, -1) * norm_weight).astype(jnp.bfloat16)
    terms = jnp.dot(
        normed,
        lax.all_gather(out_weight, SEQ, axis=1, tiled=True),
        preferred_element_type=jnp.float32,
    )
    mixed = sent_and_summed(terms.astype(jnp.bfloat16), "head", 0)
    return mixed.astype(jnp.bfloat16)


def solution(mesh):
    split = Mesh(mesh.devices.reshape(16, 4, mesh.shape["head"]), ("seq_0", "seq_1", "head"))
    return jax.shard_map(
        per_device,
        mesh=split,
        in_specs=(
            P(SEQ_HEAD, None),
            P(SEQ_HEAD, None),
            P(SEQ_HEAD, None),
            P(SEQ_HEAD, None),
            P(SEQ_HEAD, None),
            P("head"),
            P("head"),
            P("head"),
            P(None, "head"),
            P("head"),
            P(None, None, "head"),
            P(None, "head"),
            P("head"),
            P("head", SEQ),
        ),
        out_specs=P(SEQ_HEAD, None),
        check_vma=False,
    )
```

profile of v0, /device:TPU:1, one launch (start us, length us, event | category | flops | bytes accessed | tf_op | source)
XLA Modules:
  0.0 415.9 jit_solution(11446474946781498572)
XLA Ops:
  8.1 10.0 %all-to-all-start.3 = ((bf16[8,2,256]{2,1,0:T(2,128)(2,1)}), bf16[8,2,256]{2,1,0:T(2,128)(2,1)S(1)}, u32[]{:S(2)}, u32[]{:S(2)}) async-start(bf16[8,2,256]{2,1,0:T(2,128)(2,1)} %reshape.437), calls=%async_computation.3 | async-start | bytes 16384 | tf_op jit(solution)/shard_map/all_to_all | solution.py:103
  18.7 1.5 copy_bitcast_fusion.2
  20.2 1.4 slice_bitcast_fusion.3
  21.6 1.3 slice_bitcast_fusion.4
  24.4 1.9 copy.87
  26.3 4.8 %all-to-all-start.1 = ((bf16[32,8,128]{2,0,1:T(8,128)(2,1)}), bf16[32,8,128]{2,0,1:T(8,128)(2,1)S(1)}, u32[]{:S(2)}, u32[]{:S(2)}) async-start(bf16[32,8,128]{2,0,1:T(8,128)(2,1)} %copy_bitcast_fusion.3), calls=%async_computation.1 | async-start | bytes 131072 | tf_op jit(solution)/shard_map/all_to_all | solution.py:101
  32.3 3.7 all-to-all-done.1
  36.0 4.0 all-to-all-start.2
  40.0 4.8 %all-to-all-done.2 = bf16[32,8,128]{2,0,1:T(8,128)(2,1)S(1)} async-done(((bf16[32,8,128]{2,0,1:T(8,128)(2,1)}), bf16[32,8,128]{2,0,1:T(8,128)(2,1)S(1)}, u32[]{:S(2)}, u32[]{:S(2)}) %all-to-all-start.2) | async-done | bytes 65568 | tf_op jit(solution)/shard_map/all_to_all | solution.py:102
  44.9 4.2 %all-to-all-start = ((bf16[32,8,1024]{2,0,1:T(8,128)(2,1)}), bf16[32,8,1024]{2,0,1:T(8,128)(2,1)S(1)}, u32[]{:S(2)}, u32[]{:S(2)}) async-start(bf16[32,8,1024]{2,0,1:T(8,128)(2,1)} %bitcast.167), calls=%async_computation | async-start | bytes 1048576 | tf_op jit(solution)/shard_map/all_to_all | solution.py:99
  49.7 8.7 %all-to-all-done = bf16[32,8,1024]{2,0,1:T(8,128)(2,1)S(1)} async-done(((bf16[32,8,1024]{2,0,1:T(8,128)(2,1)}), bf16[32,8,1024]{2,0,1:T(8,128)(2,1)S(1)}, u32[]{:S(2)}, u32[]{:S(2)}) %all-to-all-start) | async-done | bytes 524320 | tf_op jit(solution)/shard_map/all_to_all | solution.py:99
  58.5 1.3 collective-permute-start
  64.4 1.3 dynamic-slice
  66.7 7.7 %all-reduce = f32[64]{0:T(128)S(1)} all-reduce(f32[64]{0:T(128)S(1)} %dynamic-update-slice), channel_id=2, replica_groups=mesh['seq_0'=16,'seq_1'=4,'head'=8] {'seq_1'}, use_global_device_ids=true, to_apply=%add | all-reduce | flops 64 | bytes 512
  75.1 30.7 %all-gather.6.cloned.1.call-done = f32[4,16,64,128]{3,2,1,0:T(8,128)} async-done(((f32[1,16,64,128]{3,2,1,0:T(8,128)}), f32[4,16,64,128]{3,2,1,0:T(8,128)}) %all-gather.6.cloned.1.call-update) | async-done | bytes 2097168 | tf_op jit(solution)/shard_map/all_gather | solution.py:33
  105.8 2.5 slice_add_fusion.16
  110.0 5.1 %all-to-all-start.4 = ((bf16[32,8,1024]{2,0,1:T(8,128)(2,1)}), bf16[32,8,1024]{2,0,1:T(8,128)(2,1)S(1)}, u32[]{:S(2)}, u32[]{:S(2)}) async-start(bf16[32,8,1024]{2,0,1:T(8,128)(2,1)} %bitcast.166), calls=%async_computation.4 | async-start | bytes 1048576 | tf_op jit(solution)/shard_map/all_to_all | solution.py:100
  117.1 26.5 %all-gather.1 = f32[16,1,16]{2,1,0:T(1,128)S(1)} all-gather(f32[1,1,16]{2,1,0:T(1,128)S(1)} %get-tuple-element.7), channel_id=1, replica_groups=mesh['seq_0'=16,'seq_1'=4,'head'=8] {'seq_0'}, dimensions={0}, use_global_device_ids=true | all-gather | bytes 1088 | tf_op jit(solution)/shard_map/all_gather | solution.py:33
  145.1 1.1 convert_bitcast_fusion
  146.2 1.7 reshape.345
  148.0 1.9 copy.71
  150.9 3.1 convolution_bitcast_fusion.1
  153.9 60.6 %all-gather.8.cloned.1.call-done = f32[16,16,64,128]{3,2,1,0:T(8,128)} async-done(((f32[1,16,64,128]{3,2,1,0:T(8,128)}), f32[16,16,64,128]{3,2,1,0:T(8,128)}) %all-gather.8.cloned.1.call-update) | async-done | bytes 8388624 | tf_op jit(solution)/shard_map/all_gather | solution.py:33
  214.6 4.5 %fusion.60 = (bf16[1,16,64,128]{3,2,1,0:T(8,128)(2,1)S(1)}, f32[1,16,64,128]{3,2,1,0:T(8,128)S(1)}) fusion(pred[]{:T(512)S(6)} %gt.63, pred[]{:T(512)S(6)} %gt.62, f32[4,16,64,128]{3,2,1,0:T(8,128)S(1)} %copy-done.1, f32[16]{0:T(128)S(1)} %get-tuple-element.50, f32[16]{0:T(128)S(1)} %get-tuple-element.49, f32[16]{0:T(128)S(1)} %copy-done.12, pred[]{:T(512)S(6)} %gt.61, ...), kind=kLoop, calls=%fused_computation.164 | loop fusion | flops 7995392 | bytes 11273556 | tf_op jit(solution)/shard_map/convert_element_type | solution.py:155
  219.3 1.6 multiply_reduce_fusion
  220.9 2.2 copy.74
  223.1 1.6 reshape.435
  224.7 1.6 multiply_convert_fusion.2
  226.4 137.5 %all-gather.10.cloned.1.call-done = bf16[1024,4096]{0,1:T(8,128)(2,1)} async-done(((bf16[1024,64]{0,1:T(8,128)(2,1)}), bf16[1024,4096]{0,1:T(8,128)(2,1)}) %all-gather.10.cloned.1.call-update) | async-done | bytes 8388624 | tf_op jit(solution)/shard_map/all_gather | solution.py:172
  363.9 5.7 %convolution_convert_fusion = bf16[256,4096]{1,0:T(8,128)(2,1)S(1)} fusion(bf16[256,1024]{1,0:T(8,128)(2,1)S(1)} %multiply_convert_fusion.2, bf16[1024,4096]{0,1:T(8,128)(2,1)} %all-gather.10.cloned.1.call-done), kind=kOutput, calls=%fused_computation | convolution fusion | flops 2148532224 | bytes 11010048 | tf_op jit(solution)/shard_map/dot_general | solution.py:170
  369.6 38.7 %all_to_all.88 = bf16[8,32,4096]{2,1,0:T(8,128)(2,1)S(1)} all-to-all(bf16[8,32,4096]{2,1,0:T(8,128)(2,1)S(1)} %bitcast.172), channel_id=1, replica_groups=mesh['seq_0'=16,'seq_1'=4,'head'=8] {'head'}, dimensions={0} | all-to-all | bytes 4194304 | tf_op jit(solution)/shard_map/all_to_all | solution.py:51
  408.3 1.1 reduce_sum.32
  (90 shorter events, 17.3 us)
Async XLA Ops:
  6.5 11.6 %copy-start = (bf16[32,1024]{1,0:T(8,128)(2,1)S(1)}, bf16[32,1024]{1,0:T(8,128)(2,1)}, u32[]{:S(2)}) copy-start(bf16[32,1024]{1,0:T(8,128)(2,1)} %param.16) | copy-start | bytes 196612
  6.5 43.1 %copy-start.16 = (f32[16]{0:T(128)S(1)}, f32[16]{0:T(128)}, u32[]{:S(2)}) copy-start(f32[16]{0:T(128)} %param.19) | copy-start | bytes 196
  8.1 18.2 %all-to-all-start.3 = ((bf16[8,2,256]{2,1,0:T(2,128)(2,1)}), bf16[8,2,256]{2,1,0:T(2,128)(2,1)S(1)}, u32[]{:S(2)}, u32[]{:S(2)}) async-start(bf16[8,2,256]{2,1,0:T(2,128)(2,1)} %reshape.437), calls=%async_computation.3 | async-start | bytes 16384 | tf_op jit(solution)/shard_map/all_to_all | solution.py:103
  26.3 9.7 %all-to-all-start.1 = ((bf16[32,8,128]{2,0,1:T(8,128)(2,1)}), bf16[32,8,128]{2,0,1:T(8,128)(2,1)S(1)}, u32[]{:S(2)}, u32[]{:S(2)}) async-start(bf16[32,8,128]{2,0,1:T(8,128)(2,1)} %copy_bitcast_fusion.3), calls=%async_computation.1 | async-start | bytes 131072 | tf_op jit(solution)/shard_map/all_to_all | solution.py:101
  31.3 29.4 %copy-start.14 = (f32[1024]{0:T(1024)S(1)}, f32[1024]{0:T(1024)}, u32[]{:S(2)}) copy-start(f32[1024]{0:T(1024)} %param.23) | copy-start | bytes 12292
  36.0 8.9 %all-to-all-start.2 = ((bf16[32,8,128]{2,0,1:T(8,128)(2,1)}), bf16[32,8,128]{2,0,1:T(8,128)(2,1)S(1)}, u32[]{:S(2)}, u32[]{:S(2)}) async-start(bf16[32,8,128]{2,0,1:T(8,128)(2,1)} %copy_bitcast_fusion.2), calls=%async_computation.2 | async-start | bytes 131072 | tf_op jit(solution)/shard_map/all_to_all | solution.py:102
  44.9 13.6 %all-to-all-start = ((bf16[32,8,1024]{2,0,1:T(8,128)(2,1)}), bf16[32,8,1024]{2,0,1:T(8,128)(2,1)S(1)}, u32[]{:S(2)}, u32[]{:S(2)}) async-start(bf16[32,8,1024]{2,0,1:T(8,128)(2,1)} %bitcast.167), calls=%async_computation | async-start | bytes 1048576 | tf_op jit(solution)/shard_map/all_to_all | solution.py:99
  49.1 56.8 %all-gather.6.cloned.1.call-start = ((), (), s32[]{:S(2)}) async-start(), calls=%async_computation.6 | async-start | bytes 2621440 | tf_op jit(solution)/shard_map/all_gather | solution.py:33
  58.5 2.1 collective-permute-start
  62.9 1.4 copy-start.4
  64.4 44.7 %copy-start.7 = (bf16[32,8192]{1,0:T(8,128)(2,1)S(1)}, bf16[32,8192]{1,0:T(8,128)(2,1)}, u32[]{:S(2)}) copy-start(bf16[32,8192]{1,0:T(8,128)(2,1)} %param.15) | copy-start | bytes 1572868
  64.4 150.2 %all-gather.8.cloned.1.call-start = ((), (), s32[]{:S(2)}) async-start(), calls=%async_computation.7 | async-start | bytes 8912896 | tf_op jit(solution)/shard_map/all_gather | solution.py:33
  75.1 34.9 %copy-start.11 = (f32[16]{0:T(128)}, f32[16]{0:T(128)S(1)}, u32[]{:S(2)}) copy-start(f32[16]{0:T(128)S(1)} %get-tuple-element.52) | copy-start | bytes 196
  108.4 255.5 %all-gather.10.cloned.1.call-start = ((), (), s32[]{:S(2)}) async-start(), calls=%async_computation.8 | async-start | bytes 8519680 | tf_op jit(solution)/shard_map/all_gather | solution.py:172
  110.0 34.3 %all-to-all-start.4 = ((bf16[32,8,1024]{2,0,1:T(8,128)(2,1)}), bf16[32,8,1024]{2,0,1:T(8,128)(2,1)S(1)}, u32[]{:S(2)}, u32[]{:S(2)}) async-start(bf16[32,8,1024]{2,0,1:T(8,128)(2,1)} %bitcast.166), calls=%async_computation.4 | async-start | bytes 1048576 | tf_op jit(solution)/shard_map/all_to_all | solution.py:100
  144.3 0.8 copy-start.2
  147.9 2.9 copy-start.8
  147.9 2.9 copy-start.9
  147.9 2.9 copy-start.10
  150.6 63.9 %copy-start.1 = (f32[4,16,64,128]{3,2,1,0:T(8,128)S(1)}, f32[4,16,64,128]{3,2,1,0:T(8,128)}, u32[]{:S(2)}) copy-start(f32[4,16,64,128]{3,2,1,0:T(8,128)} %all-gather.6.cloned.1.call-done) | copy-start | bytes 6291460
  150.7 63.9 %copy-start.12 = (f32[16]{0:T(128)S(1)}, f32[16]{0:T(128)}, u32[]{:S(2)}) copy-start(f32[16]{0:T(128)} %copy-done.11) | copy-start | bytes 196
  214.6 4.6 %copy-start.15 = (f32[16]{0:T(128)S(1)}, f32[16]{0:T(128)}, u32[]{:S(2)}) copy-start(f32[16]{0:T(128)} %get-tuple-element.12) | copy-start | bytes 196
  214.6 4.7 %copy-start.5 = (bf16[2,128,16,64]{1,3,2,0:T(8,128)(2,1)S(1)}, bf16[2,128,16,64]{1,3,2,0:T(8,128)(2,1)}, u32[]{:S(2)}) copy-start(bf16[2,128,16,64]{1,3,2,0:T(8,128)(2,1)} %copy-done.4) | copy-start | bytes 1572868
  214.6 4.7 %copy-start.6 = (f32[2,128,16,64]{1,3,2,0:T(8,128)S(1)}, f32[2,128,16,64]{1,3,2,0:T(8,128)}, u32[]{:S(2)}) copy-start(f32[2,128,16,64]{1,3,2,0:T(8,128)} %copy.71) | copy-start | bytes 3145732
  214.6 4.7 %copy-start.17 = (f32[16]{0:T(128)S(1)}, f32[16]{0:T(128)}, u32[]{:S(2)}) copy-start(f32[16]{0:T(128)} %param.21) | copy-start | bytes 196
  214.6 4.7 %copy-start.18 = (f32[2,128,16,64]{1,3,2,0:T(8,128)S(1)}, f32[2,128,16,64]{1,3,2,0:T(8,128)}, u32[]{:S(2)}) copy-start(f32[2,128,16,64]{1,3,2,0:T(8,128)} %convolution_bitcast_fusion.1) | copy-start | bytes 3145732
  223.1 1.6 copy-start.3
  223.1 1.6 copy-start.13
Sparse Core Ops, SparseCore 0:
  64.5 41.2 all-gather.5
  108.5 106.0 all-gather.7
  217.5 146.3 all-gather.9
where the time goes:
time: 417 us; the launch traced here: 416 us
  waiting for transfers between devices  248 us (59%)
  blocking collectives  72.9 us (17%)
  starting transfers between devices  29.5 us (7%)
  local copies, waits for them, and re-layouts  23.4 us (6%)
  other arithmetic  17.4 us (4%)
  between operations  14.2 us (3%)
  matrix products  10.9 us (3%)
    all_gather x1, waiting for transfers between devices, per_device(): lax.all_gather(out_weight, SEQ, axis=1, tiled=True)  138 us
    all_gather x2, waiting for transfers between devices, entering(): pieces = jax.tree.map(lambda part: lax.all_gather(part, axis), total)  91.4 us
    all_to_all x1, blocking collectives, sent_and_summed(): pieces = lax.all_to_all(split_up(array, dim, count), axis, 0, 0, tiled=True)  38.7 us
    all_gather x1, blocking collectives, entering(): pieces = jax.tree.map(lambda part: lax.all_gather(part, axis), total)  26.5 us
    all_to_all x1, starting transfers between devices, per_device(): lax.all_to_all(dt_raw, 'head', split_axis=1, concat_axis=0, tiled=True)  10 us
    all_to_all x1, waiting for transfers between devices, per_device(): lax.all_to_all(x_proj, 'head', split_axis=1, concat_axis=0, tiled=True)  8.7 us
  transfers between devices with their start and end apart: 9, of which 7 were waited for; matrix products, arithmetic and copies ran while one was open for 9% of the time, Pallas kernels for 0%

commit v1 on v0

v1 whole, which is shorter than its diff:
```python
import jax
import jax.numpy as jnp
from jax import lax
from jax.experimental import pallas as pl
from jax.experimental.pallas import tpu as pltpu
from jax.sharding import Mesh
from jax.sharding import PartitionSpec as P

HEAD_DIM = 64
STATE = 128
SPAN = 128
LANES = 128
F32 = jnp.float32
BF16 = jnp.bfloat16
SEQ = ("z", "x")
HEAD = ("y", "c")
PLANE = ("x", "y", "c")
ALL = ("z", "x", "y", "c")
VMEM = pl.BlockSpec(memory_space=pltpu.VMEM)


def call(kernel, outs, inputs, scratch=(), flops=1 << 22, limit=16):
    return pl.pallas_call(
        kernel,
        out_shape=outs,
        in_specs=[VMEM] * len(inputs),
        out_specs=jax.tree.map(lambda _: VMEM, outs),
        scratch_shapes=list(scratch),
        compiler_params=pltpu.CompilerParams(vmem_limit_bytes=limit << 20),
        cost_estimate=pl.CostEstimate(flops=flops, bytes_accessed=1 << 20, transcendentals=0),
    )(*inputs)


def shape(dims, dtype):
    return jax.ShapeDtypeStruct(dims, dtype)


def silu(v):
    return v * (1.0 / (1.0 + jnp.exp(-v)))


def nt(a, b):
    return lax.dot_general(a, b, (((1,), (1,)), ((), ())), preferred_element_type=F32)


def tn(a, b):
    return lax.dot_general(a, b, (((0,), (0,)), ((), ())), preferred_element_type=F32)


def by_head(values, chunk, first):
    return jnp.where(first, values[:, 2 * chunk : 2 * chunk + 1], values[:, 2 * chunk + 1 : 2 * chunk + 2])


def left_half():
    return lax.broadcasted_iota(jnp.int32, (1, LANES), 1) < HEAD_DIM


def top_half():
    return lax.broadcasted_iota(jnp.int32, (LANES, 1), 0) < HEAD_DIM


def spread_out(out_ref, wide_ref, group_ref):
    count, _, _ = out_ref.shape
    groups = group_ref.shape[1] // LANES
    cols = wide_ref.shape[1] // count
    for d in range(count):
        part, group = divmod(d, groups)
        lo = (group * (count // groups) + part) * cols
        out_ref[d, :, :cols] = wide_ref[:, lo : lo + cols]
        out_ref[d, :, cols : cols + LANES] = group_ref[:, group * LANES : (group + 1) * LANES]


def pack_first(x_ref, b_ref, dt_ref, out_ref):
    spread_out(out_ref, x_ref, b_ref)
    count, _, width = out_ref.shape
    groups = b_ref.shape[1] // LANES
    heads = dt_ref.shape[1] // count
    dt = dt_ref[...].astype(F32)
    for d in range(count):
        part, group = divmod(d, groups)
        lo = (group * (count // groups) + part) * heads
        mine = dt if lo == 0 else pltpu.roll(dt, LANES - lo, 1)
        out_ref[d, :, width - LANES :] = mine.astype(BF16)


def pack_second(z_ref, c_ref, out_ref):
    spread_out(out_ref, z_ref, c_ref)


def steps(packed_ref, heads_ref, dt_ref, cum_ref, sum_ref):
    tokens = dt_ref.shape[0]
    rows = lax.broadcasted_iota(jnp.int32, (SPAN, SPAN), 0)
    cols = lax.broadcasted_iota(jnp.int32, (SPAN, SPAN), 1)
    ones = (rows >= cols).astype(F32)
    total = jnp.zeros((1, LANES), F32)
    for k in range(tokens // SPAN):
        part = slice(k * SPAN, (k + 1) * SPAN)
        raw = packed_ref[part, packed_ref.shape[1] - LANES :].astype(F32) + heads_ref[0:1]
        dt = jnp.maximum(raw, 0.0) + jnp.log1p(jnp.exp(-jnp.abs(raw)))
        dt_ref[part] = dt
        cum = lax.dot(
            ones, heads_ref[1:2] * dt, precision=lax.Precision.HIGHEST, preferred_element_type=F32
        )
        cum_ref[part] = cum
        sum_ref[part] = cum + total
        total = total + cum[SPAN - 1 :]


def fill_padded(padded, halo_ref, packed_ref, width):
    padded[:8] = halo_ref[:, :width].astype(F32)
    padded[8:] = packed_ref[:, :width].astype(F32)


def conv(padded, taps, bias, k, lo):
    first = 8 + k * SPAN - 3
    total = bias + taps[0] * padded[first : first + SPAN, lo : lo + LANES]
    for j in range(1, 4):
        total = total + taps[j] * padded[first + j : first + j + SPAN, lo : lo + LANES]
    return silu(total).astype(BF16)


def scan_in(
    packed_ref, halo_ref, taps_ref, group_taps_ref, dt_ref, cum_ref, sum_ref,
    xs_ref, b_ref, held_ref, sent_ref, padded,
):
    tokens, cols = xs_ref.shape
    blocks = tokens // SPAN
    fill_padded(padded, halo_ref, packed_ref, cols + LANES)
    left, top = left_half(), top_half()
    group_taps = [group_taps_ref[j : j + 1] for j in range(4)]
    states = [jnp.zeros((LANES, STATE), F32) for _ in range(cols // LANES)]
    for k in range(blocks):
        part = slice(k * SPAN, (k + 1) * SPAN)
        b = conv(padded, group_taps, group_taps_ref[4:5], k, cols)
        b_ref[part] = b
        cum = cum_ref[part]
        last = cum[SPAN - 1 :]
        scale = dt_ref[part] * jnp.exp(last - cum)
        decay = jnp.exp(last)
        for chunk in range(cols // LANES):
            lo = chunk * LANES
            taps = [taps_ref[j : j + 1, lo : lo + LANES] for j in range(4)]
            xs = conv(padded, taps, taps_ref[4:5, lo : lo + LANES], k, lo)
            xs_ref[part, lo : lo + LANES] = xs
            weighted = (xs.astype(F32) * by_head(scale, chunk, left)).astype(BF16)
            held_ref[k, lo : lo + LANES] = states[chunk].astype(BF16)
            states[chunk] = by_head(decay, chunk, top) * states[chunk] + tn(weighted, b)
    count, extra = sent_ref.shape[0], sent_ref.shape[1]
    rows = cols // count
    for chunk in range(cols // LANES):
        final = states[chunk].astype(BF16)
        for i in range(LANES // rows):
            sent_ref[chunk * (LANES // rows) + i, :rows] = final[i * rows : (i + 1) * rows]
    total = sum_ref[tokens - 1 :]
    high = total.astype(BF16).astype(F32)
    middle = (total - high).astype(BF16).astype(F32)
    low = total - high - middle
    at = lax.broadcasted_iota(jnp.int32, (extra - rows, LANES), 0)
    tail = jnp.where(at == 0, high, jnp.where(at == 1, middle, jnp.where(at == 2, low, 0.0)))
    for d in range(count):
        sent_ref[d, rows:] = tail.astype(BF16)


def scan_all(inbox_ref, starts_ref, decays):
    count, rows, _ = starts_ref.shape
    tail = inbox_ref[:, rows:].astype(F32)
    logs = tail[:, 0] + tail[:, 1] + tail[:, 2]
    lanes = lax.broadcasted_iota(jnp.int32, logs.shape, 1)
    head = lax.axis_index("z") * rows // HEAD_DIM
    column = jnp.sum(jnp.where(lanes == head, logs, 0.0), axis=1, keepdims=True)
    decays[...] = jnp.broadcast_to(jnp.exp(column), decays.shape)
    state = jnp.zeros((rows, STATE), F32)
    for i in range(count):
        starts_ref[i] = state.astype(BF16)
        state = decays[i : i + 1] * state + inbox_ref[i, :rows].astype(F32)


def local(
    xs_ref, b_ref, packed_ref, halo_ref, group_taps_ref, dt_ref, cum_ref, held_ref, heads_ref,
    c_ref, y_ref, padded,
):
    tokens, cols = xs_ref.shape
    padded[:8] = halo_ref[...].astype(F32)
    padded[8:] = packed_ref[:, cols:].astype(F32)
    rows = lax.broadcasted_iota(jnp.int32, (SPAN, SPAN), 0)
    lanes = lax.broadcasted_iota(jnp.int32, (SPAN, SPAN), 1)
    causal = rows >= lanes
    left = left_half()
    taps = [group_taps_ref[8 + j : 9 + j] for j in range(4)]
    for k in range(tokens // SPAN):
        part = slice(k * SPAN, (k + 1) * SPAN)
        c = conv(padded, taps, group_taps_ref[12:13], k, 0)
        c_ref[part] = c
        scores = nt(c, b_ref[part])
        cum = cum_ref[part]
        grown = jnp.exp(cum)
        cum_t = cum.T
        dt_t = dt_ref[part].T

        def mix(h):
            spread = cum[:, h : h + 1] - cum_t[h : h + 1]
            decays = jnp.exp(jnp.where(causal, spread, -jnp.inf))
            return (decays * dt_t[h : h + 1] * scores).astype(BF16)

        for chunk in range(cols // LANES):
            lo = chunk * LANES
            xs = xs_ref[part, lo : lo + LANES]
            y0 = jnp.dot(mix(2 * chunk), xs, preferred_element_type=F32)
            y1 = jnp.dot(mix(2 * chunk + 1), xs, preferred_element_type=F32)
            y = jnp.where(left, y0, y1) + by_head(heads_ref[2:3], chunk, left) * xs.astype(F32)
            if k > 0:
                y = y + nt(c, held_ref[k, lo : lo + LANES]) * by_head(grown, chunk, left)
            y_ref[part, lo : lo + LANES] = y


def finish(start_ref, c_ref, sum_ref, y_ref, packed_ref, theirs_ref, ours_ref):
    tokens, cols = y_ref.shape
    rows = tokens // 32
    left = left_half()
    first = lax.axis_index("c") == 0
    for k in range(tokens // SPAN):
        part = slice(k * SPAN, (k + 1) * SPAN)
        grown = jnp.exp(sum_ref[part])
        for chunk in range(cols // LANES):
            lo = chunk * LANES
            carry = nt(c_ref[part], start_ref[lo : lo + LANES]) * by_head(grown, chunk, left)
            z = packed_ref[part, lo : lo + LANES].astype(F32)
            gated = ((y_ref[part, lo : lo + LANES] + carry) * silu(z)).astype(BF16)
            for i in range(SPAN // (2 * rows)):
                even = gated[2 * i * rows : (2 * i + 1) * rows]
                odd = gated[(2 * i + 1) * rows : (2 * i + 2) * rows]
                at = k * (SPAN // 2) + i * rows
                theirs_ref[at : at + rows, lo : lo + LANES] = jnp.where(first, odd, even)
                ours_ref[at : at + rows, lo : lo + LANES] = jnp.where(first, even, odd)


def multiply(parts, weights_ref, out_ref, other_ref):
    rows, cols = parts[0].shape
    width = weights_ref.shape[1]
    me = lax.axis_index("x")
    step = 128
    for lo in range(0, rows, step):
        squares = jnp.zeros((step, 1), F32)
        total = jnp.zeros((step, weights_ref.shape[0]), F32)
        middle = rows // 2
        for i, offset in enumerate((0, 3, 1, 2)):
            at = pl.multiple_of(lax.rem(me + offset, 4) * cols, cols)
            if i < 3:
                gated = parts[i][lo : lo + step]
            elif lo < middle:
                gated = parts[3][lo : lo + step]
            else:
                gated = parts[4][lo - middle : lo - middle + step]
            total = total + nt(gated, weights_ref[:, pl.ds(at, cols)])
            value = gated.astype(F32)
            squares = squares + jnp.sum(value * value, axis=1, keepdims=True)
        total = total * (1.0 / jnp.sqrt(squares / width + 1.0))
        if other_ref is not None:
            total = total + other_ref[lo : lo + step].astype(F32)
        out_ref[lo : lo + step] = total.astype(BF16)


def stack(*refs):
    out_ref = refs[-1]
    at = 0
    for ref in refs[:-1]:
        out_ref[at : at + ref.shape[0]] = ref[...]
        at += ref.shape[0]


def project(own_ref, before_ref, after_ref, low_ref, high_ref, weights_ref, out_ref):
    multiply((own_ref, before_ref, after_ref, low_ref, high_ref), weights_ref, out_ref, None)


def project_add(own_ref, before_ref, after_ref, low_ref, high_ref, weights_ref, other_ref, out_ref):
    multiply((own_ref, before_ref, after_ref, low_ref, high_ref), weights_ref, out_ref, other_ref)


def tail(array_ref, out_ref):
    rows, cols = array_ref.shape
    out_ref[...] = array_ref[rows - out_ref.shape[0] :, cols - out_ref.shape[1] :]


def collect(shares_ref, out_ref, *, ys):
    count, _, width = shares_ref.shape
    xs = count // ys
    zs = width // HEAD_DIM
    me = lax.axis_index("z")
    left = left_half()
    order = ring_order(zs)
    for pair in range(width // LANES):
        lo = pair * LANES
        sums = []
        for i in range(xs):
            total = shares_ref[i * ys, :, lo : lo + LANES].astype(F32)
            for j in range(1, ys):
                total = total + shares_ref[i * ys + j, :, lo : lo + LANES].astype(F32)
            sums.append(total)
        rolled = [pltpu.roll(total, HEAD_DIM, 1) for total in sums]
        for side in range(2):
            z = lax.rem(me + order[2 * pair + side] + zs, zs)
            for i in range(0, xs, 2):
                if side == 0:
                    value = jnp.where(left, sums[i], rolled[i + 1])
                else:
                    value = jnp.where(left, rolled[i], sums[i + 1])
                at = pl.multiple_of(z * (xs * HEAD_DIM) + i * HEAD_DIM, LANES)
                out_ref[:, pl.ds(at, LANES)] = value.astype(BF16)


def ring_order(count):
    order = [0]
    for t in range(1, count // 2):
        order += [-t, t]
    return order + [count // 2]


def shift(array, axis, by, wrap=True):
    count = lax.axis_size(axis)
    pairs = [(i, (i + by) % count) for i in range(count) if wrap or 0 <= i + by < count]
    return lax.ppermute(array, axis, pairs)


class Ring:
    def __init__(self, block):
        self.blocks = [block]
        self.up = self.down = block
        self.t = 0
        self.half = lax.axis_size("z") // 2

    def step(self):
        self.t += 1
        self.move()

    def move(self):
        if self.t < self.half:
            self.up = shift(self.up, "z", 1)
            self.down = shift(self.down, "z", -1)
            self.blocks += [self.up, self.down]
        elif self.t == self.half:
            self.blocks += [shift(self.up, "z", 1)]

    def tie(self, value):
        value, self.up, self.down = lax.optimization_barrier((value, self.up, self.down))
        if self.t and self.t < self.half:
            self.blocks[-2:] = [self.up, self.down]
        return value


def sent(array, axes):
    return lax.all_to_all(array, axes, 0, 0, tiled=True)


def gather_x(block):
    before = shift(block, "x", 1)
    after = shift(block, "x", -1)
    middle = block.shape[0] // 2
    across = (shift(before[:middle], "x", 1), shift(after[middle:], "x", -1))
    return block, before, after, *across


def per_device(
    x_proj, z_proj, b_proj, c_proj, dt_raw, dt_bias, a_log, d_skip,
    conv_x, conv_bias_x, conv_bc, conv_bias_bc, norm_weight, out_weight,
):
    xs, ys, cs = (lax.axis_size(a) for a in PLANE)
    zs = lax.axis_size("z")
    plane = xs * ys * cs
    rows, inner = x_proj.shape
    cols = inner // plane
    tokens = rows * plane
    part = lax.axis_index("x")
    heads = dt_bias.shape[0] // xs

    def own(values, axis):
        size = values.shape[axis] // xs
        return lax.dynamic_slice_in_dim(values, part * size, size, axis)

    ring = Ring((out_weight.T.astype(F32) * norm_weight[None]).astype(BF16))
    first_out = call(
        pack_first, shape((plane, rows, cols + 2 * LANES), BF16), (x_proj, b_proj, dt_raw)
    )
    first_out = ring.tie(first_out)
    first_in = sent(first_out, PLANE)
    ring.step()
    ring.step()
    second_out = call(pack_second, shape((plane, rows, cols + LANES), BF16), (z_proj, c_proj))
    per_head = jnp.stack([own(dt_bias, 0), own(-jnp.exp(a_log), 0), own(d_skip, 0)])
    per_head = jnp.pad(per_head, ((0, 5), (0, LANES - heads)))
    taps = jnp.pad(jnp.concatenate([own(conv_x, 1), own(conv_bias_x, 0)[None]]), ((0, 3), (0, 0)))
    group_taps = jnp.pad(
        jnp.concatenate([jnp.moveaxis(conv_bc, 0, 1), conv_bias_bc[:, None]], axis=1),
        ((0, 0), (0, 3), (0, 0)),
    ).reshape(16, LANES)
    first_in, second_out, per_head, taps, group_taps = ring.tie(
        (first_in, second_out, per_head, taps, group_taps)
    )
    packed = first_in.reshape(tokens, cols + 2 * LANES)
    halo = call(tail, shape((8, cols + 2 * LANES), BF16), (packed,), (), 1 << 16, 4)
    halo = shift(halo, "z", 1, wrap=False)
    second = sent(second_out, PLANE).reshape(tokens, cols + LANES)
    lanes = shape((tokens, LANES), F32)
    dt, cum, sums = call(steps, (lanes, lanes, lanes), (packed, per_head))
    x_conv, b_conv, held, states_out = call(
        scan_in,
        (
            shape((tokens, cols), BF16),
            shape((tokens, LANES), BF16),
            shape((tokens // SPAN, cols, STATE), BF16),
            shape((zs, cols // zs + 8, STATE), BF16),
        ),
        (packed, halo, taps, group_taps, dt, cum, sums),
        [pltpu.VMEM((tokens + 8, cols + LANES), F32)],
        1 << 25,
    )
    states_out, second = ring.tie((states_out, second))
    states_in = sent(states_out, "z")
    c_halo = call(tail, shape((8, LANES), BF16), (second,), (), 1 << 16, 4)
    c_halo = shift(c_halo, "z", 1, wrap=False)
    ring.step()
    ring.step()
    ring.step()
    states_in = ring.tie(states_in)
    starts = call(
        scan_all,
        shape((zs, cols // zs, STATE), BF16),
        (states_in,),
        [pltpu.VMEM((zs, LANES), F32)],
    )
    starts = ring.tie(starts)
    start = sent(starts, "z").reshape(cols, STATE)
    ring.step()
    ring.step()
    ring.step()
    c_conv, y = call(
        local,
        (shape((tokens, LANES), BF16), shape((tokens, cols), F32)),
        (x_conv, b_conv, second, c_halo, group_taps, dt, cum, held, per_head),
        [pltpu.VMEM((tokens + 8, LANES), F32)],
        1 << 27,
    )
    width = sum(block.shape[0] for block in ring.blocks)
    weights = call(stack, shape((width, inner // (ys * cs)), BF16), tuple(ring.blocks), (), 1 << 22, 8)
    start, weights = lax.optimization_barrier((start, weights))
    half = shape((tokens // 2, cols), BF16)
    theirs, ours = call(finish, (half, half), (start, c_conv, sums, y, second), (), 1 << 25)
    product = shape((tokens // 2, weights.shape[0]), BF16)
    theirs = gather_x(theirs)
    ours = gather_x(ours)
    away = call(project, product, (*theirs, weights), (), 1 << 29, 24)
    other = shift(away, "c", 1)
    both = call(project_add, product, (*ours, weights, other), (), 1 << 29, 24)
    shares = sent(both.reshape(xs * ys, rows, weights.shape[0]), ("x", "y"))

    def collect_all(shares_ref, out_ref):
        collect(shares_ref, out_ref, ys=ys)

    return call(collect_all, shape((rows, xs * weights.shape[0]), BF16), (shares,))


def solution(mesh):
    split = Mesh(mesh.devices.reshape(16, 4, 4, 2), ALL)
    return jax.shard_map(
        per_device,
        mesh=split,
        in_specs=(
            P(ALL, None),
            P(ALL, None),
            P(ALL, None),
            P(ALL, None),
            P(ALL, None),
            P(HEAD),
            P(HEAD),
            P(HEAD),
            P(None, HEAD),
            P(HEAD),
            P(None, None, HEAD),
            P(None, HEAD),
            P(HEAD),
            P(HEAD, SEQ),
        ),
        out_specs=P(ALL, None),
        check_vma=False,
    )
```

time: 417 us -> 222 us (0.53)
  waiting for transfers between devices: 248 us -> 30.7 us
  starting transfers between devices: 29.5 us -> 126 us
  blocking collectives: 72.9 us -> 18.9 us
  Pallas kernels: 0 us -> 17.9 us
  other arithmetic: 17.4 us -> 2.22 us
  between operations: 14.2 us -> 0.77 us
  matrix products: 10.9 us -> 0 us
    all_gather x3 -> x0, waiting for transfers between devices: 229 us -> none  [the longest x1 138 us: per_device(): lax.all_gather(out_weight, SEQ, axis=1, tiled=True)]
    ppermute x1 -> x26, starting transfers between devices: 1.29 us -> 89.5 us  [shift(): return lax.ppermute(array, axis, pairs)]
    all_gather x1 -> x0, blocking collectives: 26.5 us -> none  [entering(): pieces = jax.tree.map(lambda part: lax.all_gather(part, axis), total)]
    ppermute x1 -> x26, waiting for transfers between devices: 0.72 us -> 25.8 us  [shift(): return lax.ppermute(array, axis, pairs)]
    all_to_all x1, blocking collectives: 38.7 us -> 18.9 us  [sent(): return lax.all_to_all(array, axes, 0, 0, tiled=True)]
    pallas_call x0 -> x13, Pallas kernels: none -> 17.9 us  [call(): pl.pallas_call(kernel, out_shape=outs, in_specs=[VMEM] * len(inputs), out...]
    unnamed x44 -> x99, local copies, waits for them, and re-layouts: 4.08 us -> 20.1 us
    all_to_all x5 -> x4, waiting for transfers between devices: 17.2 us -> 4.86 us  [sent(): return lax.all_to_all(array, axes, 0, 0, tiled=True)]
  transfers between devices with their start and end apart: 9 -> 30, of which waited for: 7 -> 13; matrix products, arithmetic and copies ran while one was open for 9% -> 1% of each run, Pallas kernels for 0% -> 4%
where the time goes in v1:
time: 222 us; the launch traced here: 218 us
  starting transfers between devices  126 us (57%)
  waiting for transfers between devices  30.7 us (14%)
  local copies, waits for them, and re-layouts  21.7 us (10%)
  blocking collectives  18.9 us (9%)
  Pallas kernels  17.9 us (8%)
  other arithmetic  2.22 us (1%)
    ppermute x26, starting transfers between devices, shift(): return lax.ppermute(array, axis, pairs)  89.5 us
    all_to_all x4, starting transfers between devices, sent(): return lax.all_to_all(array, axes, 0, 0, tiled=True)  36.4 us
    ppermute x26, waiting for transfers between devices, shift(): return lax.ppermute(array, axis, pairs)  25.8 us
    unnamed x99, local copies, waits for them, and re-layouts  20.1 us
    all_to_all x1, blocking collectives, sent(): return lax.all_to_all(array, axes, 0, 0, tiled=True)  18.9 us
    pallas_call x13, Pallas kernels, call(): pl.pallas_call(kernel, out_shape=outs, in_specs=[VMEM] * len(inputs), out...  17.9 us
    all_to_all x4, waiting for transfers between devices, sent(): return lax.all_to_all(array, axes, 0, 0, tiled=True)  4.86 us
  transfers between devices with their start and end apart: 30, of which 13 were waited for; matrix products, arithmetic and copies ran while one was open for 1% of the time, Pallas kernels for 4%

profile of v1, /device:TPU:1, one launch (start us, length us, event | category | flops | bytes accessed | tf_op | source)
XLA Modules:
  0.0 218.1 jit_solution(4674076702660301521)
XLA Ops:
  4.7 10.4 %all-to-all-start = ((bf16[32,32,512]{2,1,0:T(8,128)(2,1)}), bf16[32,32,512]{2,1,0:T(8,128)(2,1)S(1)}, u32[]{:S(2)}, u32[]{:S(2)}) async-start(bf16[32,32,512]{2,1,0:T(8,128)(2,1)} %shard_map.136), calls=%async_computation | async-start | bytes 2097152 | tf_op jit(solution)/shard_map/all_to_all | solution.py:351
  15.2 1.9 collective-permute-start
  17.1 9.3 %collective-permute-start.2 = (bf16[64,1024]{1,0:T(8,128)(2,1)S(1)}, bf16[64,1024]{1,0:T(8,128)(2,1)S(1)}, u32[]{:S(2)}, u32[]{:S(2)}) collective-permute-start(bf16[64,1024]{1,0:T(8,128)(2,1)S(1)} %fusion.refs_0_), channel_id=1, source_target_pairs={{0,480},{32,0},{64,32},{96,64},{128,96},{160,128},{192,160},{224,1... | collective-permute-start | bytes 393224 | tf_op jit(solution)/shard_map/ppermute | solution.py:321
  30.0 4.6 %collective-permute-start.3 = (bf16[64,1024]{1,0:T(8,128)(2,1)S(1)}, bf16[64,1024]{1,0:T(8,128)(2,1)S(1)}, u32[]{:S(2)}, u32[]{:S(2)}) collective-permute-start(bf16[64,1024]{1,0:T(8,128)(2,1)S(1)} %collective-permute-done.2.refs_2_), channel_id=1, source_target_pairs={{0,480},{32,0},{64,32},{96,64},{128,96},{160,128},{192,160},{224,1... | collective-permute-start | bytes 393224 | tf_op jit(solution)/shard_map/ppermute | solution.py:321
  38.2 8.4 %all-to-all-start.1 = ((bf16[32,32,384]{2,1,0:T(8,128)(2,1)}), bf16[32,32,384]{2,1,0:T(8,128)(2,1)S(1)}, u32[]{:S(2)}, u32[]{:S(2)}) async-start(bf16[32,32,384]{2,1,0:T(8,128)(2,1)} %shard_map.137), calls=%async_computation.1 | async-start | bytes 1572864 | tf_op jit(solution)/shard_map/all_to_all | solution.py:351
  50.1 3.0 %shard_map.140 = (bf16[1024,256]{1,0:T(8,128)(2,1)S(1)}, bf16[1024,128]{1,0:T(8,128)(2,1)S(1)}, bf16[8,256,128]{2,1,0:T(8,128)(2,1)S(1)}, bf16[16,24,128]{2,1,0:T(8,128)(2,1)S(1)}) custom-call(bf16[1024,512]{1,0:T(8,128)(2,1)S(1)} %bitcast.19, bf16[8,512]{1,0:T(8,128)(2,1)S(1)} %collective-permute-done.4.halo_ref, f32[8,256]{1,0:T(8,128)S(1)} %copy-done.42, ...), custom_call_target="tpu_custom_call" | custom-call | flops 33554432 | bytes 1048576 | tf_op jit(solution)/shard_map/pallas_call | solution.py:23
  56.0 4.9 %all-to-all-done.1 = bf16[32,32,384]{2,1,0:T(8,128)(2,1)S(1)} async-done(((bf16[32,32,384]{2,1,0:T(8,128)(2,1)}), bf16[32,32,384]{2,1,0:T(8,128)(2,1)S(1)}, u32[]{:S(2)}, u32[]{:S(2)}) %all-to-all-start.1) | async-done | bytes 786464 | tf_op jit(solution)/shard_map/all_to_all | solution.py:351
  62.7 4.8 %collective-permute-start.8 = (bf16[64,1024]{1,0:T(8,128)(2,1)}, bf16[64,1024]{1,0:T(8,128)(2,1)S(1)}, u32[]{:S(2)}, u32[]{:S(2)}) collective-permute-start(bf16[64,1024]{1,0:T(8,128)(2,1)} %copy-done.19), channel_id=1, source_target_pairs={{0,480},{32,0},{64,32},{96,64},{128,96},{160,128},{192,160},{224,1... | collective-permute-start | bytes 393224 | tf_op jit(solution)/shard_map/ppermute | solution.py:321
  67.6 8.4 %all-to-all-start.2 = ((bf16[16,24,128]{2,1,0:T(8,128)(2,1)}), bf16[16,24,128]{2,1,0:T(8,128)(2,1)S(1)}, u32[]{:S(2)}, u32[]{:S(2)}) async-start(bf16[16,24,128]{2,1,0:T(8,128)(2,1)} %copy-done.35), calls=%async_computation.2 | async-start | bytes 196608 | tf_op jit(solution)/shard_map/all_to_all | solution.py:351
  76.0 3.3 %collective-permute-start.6 = (bf16[64,1024]{1,0:T(8,128)(2,1)S(1)}, bf16[64,1024]{1,0:T(8,128)(2,1)S(1)}, u32[]{:S(2)}, u32[]{:S(2)}) collective-permute-start(bf16[64,1024]{1,0:T(8,128)(2,1)S(1)} %collective-permute-done.5.refs_5_), channel_id=1, source_target_pairs={{0,32},{32,64},{64,96},{96,128},{128,160},{160,192},{192,224},{224... | collective-permute-start | bytes 393224 | tf_op jit(solution)/shard_map/ppermute | solution.py:321
  79.9 3.2 %collective-permute-start.9 = (bf16[64,1024]{1,0:T(8,128)(2,1)S(1)}, bf16[64,1024]{1,0:T(8,128)(2,1)S(1)}, u32[]{:S(2)}, u32[]{:S(2)}) collective-permute-start(bf16[64,1024]{1,0:T(8,128)(2,1)S(1)} %collective-permute-done.8.refs_6_), channel_id=1, source_target_pairs={{0,480},{32,0},{64,32},{96,64},{128,96},{160,128},{192,160},{224,1... | collective-permute-start | bytes 393224 | tf_op jit(solution)/shard_map/ppermute | solution.py:321
  83.1 3.8 %collective-permute-done.6.refs_7_ = bf16[64,1024]{1,0:T(8,128)(2,1)S(1)} collective-permute-done((bf16[64,1024]{1,0:T(8,128)(2,1)S(1)}, bf16[64,1024]{1,0:T(8,128)(2,1)S(1)}, u32[]{:S(2)}, u32[]{:S(2)}) %collective-permute-start.6) | collective-permute-done | bytes 131104 | tf_op jit(solution)/shard_map/ppermute | solution.py:321
  88.8 4.6 %collective-permute-start.10 = (bf16[64,1024]{1,0:T(8,128)(2,1)S(1)}, bf16[64,1024]{1,0:T(8,128)(2,1)S(1)}, u32[]{:S(2)}, u32[]{:S(2)}) collective-permute-start(bf16[64,1024]{1,0:T(8,128)(2,1)S(1)} %collective-permute-done.9.refs_8_), channel_id=1, source_target_pairs={{0,480},{32,0},{64,32},{96,64},{128,96},{160,128},{192,160},{224,1... | collective-permute-start | bytes 393224 | tf_op jit(solution)/shard_map/ppermute | solution.py:321
  98.0 5.4 %collective-permute-start.12 = (bf16[64,1024]{1,0:T(8,128)(2,1)S(1)}, bf16[64,1024]{1,0:T(8,128)(2,1)}, u32[]{:S(2)}, u32[]{:S(2)}) collective-permute-start(bf16[64,1024]{1,0:T(8,128)(2,1)S(1)} %collective-permute-done.10.refs_10_), channel_id=1, source_target_pairs={{0,480},{32,0},{64,32},{96,64},{128,96},{160,128},{192,160},{224,1... | collective-permute-start | bytes 393224 | tf_op jit(solution)/shard_map/ppermute | solution.py:321
  105.7 9.3 %all-to-all-start.3 = ((bf16[16,16,128]{2,1,0:T(8,128)(2,1)}), bf16[16,16,128]{2,1,0:T(8,128)(2,1)}, u32[]{:S(2)}, u32[]{:S(2)}) async-start(bf16[16,16,128]{2,1,0:T(8,128)(2,1)} %shard_map.141), calls=%async_computation.3 | async-start | bytes 131072 | tf_op jit(solution)/shard_map/all_to_all | solution.py:351
  115.0 4.6 %collective-permute-start.14 = (bf16[64,1024]{1,0:T(8,128)(2,1)}, bf16[64,1024]{1,0:T(8,128)(2,1)S(1)}, u32[]{:S(2)}, u32[]{:S(2)}) collective-permute-start(bf16[64,1024]{1,0:T(8,128)(2,1)} %collective-permute-done.12.refs_12_), channel_id=1, source_target_pairs={{0,480},{32,0},{64,32},{96,64},{128,96},{160,128},{192,160},{224,1... | collective-permute-start | bytes 393224 | tf_op jit(solution)/shard_map/ppermute | solution.py:321
  121.5 2.1 collective-permute-start.16
  128.9 1.9 shard_map.144
  141.0 2.4 %collective-permute-start.22 = (bf16[512,256]{1,0:T(8,128)(2,1)S(1)}, bf16[512,256]{1,0:T(8,128)(2,1)S(1)}, u32[]{:S(2)}, u32[]{:S(2)}) collective-permute-start(bf16[512,256]{1,0:T(8,128)(2,1)S(1)} %get-tuple-element.70.own_ref), channel_id=1, source_target_pairs={{0,24},{8,0},{16,8},{24,16},{1,25},{9,1},{17,9},{25,17},{2,26},{10... | collective-permute-start | bytes 786440 | tf_op jit(solution)/shard_map/ppermute | solution.py:321
  143.4 2.9 %collective-permute-start.21 = (bf16[512,256]{1,0:T(8,128)(2,1)S(1)}, bf16[512,256]{1,0:T(8,128)(2,1)S(1)}, u32[]{:S(2)}, u32[]{:S(2)}) collective-permute-start(bf16[512,256]{1,0:T(8,128)(2,1)S(1)} %get-tuple-element.70.own_ref), channel_id=1, source_target_pairs={{0,8},{8,16},{16,24},{24,0},{1,9},{9,17},{17,25},{25,1},{2,10},{10... | collective-permute-start | bytes 786440 | tf_op jit(solution)/shard_map/ppermute | solution.py:321
  148.2 3.6 %collective-permute-start.24 = (bf16[256,256]{1,0:T(8,128)(2,1)S(1)}, bf16[256,256]{1,0:T(8,128)(2,1)S(1)}, u32[]{:S(2)}, u32[]{:S(2)}) collective-permute-start(bf16[256,256]{1,0:T(8,128)(2,1)S(1)} %slice.19), channel_id=1, source_target_pairs={{0,24},{8,0},{16,8},{24,16},{1,25},{9,1},{17,9},{25,17},{2,26},{10... | collective-permute-start | bytes 393224 | tf_op jit(solution)/shard_map/ppermute | solution.py:321
  151.8 2.1 collective-permute-start.23
  155.6 4.8 %collective-permute-done.23.low_ref = bf16[256,256]{1,0:T(8,128)(2,1)S(1)} collective-permute-done((bf16[256,256]{1,0:T(8,128)(2,1)S(1)}, bf16[256,256]{1,0:T(8,128)(2,1)S(1)}, u32[]{:S(2)}, u32[]{:S(2)}) %collective-permute-start.23) | collective-permute-done | bytes 131104 | tf_op jit(solution)/shard_map/ppermute | solution.py:321
  160.4 2.9 %shard_map.146 = bf16[512,1024]{1,0:T(8,128)(2,1)S(1)} custom-call(bf16[512,256]{1,0:T(8,128)(2,1)S(1)} %get-tuple-element.70.own_ref, bf16[512,256]{1,0:T(8,128)(2,1)S(1)} %collective-permute-done.21.before_ref, bf16[512,256]{1,0:T(8,128)(2,1)S(1)} %collective-permute-done.22.after_ref, bf16[256,256]{1,0:T(8,128)(2,1)S(1)} %collective-permute-done.23.low_ref, ...), custom_call_target="tpu_custom_call" | custom-call | flops 536870912 | bytes 1048576 | tf_op jit(solution)/shard_map/pallas_call | solution.py:23
  163.3 11.5 %collective-permute-start.25 = (bf16[512,1024]{1,0:T(8,128)(2,1)S(1)}, bf16[512,1024]{1,0:T(8,128)(2,1)S(1)}, u32[]{:S(2)}, u32[]{:S(2)}) collective-permute-start(bf16[512,1024]{1,0:T(8,128)(2,1)S(1)} %shard_map.146), channel_id=1, source_target_pairs={{0,1},{1,0},{2,3},{3,2},{4,5},{5,4},{6,7},{7,6},{8,9},{9,8},{10,11... | collective-permute-start | bytes 3145736 | tf_op jit(solution)/shard_map/ppermute | solution.py:321
  174.8 1.9 collective-permute-start.18
  176.8 3.4 %collective-permute-start.17 = (bf16[512,256]{1,0:T(8,128)(2,1)S(1)}, bf16[512,256]{1,0:T(8,128)(2,1)S(1)}, u32[]{:S(2)}, u32[]{:S(2)}) collective-permute-start(bf16[512,256]{1,0:T(8,128)(2,1)S(1)} %get-tuple-element.68.own_ref), channel_id=1, source_target_pairs={{0,8},{8,16},{16,24},{24,0},{1,9},{9,17},{17,25},{25,1},{2,10},{10... | collective-permute-start | bytes 786440 | tf_op jit(solution)/shard_map/ppermute | solution.py:321
  180.1 4.4 %collective-permute-done.18.after_ref = bf16[512,256]{1,0:T(8,128)(2,1)S(1)} collective-permute-done((bf16[512,256]{1,0:T(8,128)(2,1)S(1)}, bf16[512,256]{1,0:T(8,128)(2,1)S(1)}, u32[]{:S(2)}, u32[]{:S(2)}) %collective-permute-start.18) | collective-permute-done | bytes 262176 | tf_op jit(solution)/shard_map/ppermute | solution.py:321
  184.6 3.4 %collective-permute-start.20 = (bf16[256,256]{1,0:T(8,128)(2,1)S(1)}, bf16[256,256]{1,0:T(8,128)(2,1)S(1)}, u32[]{:S(2)}, u32[]{:S(2)}) collective-permute-start(bf16[256,256]{1,0:T(8,128)(2,1)S(1)} %slice.17), channel_id=1, source_target_pairs={{0,24},{8,0},{16,8},{24,16},{1,25},{9,1},{17,9},{25,17},{2,26},{10... | collective-permute-start | bytes 393224 | tf_op jit(solution)/shard_map/ppermute | solution.py:321
  190.7 4.7 %collective-permute-done.19.low_ref = bf16[256,256]{1,0:T(8,128)(2,1)S(1)} collective-permute-done((bf16[256,256]{1,0:T(8,128)(2,1)S(1)}, bf16[256,256]{1,0:T(8,128)(2,1)S(1)}, u32[]{:S(2)}, u32[]{:S(2)}) %collective-permute-start.19) | collective-permute-done | bytes 131104 | tf_op jit(solution)/shard_map/ppermute | solution.py:321
  195.3 2.9 %shard_map.147 = bf16[512,1024]{1,0:T(8,128)(2,1)S(1)} custom-call(bf16[512,256]{1,0:T(8,128)(2,1)S(1)} %get-tuple-element.68.own_ref, bf16[512,256]{1,0:T(8,128)(2,1)S(1)} %collective-permute-done.17.before_ref, bf16[512,256]{1,0:T(8,128)(2,1)S(1)} %collective-permute-done.18.after_ref, bf16[256,256]{1,0:T(8,128)(2,1)S(1)} %collective-permute-done.19.low_ref, ...), custom_call_target="tpu_custom_call" | custom-call | flops 536870912 | bytes 1048576 | tf_op jit(solution)/shard_map/pallas_call | solution.py:23
  198.2 18.9 %all_to_all.25.shares_ref = bf16[16,32,1024]{2,1,0:T(8,128)(2,1)S(1)} all-to-all(bf16[16,32,1024]{2,1,0:T(8,128)(2,1)S(1)} %bitcast.23), channel_id=1, replica_groups=mesh['z'=16,'x'=4,'y'=4,'c'=2] {'x','y'}, dimensions={0} | all-to-all | bytes 2097152 | tf_op jit(solution)/shard_map/all_to_all | solution.py:351
  (155 shorter events, 53.9 us)
Async XLA Ops:
  4.7 32.8 %all-to-all-start = ((bf16[32,32,512]{2,1,0:T(8,128)(2,1)}), bf16[32,32,512]{2,1,0:T(8,128)(2,1)S(1)}, u32[]{:S(2)}, u32[]{:S(2)}) async-start(bf16[32,32,512]{2,1,0:T(8,128)(2,1)} %shard_map.136), calls=%async_computation | async-start | bytes 2097152 | tf_op jit(solution)/shard_map/all_to_all | solution.py:351
  15.2 12.9 %collective-permute-start = (bf16[64,1024]{1,0:T(8,128)(2,1)S(1)}, bf16[64,1024]{1,0:T(8,128)(2,1)S(1)}, u32[]{:S(2)}, u32[]{:S(2)}) collective-permute-start(bf16[64,1024]{1,0:T(8,128)(2,1)S(1)} %fusion.refs_0_), channel_id=1, source_target_pairs={{0,32},{32,64},{64,96},{96,128},{128,160},{160,192},{192,224},{224... | collective-permute-start | bytes 393224 | tf_op jit(solution)/shard_map/ppermute | solution.py:321
  17.1 12.9 %collective-permute-start.2 = (bf16[64,1024]{1,0:T(8,128)(2,1)S(1)}, bf16[64,1024]{1,0:T(8,128)(2,1)S(1)}, u32[]{:S(2)}, u32[]{:S(2)}) collective-permute-start(bf16[64,1024]{1,0:T(8,128)(2,1)S(1)} %fusion.refs_0_), channel_id=1, source_target_pairs={{0,480},{32,0},{64,32},{96,64},{128,96},{160,128},{192,160},{224,1... | collective-permute-start | bytes 393224 | tf_op jit(solution)/shard_map/ppermute | solution.py:321
  28.1 9.4 %collective-permute-start.1 = (bf16[64,1024]{1,0:T(8,128)(2,1)S(1)}, bf16[64,1024]{1,0:T(8,128)(2,1)S(1)}, u32[]{:S(2)}, u32[]{:S(2)}) collective-permute-start(bf16[64,1024]{1,0:T(8,128)(2,1)S(1)} %collective-permute-done.refs_1_), channel_id=1, source_target_pairs={{0,32},{32,64},{64,96},{96,128},{128,160},{160,192},{192,224},{224... | collective-permute-start | bytes 393224 | tf_op jit(solution)/shard_map/ppermute | solution.py:321
  30.0 7.5 %collective-permute-start.3 = (bf16[64,1024]{1,0:T(8,128)(2,1)S(1)}, bf16[64,1024]{1,0:T(8,128)(2,1)S(1)}, u32[]{:S(2)}, u32[]{:S(2)}) collective-permute-start(bf16[64,1024]{1,0:T(8,128)(2,1)S(1)} %collective-permute-done.2.refs_2_), channel_id=1, source_target_pairs={{0,480},{32,0},{64,32},{96,64},{128,96},{160,128},{192,160},{224,1... | collective-permute-start | bytes 393224 | tf_op jit(solution)/shard_map/ppermute | solution.py:321
  38.2 22.6 %all-to-all-start.1 = ((bf16[32,32,384]{2,1,0:T(8,128)(2,1)}), bf16[32,32,384]{2,1,0:T(8,128)(2,1)S(1)}, u32[]{:S(2)}, u32[]{:S(2)}) async-start(bf16[32,32,384]{2,1,0:T(8,128)(2,1)} %shard_map.137), calls=%async_computation.1 | async-start | bytes 1572864 | tf_op jit(solution)/shard_map/all_to_all | solution.py:351
  46.6 2.7 %collective-permute-start.4 = (bf16[8,512]{1,0:T(8,128)(2,1)S(1)}, bf16[8,512]{1,0:T(8,128)(2,1)S(1)}, u32[]{:S(2)}, u32[]{:S(2)}) collective-permute-start(bf16[8,512]{1,0:T(8,128)(2,1)S(1)} %shard_map.138), channel_id=1, source_target_pairs={{0,32},{32,64},{64,96},{96,128},{128,160},{160,192},{192,224},{224... | collective-permute-start | bytes 24584 | tf_op jit(solution)/shard_map/ppermute | solution.py:321
  60.8 15.1 %collective-permute-start.5 = (bf16[64,1024]{1,0:T(8,128)(2,1)}, bf16[64,1024]{1,0:T(8,128)(2,1)S(1)}, u32[]{:S(2)}, u32[]{:S(2)}) collective-permute-start(bf16[64,1024]{1,0:T(8,128)(2,1)} %copy-done.17), channel_id=1, source_target_pairs={{0,32},{32,64},{64,96},{96,128},{128,160},{160,192},{192,224},{224... | collective-permute-start | bytes 393224 | tf_op jit(solution)/shard_map/ppermute | solution.py:321
  62.7 17.1 %collective-permute-start.8 = (bf16[64,1024]{1,0:T(8,128)(2,1)}, bf16[64,1024]{1,0:T(8,128)(2,1)S(1)}, u32[]{:S(2)}, u32[]{:S(2)}) collective-permute-start(bf16[64,1024]{1,0:T(8,128)(2,1)} %copy-done.19), channel_id=1, source_target_pairs={{0,480},{32,0},{64,32},{96,64},{128,96},{160,128},{192,160},{224,1... | collective-permute-start | bytes 393224 | tf_op jit(solution)/shard_map/ppermute | solution.py:321
  67.6 25.8 %all-to-all-start.2 = ((bf16[16,24,128]{2,1,0:T(8,128)(2,1)}), bf16[16,24,128]{2,1,0:T(8,128)(2,1)S(1)}, u32[]{:S(2)}, u32[]{:S(2)}) async-start(bf16[16,24,128]{2,1,0:T(8,128)(2,1)} %copy-done.35), calls=%async_computation.2 | async-start | bytes 196608 | tf_op jit(solution)/shard_map/all_to_all | solution.py:351
  76.0 10.9 %collective-permute-start.6 = (bf16[64,1024]{1,0:T(8,128)(2,1)S(1)}, bf16[64,1024]{1,0:T(8,128)(2,1)S(1)}, u32[]{:S(2)}, u32[]{:S(2)}) collective-permute-start(bf16[64,1024]{1,0:T(8,128)(2,1)S(1)} %collective-permute-done.5.refs_5_), channel_id=1, source_target_pairs={{0,32},{32,64},{64,96},{96,128},{128,160},{160,192},{192,224},{224... | collective-permute-start | bytes 393224 | tf_op jit(solution)/shard_map/ppermute | solution.py:321
  79.9 44.5 %copy-start.23 = (bf16[64,1024]{1,0:T(8,128)(2,1)}, bf16[64,1024]{1,0:T(8,128)(2,1)S(1)}, u32[]{:S(2)}) copy-start(bf16[64,1024]{1,0:T(8,128)(2,1)S(1)} %collective-permute-done.8.refs_6_) | copy-start | bytes 393220
  79.9 8.9 %collective-permute-start.9 = (bf16[64,1024]{1,0:T(8,128)(2,1)S(1)}, bf16[64,1024]{1,0:T(8,128)(2,1)S(1)}, u32[]{:S(2)}, u32[]{:S(2)}) collective-permute-start(bf16[64,1024]{1,0:T(8,128)(2,1)S(1)} %collective-permute-done.8.refs_6_), channel_id=1, source_target_pairs={{0,480},{32,0},{64,32},{96,64},{128,96},{160,128},{192,160},{224,1... | collective-permute-start | bytes 393224 | tf_op jit(solution)/shard_map/ppermute | solution.py:321
  86.9 37.5 %copy-start.25 = (bf16[64,1024]{1,0:T(8,128)(2,1)}, bf16[64,1024]{1,0:T(8,128)(2,1)S(1)}, u32[]{:S(2)}) copy-start(bf16[64,1024]{1,0:T(8,128)(2,1)S(1)} %collective-permute-done.6.refs_7_) | copy-start | bytes 393220
  86.9 7.6 %collective-permute-start.7 = (bf16[64,1024]{1,0:T(8,128)(2,1)S(1)}, bf16[64,1024]{1,0:T(8,128)(2,1)S(1)}, u32[]{:S(2)}, u32[]{:S(2)}) collective-permute-start(bf16[64,1024]{1,0:T(8,128)(2,1)S(1)} %collective-permute-done.6.refs_7_), channel_id=1, source_target_pairs={{0,32},{32,64},{64,96},{96,128},{128,160},{160,192},{192,224},{224... | collective-permute-start | bytes 393224 | tf_op jit(solution)/shard_map/ppermute | solution.py:321
  88.8 6.5 %collective-permute-start.10 = (bf16[64,1024]{1,0:T(8,128)(2,1)S(1)}, bf16[64,1024]{1,0:T(8,128)(2,1)S(1)}, u32[]{:S(2)}, u32[]{:S(2)}) collective-permute-start(bf16[64,1024]{1,0:T(8,128)(2,1)S(1)} %collective-permute-done.9.refs_8_), channel_id=1, source_target_pairs={{0,480},{32,0},{64,32},{96,64},{128,96},{160,128},{192,160},{224,1... | collective-permute-start | bytes 393224 | tf_op jit(solution)/shard_map/ppermute | solution.py:321
  96.1 7.7 %collective-permute-start.11 = (bf16[64,1024]{1,0:T(8,128)(2,1)S(1)}, bf16[64,1024]{1,0:T(8,128)(2,1)S(1)}, u32[]{:S(2)}, u32[]{:S(2)}) collective-permute-start(bf16[64,1024]{1,0:T(8,128)(2,1)S(1)} %collective-permute-done.7.refs_9_), channel_id=1, source_target_pairs={{0,32},{32,64},{64,96},{96,128},{128,160},{160,192},{192,224},{224... | collective-permute-start | bytes 393224 | tf_op jit(solution)/shard_map/ppermute | solution.py:321
  98.0 17.0 %collective-permute-start.12 = (bf16[64,1024]{1,0:T(8,128)(2,1)S(1)}, bf16[64,1024]{1,0:T(8,128)(2,1)}, u32[]{:S(2)}, u32[]{:S(2)}) collective-permute-start(bf16[64,1024]{1,0:T(8,128)(2,1)S(1)} %collective-permute-done.10.refs_10_), channel_id=1, source_target_pairs={{0,480},{32,0},{64,32},{96,64},{128,96},{160,128},{192,160},{224,1... | collective-permute-start | bytes 393224 | tf_op jit(solution)/shard_map/ppermute | solution.py:321
  103.8 15.8 %collective-permute-start.13 = (bf16[64,1024]{1,0:T(8,128)(2,1)S(1)}, bf16[64,1024]{1,0:T(8,128)(2,1)}, u32[]{:S(2)}, u32[]{:S(2)}) collective-permute-start(bf16[64,1024]{1,0:T(8,128)(2,1)S(1)} %collective-permute-done.11.refs_11_), channel_id=1, source_target_pairs={{0,32},{32,64},{64,96},{96,128},{128,160},{160,192},{192,224},{224... | collective-permute-start | bytes 393224 | tf_op jit(solution)/shard_map/ppermute | solution.py:321
  105.7 31.6 %all-to-all-start.3 = ((bf16[16,16,128]{2,1,0:T(8,128)(2,1)}), bf16[16,16,128]{2,1,0:T(8,128)(2,1)}, u32[]{:S(2)}, u32[]{:S(2)}) async-start(bf16[16,16,128]{2,1,0:T(8,128)(2,1)} %shard_map.141), calls=%async_computation.3 | async-start | bytes 131072 | tf_op jit(solution)/shard_map/all_to_all | solution.py:351
  115.0 17.5 %collective-permute-start.14 = (bf16[64,1024]{1,0:T(8,128)(2,1)}, bf16[64,1024]{1,0:T(8,128)(2,1)S(1)}, u32[]{:S(2)}, u32[]{:S(2)}) collective-permute-start(bf16[64,1024]{1,0:T(8,128)(2,1)} %collective-permute-done.12.refs_12_), channel_id=1, source_target_pairs={{0,480},{32,0},{64,32},{96,64},{128,96},{160,128},{192,160},{224,1... | collective-permute-start | bytes 393224 | tf_op jit(solution)/shard_map/ppermute | solution.py:321
  119.6 12.9 %collective-permute-start.15 = (bf16[64,1024]{1,0:T(8,128)(2,1)}, bf16[64,1024]{1,0:T(8,128)(2,1)S(1)}, u32[]{:S(2)}, u32[]{:S(2)}) collective-permute-start(bf16[64,1024]{1,0:T(8,128)(2,1)} %collective-permute-done.13.refs_13_), channel_id=1, source_target_pairs={{0,32},{32,64},{64,96},{96,128},{128,160},{160,192},{192,224},{224... | collective-permute-start | bytes 393224 | tf_op jit(solution)/shard_map/ppermute | solution.py:321
  121.5 2.9 %collective-permute-start.16 = (bf16[8,128]{1,0:T(8,128)(2,1)S(1)}, bf16[8,128]{1,0:T(8,128)(2,1)S(1)}, u32[]{:S(2)}, u32[]{:S(2)}) collective-permute-start(bf16[8,128]{1,0:T(8,128)(2,1)S(1)} %shard_map.143), channel_id=1, source_target_pairs={{0,32},{32,64},{64,96},{96,128},{128,160},{160,192},{192,224},{224... | collective-permute-start | bytes 6152 | tf_op jit(solution)/shard_map/ppermute | solution.py:321
  141.0 7.1 %collective-permute-start.22 = (bf16[512,256]{1,0:T(8,128)(2,1)S(1)}, bf16[512,256]{1,0:T(8,128)(2,1)S(1)}, u32[]{:S(2)}, u32[]{:S(2)}) collective-permute-start(bf16[512,256]{1,0:T(8,128)(2,1)S(1)} %get-tuple-element.70.own_ref), channel_id=1, source_target_pairs={{0,24},{8,0},{16,8},{24,16},{1,25},{9,1},{17,9},{25,17},{2,26},{10... | collective-permute-start | bytes 786440 | tf_op jit(solution)/shard_map/ppermute | solution.py:321
  143.4 8.3 %collective-permute-start.21 = (bf16[512,256]{1,0:T(8,128)(2,1)S(1)}, bf16[512,256]{1,0:T(8,128)(2,1)S(1)}, u32[]{:S(2)}, u32[]{:S(2)}) collective-permute-start(bf16[512,256]{1,0:T(8,128)(2,1)S(1)} %get-tuple-element.70.own_ref), channel_id=1, source_target_pairs={{0,8},{8,16},{16,24},{24,0},{1,9},{9,17},{17,25},{25,1},{2,10},{10... | collective-permute-start | bytes 786440 | tf_op jit(solution)/shard_map/ppermute | solution.py:321
  148.2 7.4 %collective-permute-start.24 = (bf16[256,256]{1,0:T(8,128)(2,1)S(1)}, bf16[256,256]{1,0:T(8,128)(2,1)S(1)}, u32[]{:S(2)}, u32[]{:S(2)}) collective-permute-start(bf16[256,256]{1,0:T(8,128)(2,1)S(1)} %slice.19), channel_id=1, source_target_pairs={{0,24},{8,0},{16,8},{24,16},{1,25},{9,1},{17,9},{25,17},{2,26},{10... | collective-permute-start | bytes 393224 | tf_op jit(solution)/shard_map/ppermute | solution.py:321
  151.8 8.6 %collective-permute-start.23 = (bf16[256,256]{1,0:T(8,128)(2,1)S(1)}, bf16[256,256]{1,0:T(8,128)(2,1)S(1)}, u32[]{:S(2)}, u32[]{:S(2)}) collective-permute-start(bf16[256,256]{1,0:T(8,128)(2,1)S(1)} %slice.18), channel_id=1, source_target_pairs={{0,8},{8,16},{16,24},{24,0},{1,9},{9,17},{17,25},{25,1},{2,10},{10... | collective-permute-start | bytes 393224 | tf_op jit(solution)/shard_map/ppermute | solution.py:321
  163.3 32.0 %collective-permute-start.25 = (bf16[512,1024]{1,0:T(8,128)(2,1)S(1)}, bf16[512,1024]{1,0:T(8,128)(2,1)S(1)}, u32[]{:S(2)}, u32[]{:S(2)}) collective-permute-start(bf16[512,1024]{1,0:T(8,128)(2,1)S(1)} %shard_map.146), channel_id=1, source_target_pairs={{0,1},{1,0},{2,3},{3,2},{4,5},{5,4},{6,7},{7,6},{8,9},{9,8},{10,11... | collective-permute-start | bytes 3145736 | tf_op jit(solution)/shard_map/ppermute | solution.py:321
  174.8 9.7 %collective-permute-start.18 = (bf16[512,256]{1,0:T(8,128)(2,1)S(1)}, bf16[512,256]{1,0:T(8,128)(2,1)S(1)}, u32[]{:S(2)}, u32[]{:S(2)}) collective-permute-start(bf16[512,256]{1,0:T(8,128)(2,1)S(1)} %get-tuple-element.68.own_ref), channel_id=1, source_target_pairs={{0,24},{8,0},{16,8},{24,16},{1,25},{9,1},{17,9},{25,17},{2,26},{10... | collective-permute-start | bytes 786440 | tf_op jit(solution)/shard_map/ppermute | solution.py:321
  176.8 11.2 %collective-permute-start.17 = (bf16[512,256]{1,0:T(8,128)(2,1)S(1)}, bf16[512,256]{1,0:T(8,128)(2,1)S(1)}, u32[]{:S(2)}, u32[]{:S(2)}) collective-permute-start(bf16[512,256]{1,0:T(8,128)(2,1)S(1)} %get-tuple-element.68.own_ref), channel_id=1, source_target_pairs={{0,8},{8,16},{16,24},{24,0},{1,9},{9,17},{17,25},{25,1},{2,10},{10... | collective-permute-start | bytes 786440 | tf_op jit(solution)/shard_map/ppermute | solution.py:321
  184.6 6.1 %collective-permute-start.20 = (bf16[256,256]{1,0:T(8,128)(2,1)S(1)}, bf16[256,256]{1,0:T(8,128)(2,1)S(1)}, u32[]{:S(2)}, u32[]{:S(2)}) collective-permute-start(bf16[256,256]{1,0:T(8,128)(2,1)S(1)} %slice.17), channel_id=1, source_target_pairs={{0,24},{8,0},{16,8},{24,16},{1,25},{9,1},{17,9},{25,17},{2,26},{10... | collective-permute-start | bytes 393224 | tf_op jit(solution)/shard_map/ppermute | solution.py:321
  188.0 7.3 %collective-permute-start.19 = (bf16[256,256]{1,0:T(8,128)(2,1)S(1)}, bf16[256,256]{1,0:T(8,128)(2,1)S(1)}, u32[]{:S(2)}, u32[]{:S(2)}) collective-permute-start(bf16[256,256]{1,0:T(8,128)(2,1)S(1)} %slice.16), channel_id=1, source_target_pairs={{0,8},{8,16},{16,24},{24,0},{1,9},{9,17},{17,25},{25,1},{2,10},{10... | collective-permute-start | bytes 393224 | tf_op jit(solution)/shard_map/ppermute | solution.py:321
  (47 other events, 440.6 us)

commit v2 on v1

v2 whole, which is shorter than its diff:
```python
import jax
import jax.numpy as jnp
from jax import lax
from jax.experimental import pallas as pl
from jax.experimental.pallas import tpu as pltpu
from jax.sharding import Mesh
from jax.sharding import PartitionSpec as P

HEAD_DIM = 64
STATE = 128
SPAN = 128
LANES = 128
F32 = jnp.float32
BF16 = jnp.bfloat16
SEQ = ("z", "x")
HEAD = ("y", "c")
PLANE = ("x", "y", "c")
ALL = ("z", "x", "y", "c")
VMEM = pl.BlockSpec(memory_space=pltpu.VMEM)
HBM = pl.BlockSpec(memory_space=pltpu.HBM)


def call(kernel, outs, inputs, scratch=(), flops=1 << 22, limit=16, far=(), far_out=False):
    return pl.pallas_call(
        kernel,
        out_shape=outs,
        in_specs=[HBM if i in far else VMEM for i in range(len(inputs))],
        out_specs=jax.tree.map(lambda _: HBM if far_out else VMEM, outs),
        scratch_shapes=list(scratch),
        compiler_params=pltpu.CompilerParams(vmem_limit_bytes=limit << 20),
        cost_estimate=pl.CostEstimate(flops=flops, bytes_accessed=1 << 20, transcendentals=0),
        name=kernel.__name__,
    )(*inputs)


def shape(dims, dtype):
    return jax.ShapeDtypeStruct(dims, dtype)


def silu(v):
    return v * (1.0 / (1.0 + jnp.exp(-v)))


def nt(a, b):
    return lax.dot_general(a, b, (((1,), (1,)), ((), ())), preferred_element_type=F32)


def tn(a, b):
    return lax.dot_general(a, b, (((0,), (0,)), ((), ())), preferred_element_type=F32)


def by_head(values, chunk, first):
    return jnp.where(first, values[:, 2 * chunk : 2 * chunk + 1], values[:, 2 * chunk + 1 : 2 * chunk + 2])


def left_half():
    return lax.broadcasted_iota(jnp.int32, (1, LANES), 1) < HEAD_DIM


def top_half():
    return lax.broadcasted_iota(jnp.int32, (LANES, 1), 0) < HEAD_DIM


def pack(
    x_far, z_far, b_far, c_far, dt_far, out_far,
    x_ref, z_ref, b_ref, c_ref, dt_ref, out_ref, in_sems, out_sems,
):
    pairs = ((dt_far, dt_ref), (b_far, b_ref), (c_far, c_ref), (x_far, x_ref), (z_far, z_ref))
    loads = [pltpu.make_async_copy(*pair, in_sems.at[i]) for i, pair in enumerate(pairs)]
    for load in loads:
        load.start()
    for load in loads:
        load.wait()
    count, _, width = out_ref.shape
    groups = b_ref.shape[1] // LANES
    parts = count // groups
    cols = x_ref.shape[1] // count
    heads = dt_ref.shape[1] // count
    dt = dt_ref[...].astype(F32)
    stores = [
        pltpu.make_async_copy(out_ref.at[d], out_far.at[d], out_sems.at[d]) for d in range(count)
    ]
    for d in range(count):
        part, group = divmod(d, groups)
        at = group * parts + part
        mine = dt if at == 0 else pltpu.roll(dt, LANES - at * heads, 1)
        side = slice(group * LANES, (group + 1) * LANES)
        out_ref[d, :, :cols] = x_ref[:, at * cols : (at + 1) * cols]
        out_ref[d, :, cols : cols + LANES] = b_ref[:, side]
        out_ref[d, :, cols + LANES : cols + 2 * LANES] = c_ref[:, side]
        out_ref[d, :, cols + 2 * LANES : width - LANES] = z_ref[:, at * cols : (at + 1) * cols]
        out_ref[d, :, width - LANES :] = mine.astype(BF16)
        if d > 0:
            stores[d - 1].start()
    stores[-1].start()
    for store in stores:
        store.wait()


def steps(packed_ref, heads_ref, dt_ref, cum_ref, sum_ref):
    rows, tokens = dt_ref.shape
    before = lax.broadcasted_iota(jnp.int32, (SPAN, SPAN), 0)
    after = lax.broadcasted_iota(jnp.int32, (SPAN, SPAN), 1)
    ones = (before <= after).astype(F32)
    bias, coeff = heads_ref[:, 0:1], heads_ref[:, 1:2]
    total = jnp.zeros((rows, 1), F32)
    for k in range(tokens // SPAN):
        part = slice(k * SPAN, (k + 1) * SPAN)
        raw = packed_ref[part, packed_ref.shape[1] - LANES :].astype(F32).T[:rows] + bias
        dt = jnp.maximum(raw, 0.0) + jnp.log1p(jnp.exp(-jnp.abs(raw)))
        dt_ref[:, part] = dt
        cum = lax.dot(
            coeff * dt, ones, precision=lax.Precision.HIGHEST, preferred_element_type=F32
        )
        cum_ref[:, part] = cum
        sum_ref[:, part] = cum + total
        total = total + cum[:, SPAN - 1 :]


def columns(rows):
    filled = jnp.concatenate([rows, jnp.zeros((SPAN - rows.shape[0], SPAN), F32)])
    return filled.T


def fill_padded(padded, halo_ref, packed_ref, width):
    padded[:8] = halo_ref[:, :width].astype(F32)
    padded[8:] = packed_ref[:, :width].astype(F32)


def conv(padded, taps, bias, k, lo):
    first = 8 + k * SPAN - 3
    total = bias + taps[0] * padded[first : first + SPAN, lo : lo + LANES]
    for j in range(1, 4):
        total = total + taps[j] * padded[first + j : first + j + SPAN, lo : lo + LANES]
    return silu(total).astype(BF16)


def scan_in(
    packed_ref, halo_ref, taps_ref, group_taps_ref, dt_ref, cum_ref, sum_ref,
    xs_ref, b_ref, held_ref, sent_ref, padded,
):
    tokens, cols = xs_ref.shape
    blocks = tokens // SPAN
    fill_padded(padded, halo_ref, packed_ref, cols + LANES)
    left, top = left_half(), top_half()
    group_taps = [group_taps_ref[j : j + 1] for j in range(4)]
    states = [jnp.zeros((LANES, STATE), F32) for _ in range(cols // LANES)]
    for k in range(blocks):
        part = slice(k * SPAN, (k + 1) * SPAN)
        b = conv(padded, group_taps, group_taps_ref[4:5], k, cols)
        b_ref[part] = b
        cum = cum_ref[:, part]
        scale = columns(dt_ref[:, part] * jnp.exp(cum[:, SPAN - 1 :] - cum))
        decay = columns(jnp.broadcast_to(jnp.exp(cum[:, SPAN - 1 :]), cum.shape))
        for chunk in range(cols // LANES):
            lo = chunk * LANES
            taps = [taps_ref[j : j + 1, lo : lo + LANES] for j in range(4)]
            xs = conv(padded, taps, taps_ref[4:5, lo : lo + LANES], k, lo)
            xs_ref[part, lo : lo + LANES] = xs
            weighted = (xs.astype(F32) * by_head(scale, chunk, left)).astype(BF16)
            held_ref[k, lo : lo + LANES] = states[chunk].astype(BF16)
            states[chunk] = by_head(decay, chunk, top) * states[chunk] + tn(weighted, b)
    count, extra = sent_ref.shape[0], sent_ref.shape[1]
    rows = cols // count
    for chunk in range(cols // LANES):
        final = states[chunk].astype(BF16)
        for i in range(LANES // rows):
            sent_ref[chunk * (LANES // rows) + i, :rows] = final[i * rows : (i + 1) * rows]
    total = columns(jnp.broadcast_to(sum_ref[:, tokens - 1 :], (sum_ref.shape[0], SPAN)))[:1]
    high = total.astype(BF16).astype(F32)
    middle = (total - high).astype(BF16).astype(F32)
    low = total - high - middle
    at = lax.broadcasted_iota(jnp.int32, (extra - rows, LANES), 0)
    tail = jnp.where(at == 0, high, jnp.where(at == 1, middle, jnp.where(at == 2, low, 0.0)))
    for d in range(count):
        sent_ref[d, rows:] = tail.astype(BF16)


def scan_all(inbox_ref, starts_ref, decays):
    count, rows, _ = starts_ref.shape
    tail = inbox_ref[:, rows:].astype(F32)
    logs = tail[:, 0] + tail[:, 1] + tail[:, 2]
    lanes = lax.broadcasted_iota(jnp.int32, logs.shape, 1)
    head = lax.axis_index("z") * rows // HEAD_DIM
    column = jnp.sum(jnp.where(lanes == head, logs, 0.0), axis=1, keepdims=True)
    decays[...] = jnp.broadcast_to(jnp.exp(column), decays.shape)
    state = jnp.zeros((rows, STATE), F32)
    for i in range(count):
        starts_ref[i] = state.astype(BF16)
        state = decays[i : i + 1] * state + inbox_ref[i, :rows].astype(F32)


def local(
    xs_ref, b_ref, packed_ref, halo_ref, group_taps_ref, dt_ref, cum_ref, held_ref, skip_ref,
    c_ref, y_ref, padded,
):
    tokens, cols = xs_ref.shape
    padded[:8] = halo_ref[:, cols + LANES : cols + 2 * LANES].astype(F32)
    padded[8:] = packed_ref[:, cols + LANES : cols + 2 * LANES].astype(F32)
    rows = lax.broadcasted_iota(jnp.int32, (SPAN, SPAN), 0)
    lanes = lax.broadcasted_iota(jnp.int32, (SPAN, SPAN), 1)
    causal = rows >= lanes
    left = left_half()
    taps = [group_taps_ref[8 + j : 9 + j] for j in range(4)]
    for k in range(tokens // SPAN):
        part = slice(k * SPAN, (k + 1) * SPAN)
        c = conv(padded, taps, group_taps_ref[12:13], k, 0)
        c_ref[part] = c
        scores = nt(c, b_ref[part])
        cum_t = cum_ref[:, part]
        dt_t = dt_ref[:, part]
        cum = columns(cum_t)
        grown = jnp.exp(cum)

        def mix(h):
            spread = cum[:, h : h + 1] - cum_t[h : h + 1]
            decays = jnp.exp(jnp.where(causal, spread, -jnp.inf))
            return (decays * dt_t[h : h + 1] * scores).astype(BF16)

        for chunk in range(cols // LANES):
            lo = chunk * LANES
            xs = xs_ref[part, lo : lo + LANES]
            y0 = jnp.dot(mix(2 * chunk), xs, preferred_element_type=F32)
            y1 = jnp.dot(mix(2 * chunk + 1), xs, preferred_element_type=F32)
            y = jnp.where(left, y0, y1) + by_head(skip_ref[...], chunk, left) * xs.astype(F32)
            if k > 0:
                y = y + nt(c, held_ref[k, lo : lo + LANES]) * by_head(grown, chunk, left)
            y_ref[part, lo : lo + LANES] = y


def finish(start_ref, c_ref, sum_ref, y_ref, packed_ref, out_ref):
    tokens, cols = y_ref.shape
    copies = out_ref.shape[0]
    rows = tokens // 32
    left = left_half()
    first = lax.axis_index("c") == 0
    for k in range(tokens // SPAN):
        part = slice(k * SPAN, (k + 1) * SPAN)
        grown = jnp.exp(columns(sum_ref[:, part]))
        for chunk in range(cols // LANES):
            lo = chunk * LANES
            carry = nt(c_ref[part], start_ref[lo : lo + LANES]) * by_head(grown, chunk, left)
            at = cols + 2 * LANES + lo
            z = packed_ref[part, at : at + LANES].astype(F32)
            gated = ((y_ref[part, lo : lo + LANES] + carry) * silu(z)).astype(BF16)
            for i in range(SPAN // (2 * rows)):
                even = gated[2 * i * rows : (2 * i + 1) * rows]
                odd = gated[(2 * i + 1) * rows : (2 * i + 2) * rows]
                theirs = jnp.where(first, odd, even)
                ours = jnp.where(first, even, odd)
                at = k * (SPAN // 2) + i * rows
                for d in range(copies):
                    out_ref[d, at : at + rows, lo : lo + LANES] = theirs
                    out_ref[d, tokens // 2 + at : tokens // 2 + at + rows, lo : lo + LANES] = ours


def multiply(gated_ref, first, weights_ref, out_ref, other_ref):
    parts, _, cols = gated_ref.shape
    rows, width = out_ref.shape
    squares = jnp.zeros((rows, 1), F32)
    for i in range(parts):
        value = gated_ref[i, first : first + rows].astype(F32)
        squares = squares + jnp.sum(value * value, axis=1, keepdims=True)
    scale = 1.0 / jnp.sqrt(squares / weights_ref.shape[1] + 1.0)
    step = 2 * LANES
    for lo in range(0, width, step):
        total = jnp.zeros((rows, step), F32)
        for i in range(parts):
            weights = weights_ref[lo : lo + step, i * cols : (i + 1) * cols]
            total = total + nt(gated_ref[i, first : first + rows], weights)
        total = total * scale
        if other_ref is not None:
            total = total + other_ref[:, lo : lo + step].astype(F32)
        out_ref[:, lo : lo + step] = total.astype(BF16)


def rescale(weights_ref, gain_ref, out_ref):
    for lo in range(0, out_ref.shape[0], SPAN):
        part = slice(lo, lo + SPAN)
        out_ref[part] = (weights_ref[part].astype(F32) * gain_ref[...]).astype(BF16)


def project(gated_ref, weights_ref, out_ref):
    multiply(gated_ref, 0, weights_ref, out_ref, None)


def project_add(gated_ref, weights_ref, other_ref, out_ref):
    multiply(gated_ref, out_ref.shape[0], weights_ref, out_ref, other_ref)


def tail(array_ref, out_ref):
    out_ref[...] = array_ref[array_ref.shape[0] - out_ref.shape[0] :, : out_ref.shape[1]]


def collect(shares_ref, out_ref, *, ys):
    count, rows, width = shares_ref.shape
    xs = count // ys
    left = left_half()
    for pair in range(width // LANES):
        lo = pair * LANES
        sums = []
        for i in range(xs):
            total = shares_ref[i * ys, :, lo : lo + LANES].astype(F32)
            for j in range(1, ys):
                total = total + shares_ref[i * ys + j, :, lo : lo + LANES].astype(F32)
            sums.append(total)
        rolled = [pltpu.roll(total, HEAD_DIM, 1) for total in sums]
        for side in range(2):
            for i in range(0, xs, 2):
                if side == 0:
                    value = jnp.where(left, sums[i], rolled[i + 1])
                else:
                    value = jnp.where(left, rolled[i], sums[i + 1])
                at = (2 * pair + side) * (xs * HEAD_DIM) + i * HEAD_DIM
                out_ref[:, at : at + LANES] = value.astype(BF16)


def shift(array, axis, by, wrap=True):
    count = lax.axis_size(axis)
    pairs = [(i, (i + by) % count) for i in range(count) if wrap or 0 <= i + by < count]
    return lax.ppermute(array, axis, pairs)


def sent(array, axes, name):
    with jax.named_scope(name):
        return lax.all_to_all(array, axes, 0, 0, tiled=True)


def per_device(
    x_proj, z_proj, b_proj, c_proj, dt_raw, dt_bias, a_log, d_skip,
    conv_x, conv_bias_x, conv_bc, conv_bias_bc, norm_weight, out_weight,
):
    xs, ys, cs = (lax.axis_size(a) for a in PLANE)
    zs = lax.axis_size("z")
    plane = xs * ys * cs
    rows, inner = x_proj.shape
    cols = inner // plane
    tokens = rows * plane
    part = lax.axis_index("x")
    heads = dt_bias.shape[0] // xs

    def own(values, axis):
        size = values.shape[axis] // xs
        return lax.dynamic_slice_in_dim(values, part * size, size, axis)

    weights = lax.all_gather(out_weight.T, "z", axis=0, tiled=True)
    out = call(
        pack,
        shape((plane, rows, 2 * cols + 3 * LANES), BF16),
        (x_proj, z_proj, b_proj, c_proj, dt_raw),
        [pltpu.VMEM(a.shape, BF16) for a in (x_proj, z_proj, b_proj, c_proj, dt_raw)]
        + [
            pltpu.VMEM((plane, rows, 2 * cols + 3 * LANES), BF16),
            pltpu.SemaphoreType.DMA((5,)),
            pltpu.SemaphoreType.DMA((plane,)),
        ],
        limit=60,
        far=range(5),
        far_out=True,
    )
    per_head = jnp.stack([own(dt_bias, 0), own(-jnp.exp(a_log), 0)], axis=1)
    per_head = jnp.pad(per_head, ((0, 8 - heads), (0, LANES - 2)))
    skip = jnp.pad(own(d_skip, 0), (0, LANES - heads))[None]
    taps = jnp.pad(jnp.concatenate([own(conv_x, 1), own(conv_bias_x, 0)[None]]), ((0, 3), (0, 0)))
    group_taps = jnp.pad(
        jnp.concatenate([jnp.moveaxis(conv_bc, 0, 1), conv_bias_bc[:, None]], axis=1),
        ((0, 0), (0, 3), (0, 0)),
    ).reshape(16, LANES)
    packed, per_head, skip, taps, group_taps = lax.optimization_barrier(
        (sent(out, PLANE, "entry"), per_head, skip, taps, group_taps)
    )
    packed = packed.reshape(tokens, 2 * cols + 3 * LANES)
    halo = call(tail, shape((8, cols + 2 * LANES), BF16), (packed,), (), 1 << 16, 4)
    halo = shift(halo, "z", 1, wrap=False)
    by_token = shape((8, tokens), F32)
    dt, cum, sums = call(steps, (by_token, by_token, by_token), (packed, per_head))
    x_conv, b_conv, held, states_out = call(
        scan_in,
        (
            shape((tokens, cols), BF16),
            shape((tokens, LANES), BF16),
            shape((tokens // SPAN, cols, STATE), BF16),
            shape((zs, cols // zs + 8, STATE), BF16),
        ),
        (packed, halo, taps, group_taps, dt, cum, sums),
        [pltpu.VMEM((tokens + 8, cols + LANES), F32)],
        1 << 25,
    )
    states_in = sent(states_out, "z", "pieces")
    c_conv, y = call(
        local,
        (shape((tokens, LANES), BF16), shape((tokens, cols), F32)),
        (x_conv, b_conv, packed, halo, group_taps, dt, cum, held, skip),
        [pltpu.VMEM((tokens + 8, LANES), F32)],
        1 << 27,
    )
    states_in, y = lax.optimization_barrier((states_in, y))
    starts = call(
        scan_all,
        shape((zs, cols // zs, STATE), BF16),
        (states_in,),
        [pltpu.VMEM((zs, LANES), F32)],
    )
    start = sent(starts, "z", "starts").reshape(cols, STATE)
    copies = call(
        finish, shape((xs, tokens, cols), BF16), (start, c_conv, sums, y, packed), (), 1 << 25
    )
    gated = sent(copies, "x", "gather")
    weights = call(rescale, shape(weights.shape, BF16), (weights, norm_weight[None]))
    product = shape((tokens // 2, weights.shape[0]), BF16)
    away = call(project, product, (gated, weights), (), 1 << 29, 24)
    other = shift(away, "c", 1)
    both = call(project_add, product, (gated, weights, other), (), 1 << 29, 24)
    shares = sent(both.reshape(xs * ys, rows, weights.shape[0]), ("x", "y"), "exit")

    def collect_all(shares_ref, out_ref):
        collect(shares_ref, out_ref, ys=ys)

    return call(collect_all, shape((rows, xs * weights.shape[0]), BF16), (shares,))


def solution(mesh):
    split = Mesh(mesh.devices.reshape(16, 4, 4, 2), ALL)
    return jax.shard_map(
        per_device,
        mesh=split,
        in_specs=(
            P(ALL, None),
            P(ALL, None),
            P(ALL, None),
            P(ALL, None),
            P(ALL, None),
            P(HEAD),
            P(HEAD),
            P(HEAD),
            P(None, HEAD),
            P(HEAD),
            P(None, None, HEAD),
            P(None, HEAD),
            P(HEAD),
            P(HEAD, SEQ),
        ),
        out_specs=P(ALL, None),
        check_vma=False,
    )
```

time: 222 us -> 172 us (0.77); the launches traced: 218 us -> 171 us
  starting transfers between devices: 126 us -> 38.8 us
  blocking collectives: 18.9 us -> 38.4 us
  waiting for transfers between devices: 30.7 us -> 49 us
  between operations: 0.77 us -> 13.6 us
  local copies, waits for them, and re-layouts: 21.7 us -> 16.2 us
  Pallas kernels: 17.9 us -> 15.3 us
    ppermute x26 -> x2, starting transfers between devices: 89.5 us -> 8.22 us  [shift(): return lax.ppermute(array, axis, pairs)]
    all_to_all x4 -> x3, waiting for transfers between devices: 4.86 us -> 45.9 us  [sent(): return lax.all_to_all(array, axes, 0, 0, tiled=True)]
    ppermute x26 -> x2, waiting for transfers between devices: 25.8 us -> 2.37 us  [shift(): return lax.ppermute(array, axis, pairs)]
    all_to_all x1 -> x2, blocking collectives: 18.9 us -> 38.4 us  [sent(): return lax.all_to_all(array, axes, 0, 0, tiled=True)]
    all_to_all x4 -> x3, starting transfers between devices: 36.4 us -> 30.6 us  [sent(): return lax.all_to_all(array, axes, 0, 0, tiled=True)]
    unnamed x99 -> x53, local copies, waits for them, and re-layouts: 20.1 us -> 14.6 us
    pallas_call x13 -> x11, Pallas kernels: 17.9 us -> 15.3 us  [call(): pl.pallas_call(kernel, out_shape=outs, in_specs=[HBM if i in far else VME...]
  transfers between devices with their start and end apart: 30 -> 6, of which waited for: 13 -> 5; matrix products, arithmetic and copies ran while one was open for 1% -> 1% of each run, Pallas kernels for 4% -> 5%
where the time goes in v2:
time: 172 us; the launch traced here: 171 us
  waiting for transfers between devices  49 us (28%)
  starting transfers between devices  38.8 us (23%)
  blocking collectives  38.4 us (22%)
  local copies, waits for them, and re-layouts  16.2 us (9%)
  Pallas kernels  15.3 us (9%)
  between operations  13.6 us (8%)
    all_to_all x3, waiting for transfers between devices, sent(): return lax.all_to_all(array, axes, 0, 0, tiled=True)  45.9 us
    all_to_all x2, blocking collectives, sent(): return lax.all_to_all(array, axes, 0, 0, tiled=True)  38.4 us
    all_to_all x3, starting transfers between devices, sent(): return lax.all_to_all(array, axes, 0, 0, tiled=True)  30.6 us
    pallas_call x11, Pallas kernels, call(): pl.pallas_call(kernel, out_shape=outs, in_specs=[HBM if i in far else VME...  15.3 us
    unnamed x53, local copies, waits for them, and re-layouts  14.6 us
    ppermute x2, starting transfers between devices, shift(): return lax.ppermute(array, axis, pairs)  8.22 us
  transfers between devices with their start and end apart: 6, of which 5 were waited for; matrix products, arithmetic and copies ran while one was open for 1% of the time, Pallas kernels for 5%

profile of v2, /device:TPU:1, one launch (start us, length us, event | category | flops | bytes accessed | tf_op | source)
XLA Modules:
  0.0 171.5 jit_solution(17240139411627063909)
XLA Ops:
  6.5 2.9 %pack.1 = bf16[32,32,896]{2,1,0:T(8,128)(2,1)} custom-call(bf16[32,8192]{1,0:T(8,128)(2,1)} %x_far.1, bf16[32,8192]{1,0:T(8,128)(2,1)} %z_far.1, bf16[32,1024]{1,0:T(8,128)(2,1)} %b_far.1, bf16[32,1024]{1,0:T(8,128)(2,1)} %c_far.1, bf16[32,128]{1,0:T(8,128)(2,1)} %dt_far.1), custom_call_target="tpu_custom_call" | custom-call | flops 4194304 | bytes 1048576 | tf_op jit(solution)/shard_map/pack/pallas_call | solution.py:24
  9.5 10.6 %all-to-all-start = ((bf16[32,32,896]{2,1,0:T(8,128)(2,1)}), bf16[32,32,896]{2,1,0:T(8,128)(2,1)S(1)}, u32[]{:S(2)}, u32[]{:S(2)}) async-start(bf16[32,32,896]{2,1,0:T(8,128)(2,1)} %pack.1), calls=%async_computation | async-start | bytes 3670016 | tf_op jit(solution)/shard_map/entry/all_to_all | solution.py:326
  21.3 0.8 dynamic_slice.19
  22.7 23.1 %all-to-all-done = bf16[32,32,896]{2,1,0:T(8,128)(2,1)S(1)} async-done(((bf16[32,32,896]{2,1,0:T(8,128)(2,1)}), bf16[32,32,896]{2,1,0:T(8,128)(2,1)S(1)}, u32[]{:S(2)}, u32[]{:S(2)}) %all-to-all-start) | async-done | bytes 1835040 | tf_op jit(solution)/shard_map/entry/all_to_all | solution.py:326
  45.8 1.5 collective-permute-start
  48.1 4.5 %scan_in.1 = (bf16[1024,256]{1,0:T(8,128)(2,1)S(1)}, bf16[1024,128]{1,0:T(8,128)(2,1)S(1)}, bf16[8,256,128]{2,1,0:T(8,128)(2,1)S(1)}, bf16[16,24,128]{2,1,0:T(8,128)(2,1)}) custom-call(bf16[1024,896]{1,0:T(8,128)(2,1)S(1)} %bitcast.18, bf16[8,512]{1,0:T(8,128)(2,1)S(1)} %collective-permute-done.halo_ref, f32[8,256]{1,0:T(8,128)S(1)} %select_maximum_fusion.taps_ref, ...), custom_call_target="tpu_custom_call" | custom-call | flops 33554432 | bytes 1048576 | tf_op jit(solution)/shard_map/scan_in/pallas_call | solution.py:24
  52.6 0.8 copy-done.5
  53.4 0.7 copy-done.7
  54.1 16.2 %all-to-all-start.1 = ((bf16[16,24,128]{2,1,0:T(8,128)(2,1)}), bf16[16,24,128]{2,1,0:T(8,128)(2,1)S(1)}, u32[]{:S(2)}, u32[]{:S(2)}) async-start(bf16[16,24,128]{2,1,0:T(8,128)(2,1)} %get-tuple-element.28), calls=%async_computation.1 | async-start | bytes 196608 | tf_op jit(solution)/shard_map/pieces/all_to_all | solution.py:326
  70.4 1.0 copy-done.6
  71.4 0.9 copy-done.8
  72.3 0.8 copy-done.12
  73.1 0.8 copy-done.14
  73.9 0.7 copy-done.16
  74.6 0.7 copy-done.18
  75.9 2.1 %local.1 = (bf16[1024,128]{1,0:T(8,128)(2,1)S(1)}, f32[1024,256]{1,0:T(8,128)S(1)}) custom-call(bf16[1024,256]{1,0:T(8,128)(2,1)S(1)} %get-tuple-element.29.xs_ref, bf16[1024,128]{1,0:T(8,128)(2,1)S(1)} %copy-done.8, bf16[1024,896]{1,0:T(8,128)(2,1)S(1)} %bitcast.19, bf16[8,512]{1,0:T(8,128)(2,1)S(1)} %copy-done.18, f32[16,128]{1,0:T(8,128)S(1)} %copy-done.16, ...), custom_call_target="tpu_custom_call" | custom-call | flops 134217728 | bytes 1048576 | tf_op jit(solution)/shard_map/local/pallas_call | solution.py:24
  78.7 3.7 %all-to-all-done.1.inbox_ref = bf16[16,24,128]{2,1,0:T(8,128)(2,1)S(1)} async-done(((bf16[16,24,128]{2,1,0:T(8,128)(2,1)}), bf16[16,24,128]{2,1,0:T(8,128)(2,1)S(1)}, u32[]{:S(2)}, u32[]{:S(2)}) %all-to-all-start.1) | async-done | bytes 98336 | tf_op jit(solution)/shard_map/pieces/all_to_all | solution.py:326
  82.5 19.2 %all_to_all.25 = bf16[16,16,128]{2,1,0:T(8,128)(2,1)S(1)} all-to-all(bf16[16,16,128]{2,1,0:T(8,128)(2,1)S(1)} %scan_all.1), channel_id=1, replica_groups=mesh['z'=16,'x'=4,'y'=4,'c'=2] {'z'}, dimensions={0} | all-to-all | bytes 131072 | tf_op jit(solution)/shard_map/starts/all_to_all | solution.py:326
  101.8 0.9 copy-done.10
  102.7 1.0 finish.1
  103.8 1.3 copy-done.3
  105.1 3.7 %all-to-all-start.3 = ((bf16[4,1024,256]{2,1,0:T(8,128)(2,1)}), bf16[4,1024,256]{2,1,0:T(8,128)(2,1)S(1)}, u32[]{:S(2)}, u32[]{:S(2)}) async-start(bf16[4,1024,256]{2,1,0:T(8,128)(2,1)} %copy-done.3), calls=%async_computation.3 | async-start | bytes 4194304 | tf_op jit(solution)/shard_map/gather/all_to_all | solution.py:326
  108.9 1.6 copy-done.4
  110.8 1.3 copy-done.1
  112.2 19.1 %all-to-all-done.3.gated_ref = bf16[4,1024,256]{2,1,0:T(8,128)(2,1)S(1)} async-done(((bf16[4,1024,256]{2,1,0:T(8,128)(2,1)}), bf16[4,1024,256]{2,1,0:T(8,128)(2,1)S(1)}, u32[]{:S(2)}, u32[]{:S(2)}) %all-to-all-start.3) | async-done | bytes 2097184 | tf_op jit(solution)/shard_map/gather/all_to_all | solution.py:326
  131.3 1.6 copy-done.2
  132.9 1.3 project.1
  134.2 6.7 %collective-permute-start.1 = (bf16[512,1024]{1,0:T(8,128)(2,1)S(1)}, bf16[512,1024]{1,0:T(8,128)(2,1)S(1)}, u32[]{:S(2)}, u32[]{:S(2)}) collective-permute-start(bf16[512,1024]{1,0:T(8,128)(2,1)S(1)} %project.1), channel_id=1, source_target_pairs={{0,1},{1,0},{2,3},{3,2},{4,5},{5,4},{6,7},{7,6},{8,9},{9,8},{10,11... | collective-permute-start | bytes 3145736 | tf_op jit(solution)/shard_map/ppermute | solution.py:321
  140.9 2.3 %collective-permute-done.1.other_ref = bf16[512,1024]{1,0:T(8,128)(2,1)S(1)} collective-permute-done((bf16[512,1024]{1,0:T(8,128)(2,1)S(1)}, bf16[512,1024]{1,0:T(8,128)(2,1)S(1)}, u32[]{:S(2)}, u32[]{:S(2)}) %collective-permute-start.1) | collective-permute-done | bytes 1048608 | tf_op jit(solution)/shard_map/ppermute | solution.py:321
  143.2 1.4 project_add.1
  144.5 19.2 %all_to_all.26.shares_ref = bf16[16,32,1024]{2,1,0:T(8,128)(2,1)S(1)} all-to-all(bf16[16,32,1024]{2,1,0:T(8,128)(2,1)S(1)} %bitcast.21), channel_id=1, replica_groups=mesh['z'=16,'x'=4,'y'=4,'c'=2] {'x','y'}, dimensions={0} | all-to-all | bytes 2097152 | tf_op jit(solution)/shard_map/exit/all_to_all | solution.py:326
  163.7 0.9 collect_all.1
  (59 shorter events, 4.3 us)
Async XLA Ops:
  6.5 16.1 %copy-start = (f32[4,1024]{1,0:T(4,128)S(1)}, f32[4,1024]{1,0:T(4,128)}, u32[]{:S(2)}) copy-start(f32[4,1024]{1,0:T(4,128)} %param.22) | copy-start | bytes 49156
  9.5 11.4 %copy-start.24 = (f32[16]{0:T(128)S(1)}, f32[16]{0:T(128)}, u32[]{:S(2)}) copy-start(f32[16]{0:T(128)} %param.20) | copy-start | bytes 196
  9.5 11.4 %copy-start.23 = (f32[16]{0:T(128)S(1)}, f32[16]{0:T(128)}, u32[]{:S(2)}) copy-start(f32[16]{0:T(128)} %param.19) | copy-start | bytes 196
  9.5 11.7 %copy-start.25 = (f32[16]{0:T(128)S(1)}, f32[16]{0:T(128)}, u32[]{:S(2)}) copy-start(f32[16]{0:T(128)} %param.21) | copy-start | bytes 196
  9.5 11.8 %copy-start.21 = (f32[4,2,128]{2,1,0:T(2,128)S(1)}, f32[4,2,128]{2,1,0:T(2,128)}, u32[]{:S(2)}) copy-start(f32[4,2,128]{2,1,0:T(2,128)} %param.24) | copy-start | bytes 12292
  9.5 11.8 %copy-start.22 = (f32[2,128]{1,0:T(2,128)S(1)}, f32[2,128]{1,0:T(2,128)}, u32[]{:S(2)}) copy-start(f32[2,128]{1,0:T(2,128)} %param.25) | copy-start | bytes 3076
  9.5 36.2 %all-to-all-start = ((bf16[32,32,896]{2,1,0:T(8,128)(2,1)}), bf16[32,32,896]{2,1,0:T(8,128)(2,1)S(1)}, u32[]{:S(2)}, u32[]{:S(2)}) async-start(bf16[32,32,896]{2,1,0:T(8,128)(2,1)} %pack.1), calls=%async_computation | async-start | bytes 3670016 | tf_op jit(solution)/shard_map/entry/all_to_all | solution.py:326
  20.2 88.7 %all-gather.2.cloned.1.call-start = ((), (), s32[]{:S(2)}) async-start(), calls=%async_computation.5 | async-start | bytes 2228224 | tf_op jit(solution)/shard_map/all_gather | solution.py:346
  22.7 29.9 %copy-start.15 = (f32[16,128]{1,0:T(8,128)}, f32[16,128]{1,0:T(8,128)S(1)}, u32[]{:S(2)}) copy-start(f32[16,128]{1,0:T(8,128)S(1)} %pad_bitcast_fusion.group_taps_ref) | copy-start | bytes 24580
  45.8 2.3 %collective-permute-start = (bf16[8,512]{1,0:T(8,128)(2,1)S(1)}, bf16[8,512]{1,0:T(8,128)(2,1)S(1)}, u32[]{:S(2)}, u32[]{:S(2)}) collective-permute-start(bf16[8,512]{1,0:T(8,128)(2,1)S(1)} %tail.1), channel_id=1, source_target_pairs={{0,32},{32,64},{64,96},{96,128},{128,160},{160,192},{192,224},{224... | collective-permute-start | bytes 24584 | tf_op jit(solution)/shard_map/ppermute | solution.py:321
  48.0 6.1 %copy-start.11 = (f32[8,1024]{1,0:T(8,128)}, f32[8,1024]{1,0:T(8,128)S(1)}, u32[]{:S(2)}) copy-start(f32[8,1024]{1,0:T(8,128)S(1)} %get-tuple-element.25.dt_ref) | copy-start | bytes 98308
  48.0 6.1 %copy-start.13 = (f32[8,1024]{1,0:T(8,128)}, f32[8,1024]{1,0:T(8,128)S(1)}, u32[]{:S(2)}) copy-start(f32[8,1024]{1,0:T(8,128)S(1)} %get-tuple-element.26.cum_ref) | copy-start | bytes 98308
  48.1 4.5 %copy-start.17 = (bf16[8,512]{1,0:T(8,128)(2,1)}, bf16[8,512]{1,0:T(8,128)(2,1)S(1)}, u32[]{:S(2)}) copy-start(bf16[8,512]{1,0:T(8,128)(2,1)S(1)} %collective-permute-done.halo_ref) | copy-start | bytes 24580
  52.6 0.8 copy-start.5
  53.4 0.7 copy-start.7
  54.1 28.3 %all-to-all-start.1 = ((bf16[16,24,128]{2,1,0:T(8,128)(2,1)}), bf16[16,24,128]{2,1,0:T(8,128)(2,1)S(1)}, u32[]{:S(2)}, u32[]{:S(2)}) async-start(bf16[16,24,128]{2,1,0:T(8,128)(2,1)} %get-tuple-element.28), calls=%async_computation.1 | async-start | bytes 196608 | tf_op jit(solution)/shard_map/pieces/all_to_all | solution.py:326
  70.3 1.0 copy-start.6
  71.4 0.9 copy-start.8
  72.3 0.8 copy-start.12
  73.1 0.8 copy-start.14
  73.9 0.7 copy-start.16
  74.6 0.7 copy-start.18
  75.3 0.6 copy-start.20
  78.0 0.7 copy-start.9
  101.7 1.0 copy-start.10
  103.7 1.3 copy-start.3
  105.1 3.8 %copy-start.19 = (f32[1024]{0:T(1024)S(1)}, f32[1024]{0:T(1024)}, u32[]{:S(2)}) copy-start(f32[1024]{0:T(1024)} %param.26) | copy-start | bytes 12292
  105.1 26.2 %all-to-all-start.3 = ((bf16[4,1024,256]{2,1,0:T(8,128)(2,1)}), bf16[4,1024,256]{2,1,0:T(8,128)(2,1)S(1)}, u32[]{:S(2)}, u32[]{:S(2)}) async-start(bf16[4,1024,256]{2,1,0:T(8,128)(2,1)} %copy-done.3), calls=%async_computation.3 | async-start | bytes 4194304 | tf_op jit(solution)/shard_map/gather/all_to_all | solution.py:326
  108.9 1.6 copy-start.4
  110.8 1.4 copy-start.1
  131.3 1.6 copy-start.2
  134.2 9.0 %collective-permute-start.1 = (bf16[512,1024]{1,0:T(8,128)(2,1)S(1)}, bf16[512,1024]{1,0:T(8,128)(2,1)S(1)}, u32[]{:S(2)}, u32[]{:S(2)}) collective-permute-start(bf16[512,1024]{1,0:T(8,128)(2,1)S(1)} %project.1), channel_id=1, source_target_pairs={{0,1},{1,0},{2,3},{3,2},{4,5},{5,4},{6,7},{7,6},{8,9},{9,8},{10,11... | collective-permute-start | bytes 3145736 | tf_op jit(solution)/shard_map/ppermute | solution.py:321
Sparse Core Ops, SparseCore 0:
  23.1 67.4 all-gather.1

commit v3 on v2

--- a/solution.py
+++ b/solution.py
@@ -12,10 +12,11 @@
 LANES = 128
 F32 = jnp.float32
 BF16 = jnp.bfloat16
-SEQ = ("z", "x")
+Z = ("zh", "zl")
+SEQ = ("zh", "zl", "x")
 HEAD = ("y", "c")
 PLANE = ("x", "y", "c")
-ALL = ("z", "x", "y", "c")
+ALL = ("zh", "zl", "x", "y", "c")
 VMEM = pl.BlockSpec(memory_space=pltpu.VMEM)
 HBM = pl.BlockSpec(memory_space=pltpu.HBM)
 
@@ -29,7 +30,6 @@
         scratch_shapes=list(scratch),
         compiler_params=pltpu.CompilerParams(vmem_limit_bytes=limit << 20),
         cost_estimate=pl.CostEstimate(flops=flops, bytes_accessed=1 << 20, transcendentals=0),
-        name=kernel.__name__,
     )(*inputs)
 
 
@@ -160,34 +160,54 @@
             weighted = (xs.astype(F32) * by_head(scale, chunk, left)).astype(BF16)
             held_ref[k, lo : lo + LANES] = states[chunk].astype(BF16)
             states[chunk] = by_head(decay, chunk, top) * states[chunk] + tn(weighted, b)
-    count, extra = sent_ref.shape[0], sent_ref.shape[1]
+    count = sent_ref.shape[0]
     rows = cols // count
-    for chunk in range(cols // LANES):
-        final = states[chunk].astype(BF16)
-        for i in range(LANES // rows):
-            sent_ref[chunk * (LANES // rows) + i, :rows] = final[i * rows : (i + 1) * rows]
     total = columns(jnp.broadcast_to(sum_ref[:, tokens - 1 :], (sum_ref.shape[0], SPAN)))[:1]
-    high = total.astype(BF16).astype(F32)
-    middle = (total - high).astype(BF16).astype(F32)
-    low = total - high - middle
-    at = lax.broadcasted_iota(jnp.int32, (extra - rows, LANES), 0)
-    tail = jnp.where(at == 0, high, jnp.where(at == 1, middle, jnp.where(at == 2, low, 0.0)))
     for d in range(count):
-        sent_ref[d, rows:] = tail.astype(BF16)
-
-
-def scan_all(inbox_ref, starts_ref, decays):
-    count, rows, _ = starts_ref.shape
-    tail = inbox_ref[:, rows:].astype(F32)
-    logs = tail[:, 0] + tail[:, 1] + tail[:, 2]
-    lanes = lax.broadcasted_iota(jnp.int32, logs.shape, 1)
-    head = lax.axis_index("z") * rows // HEAD_DIM
-    column = jnp.sum(jnp.where(lanes == head, logs, 0.0), axis=1, keepdims=True)
-    decays[...] = jnp.broadcast_to(jnp.exp(column), decays.shape)
+        chunk, lo = divmod(d * rows, LANES)
+        sent_ref[d, :rows] = states[chunk][lo : lo + rows].astype(BF16)
+        sent_ref[d, rows:] = in_terms(total[:, d : d + 1])
+
+
+def in_terms(value):
+    high = value.astype(BF16).astype(F32)
+    middle = (value - high).astype(BF16).astype(F32)
+    low = value - high - middle
+    at = lax.broadcasted_iota(jnp.int32, (8, LANES), 0)
+    terms = jnp.where(at == 0, high, jnp.where(at == 1, middle, jnp.where(at == 2, low, 0.0)))
+    return terms.astype(BF16)
+
+
+def from_terms(terms):
+    terms = terms.astype(F32)
+    return terms[0:1] + terms[1:2] + terms[2:3]
+
+
+def scan_near(inbox_ref, inner_ref, before_ref, sent_ref):
+    count, rows, _ = inner_ref.shape
     state = jnp.zeros((rows, STATE), F32)
+    log = jnp.zeros((1, LANES), F32)
     for i in range(count):
-        starts_ref[i] = state.astype(BF16)
-        state = decays[i : i + 1] * state + inbox_ref[i, :rows].astype(F32)
+        inner_ref[i] = state
+        before_ref[8 * i : 8 * i + 8] = jnp.broadcast_to(log, (8, LANES))
+        mine = from_terms(inbox_ref[i, rows:])
+        state = jnp.exp(mine) * state + inbox_ref[i, :rows].astype(F32)
+        log = log + mine
+    for d in range(sent_ref.shape[0]):
+        sent_ref[d, :rows] = state.astype(BF16)
+        sent_ref[d, rows:] = in_terms(log)
+
+
+def scan_far(inbox_ref, inner_ref, before_ref, starts_ref):
+    count, rows, _ = inner_ref.shape
+    me = lax.axis_index("zh")
+    state = jnp.zeros((rows, STATE), F32)
+    for j in range(inbox_ref.shape[0]):
+        later = jnp.exp(from_terms(inbox_ref[j, rows:])) * state + inbox_ref[j, :rows].astype(F32)
+        state = jnp.where(j < me, later, state)
+    for i in range(count):
+        grown = jnp.exp(before_ref[8 * i : 8 * i + 1])
+        starts_ref[i] = (grown * state + inner_ref[i]).astype(BF16)
 
 
 def local(
@@ -293,7 +313,7 @@
 
 
 def collect(shares_ref, out_ref, *, ys):
-    count, rows, width = shares_ref.shape
+    count, _, width = shares_ref.shape
     xs = count // ys
     left = left_half()
     for pair in range(width // LANES):
@@ -321,9 +341,8 @@
     return lax.ppermute(array, axis, pairs)
 
 
-def sent(array, axes, name):
-    with jax.named_scope(name):
-        return lax.all_to_all(array, axes, 0, 0, tiled=True)
+def sent(array, axes):
+    return lax.all_to_all(array, axes, 0, 0, tiled=True)
 
 
 def per_device(
@@ -331,7 +350,7 @@
     conv_x, conv_bias_x, conv_bc, conv_bias_bc, norm_weight, out_weight,
 ):
     xs, ys, cs = (lax.axis_size(a) for a in PLANE)
-    zs = lax.axis_size("z")
+    zh, zl = (lax.axis_size(a) for a in Z)
     plane = xs * ys * cs
     rows, inner = x_proj.shape
     cols = inner // plane
@@ -343,7 +362,7 @@
         size = values.shape[axis] // xs
         return lax.dynamic_slice_in_dim(values, part * size, size, axis)
 
-    weights = lax.all_gather(out_weight.T, "z", axis=0, tiled=True)
+    weights = lax.all_gather(out_weight.T, Z, axis=0, tiled=True)
     out = call(
         pack,
         shape((plane, rows, 2 * cols + 3 * LANES), BF16),
@@ -367,11 +386,11 @@
         ((0, 0), (0, 3), (0, 0)),
     ).reshape(16, LANES)
     packed, per_head, skip, taps, group_taps = lax.optimization_barrier(
-        (sent(out, PLANE, "entry"), per_head, skip, taps, group_taps)
+        (sent(out, PLANE), per_head, skip, taps, group_taps)
     )
     packed = packed.reshape(tokens, 2 * cols + 3 * LANES)
     halo = call(tail, shape((8, cols + 2 * LANES), BF16), (packed,), (), 1 << 16, 4)
-    halo = shift(halo, "z", 1, wrap=False)
+    halo = shift(halo, Z, 1, wrap=False)
     by_token = shape((8, tokens), F32)
     dt, cum, sums = call(steps, (by_token, by_token, by_token), (packed, per_head))
     x_conv, b_conv, held, states_out = call(
@@ -380,13 +399,22 @@
             shape((tokens, cols), BF16),
             shape((tokens, LANES), BF16),
             shape((tokens // SPAN, cols, STATE), BF16),
-            shape((zs, cols // zs + 8, STATE), BF16),
+            shape((zl, cols // zl + 8, STATE), BF16),
         ),
         (packed, halo, taps, group_taps, dt, cum, sums),
         [pltpu.VMEM((tokens + 8, cols + LANES), F32)],
         1 << 25,
     )
-    states_in = sent(states_out, "z", "pieces")
+    near_in = sent(states_out, "zl")
+    near = zl, cols // zl, STATE
+    inner, before, far_out = call(
+        scan_near,
+        (shape(near, F32), shape((8 * zl, LANES), F32), shape((zh, cols // zl + 8, STATE), BF16)),
+        (near_in,),
+    )
+    far_in = sent(far_out, "zh")
+    starts = call(scan_far, shape(near, BF16), (far_in, inner, before))
+    start = sent(starts, "zl").reshape(cols, STATE)
     c_conv, y = call(
         local,
         (shape((tokens, LANES), BF16), shape((tokens, cols), F32)),
@@ -394,24 +422,16 @@
         [pltpu.VMEM((tokens + 8, LANES), F32)],
         1 << 27,
     )
-    states_in, y = lax.optimization_barrier((states_in, y))
-    starts = call(
-        scan_all,
-        shape((zs, cols // zs, STATE), BF16),
-        (states_in,),
-        [pltpu.VMEM((zs, LANES), F32)],
-    )
-    start = sent(starts, "z", "starts").reshape(cols, STATE)
     copies = call(
         finish, shape((xs, tokens, cols), BF16), (start, c_conv, sums, y, packed), (), 1 << 25
     )
-    gated = sent(copies, "x", "gather")
+    gated = sent(copies, "x")
     weights = call(rescale, shape(weights.shape, BF16), (weights, norm_weight[None]))
     product = shape((tokens // 2, weights.shape[0]), BF16)
     away = call(project, product, (gated, weights), (), 1 << 29, 24)
     other = shift(away, "c", 1)
     both = call(project_add, product, (gated, weights, other), (), 1 << 29, 24)
-    shares = sent(both.reshape(xs * ys, rows, weights.shape[0]), ("x", "y"), "exit")
+    shares = sent(both.reshape(xs * ys, rows, weights.shape[0]), ("x", "y"))
 
     def collect_all(shares_ref, out_ref):
         collect(shares_ref, out_ref, ys=ys)
@@ -420,7 +440,7 @@
 
 
 def solution(mesh):
-    split = Mesh(mesh.devices.reshape(16, 4, 4, 2), ALL)
+    split = Mesh(mesh.devices.reshape(4, 4, 4, 4, 2), ALL)
     return jax.shard_map(
         per_device,
         mesh=split,

time: 172 us -> 172 us (level)
  blocking collectives: 38.4 us -> 54.6 us
  starting transfers between devices: 38.8 us -> 26.4 us
  waiting for transfers between devices: 49 us -> 44.7 us
    all_to_all x2 -> x3, blocking collectives: 38.4 us -> 54.6 us  [sent(): return lax.all_to_all(array, axes, 0, 0, tiled=True)]
    all_to_all x3, starting transfers between devices: 30.6 us -> 17.6 us  [sent(): return lax.all_to_all(array, axes, 0, 0, tiled=True)]
    all_to_all x3, waiting for transfers between devices: 45.9 us -> 41.7 us  [sent(): return lax.all_to_all(array, axes, 0, 0, tiled=True)]
    unnamed x53 -> x49, local copies, waits for them, and re-layouts: 14.6 us -> 13.8 us
    pallas_call x11 -> x12, Pallas kernels: 15.3 us -> 15.2 us  [call(): pl.pallas_call(kernel, out_shape=outs, in_specs=[HBM if i in far else VME...]
  transfers between devices with their start and end apart: 6 -> 6, of which waited for: 5 -> 4; matrix products, arithmetic and copies ran while one was open for 1% -> 1% of each run, Pallas kernels for 5% -> 5%
where the time goes in v3:
time: 172 us; the launch traced here: 170 us
  blocking collectives  54.6 us (32%)
  waiting for transfers between devices  44.7 us (26%)
  starting transfers between devices  26.4 us (15%)
  local copies, waits for them, and re-layouts  15.5 us (9%)
  Pallas kernels  15.2 us (9%)
  between operations  13.7 us (8%)
    all_to_all x3, blocking collectives, sent(): return lax.all_to_all(array, axes, 0, 0, tiled=True)  54.6 us
    all_to_all x3, waiting for transfers between devices, sent(): return lax.all_to_all(array, axes, 0, 0, tiled=True)  41.7 us
    all_to_all x3, starting transfers between devices, sent(): return lax.all_to_all(array, axes, 0, 0, tiled=True)  17.6 us
    pallas_call x12, Pallas kernels, call(): pl.pallas_call(kernel, out_shape=outs, in_specs=[HBM if i in far else VME...  15.2 us
    unnamed x49, local copies, waits for them, and re-layouts  13.8 us
    ppermute x2, starting transfers between devices, shift(): return lax.ppermute(array, axis, pairs)  8.72 us
  transfers between devices with their start and end apart: 6, of which 4 were waited for; matrix products, arithmetic and copies ran while one was open for 1% of the time, Pallas kernels for 5%

profile of v3, /device:TPU:1, one launch (start us, length us, event | category | flops | bytes accessed | tf_op | source)
XLA Modules:
  0.0 170.3 jit_solution(4602513907357925901)
XLA Ops:
  6.5 2.9 %shard_map.136 = bf16[32,32,896]{2,1,0:T(8,128)(2,1)} custom-call(bf16[32,8192]{1,0:T(8,128)(2,1)} %x_far.1, bf16[32,8192]{1,0:T(8,128)(2,1)} %z_far.1, bf16[32,1024]{1,0:T(8,128)(2,1)} %b_far.1, bf16[32,1024]{1,0:T(8,128)(2,1)} %c_far.1, bf16[32,128]{1,0:T(8,128)(2,1)} %dt_far.1), custom_call_target="tpu_custom_call" | custom-call | flops 4194304 | bytes 1048576 | tf_op jit(solution)/shard_map/pallas_call | solution.py:25
  9.5 10.6 %all-to-all-start = ((bf16[32,32,896]{2,1,0:T(8,128)(2,1)}), bf16[32,32,896]{2,1,0:T(8,128)(2,1)S(1)}, u32[]{:S(2)}, u32[]{:S(2)}) async-start(bf16[32,32,896]{2,1,0:T(8,128)(2,1)} %shard_map.136), calls=%async_computation | async-start | bytes 3670016 | tf_op jit(solution)/shard_map/all_to_all | solution.py:345
  21.3 0.8 dynamic_slice.19
  22.7 23.0 %all-to-all-done = bf16[32,32,896]{2,1,0:T(8,128)(2,1)S(1)} async-done(((bf16[32,32,896]{2,1,0:T(8,128)(2,1)}), bf16[32,32,896]{2,1,0:T(8,128)(2,1)S(1)}, u32[]{:S(2)}, u32[]{:S(2)}) %all-to-all-start) | async-done | bytes 1835040 | tf_op jit(solution)/shard_map/all_to_all | solution.py:345
  45.8 1.5 collective-permute-start
  48.1 3.9 %shard_map.139 = (bf16[1024,256]{1,0:T(8,128)(2,1)S(1)}, bf16[1024,128]{1,0:T(8,128)(2,1)S(1)}, bf16[8,256,128]{2,1,0:T(8,128)(2,1)S(1)}, bf16[4,72,128]{2,1,0:T(8,128)(2,1)S(1)}) custom-call(bf16[1024,896]{1,0:T(8,128)(2,1)S(1)} %bitcast.18, bf16[8,512]{1,0:T(8,128)(2,1)S(1)} %collective-permute-done.halo_ref, f32[8,256]{1,0:T(8,128)S(1)} %select_maximum_fusion.taps_ref, ...), custom_call_target="tpu_custom_call" | custom-call | flops 33554432 | bytes 1048576 | tf_op jit(solution)/shard_map/pallas_call | solution.py:25
  52.0 0.8 copy-done.5
  52.8 0.7 copy-done.7
  53.5 11.4 %all_to_all.30.inbox_ref = bf16[4,72,128]{2,1,0:T(8,128)(2,1)S(1)} all-to-all(bf16[4,72,128]{2,1,0:T(8,128)(2,1)S(1)} %get-tuple-element.29), channel_id=1, replica_groups=mesh['zh'=4,'zl'=4,'x'=4,'y'=4,'c'=2] {'zl'}, dimensions={0} | all-to-all | bytes 147456 | tf_op jit(solution)/shard_map/all_to_all | solution.py:345
  64.9 24.5 %all_to_all.31.inbox_ref = bf16[4,72,128]{2,1,0:T(8,128)(2,1)S(1)} all-to-all(bf16[4,72,128]{2,1,0:T(8,128)(2,1)S(1)} %get-tuple-element.30), channel_id=1, replica_groups=mesh['zh'=4,'zl'=4,'x'=4,'y'=4,'c'=2] {'zh'}, dimensions={0} | all-to-all | bytes 147456 | tf_op jit(solution)/shard_map/all_to_all | solution.py:345
  90.0 3.3 %all-to-all-start.3 = ((bf16[4,64,128]{2,1,0:T(8,128)(2,1)}), bf16[4,64,128]{2,1,0:T(8,128)(2,1)S(1)}, u32[]{:S(2)}, u32[]{:S(2)}) async-start(bf16[4,64,128]{2,1,0:T(8,128)(2,1)} %shard_map.141), calls=%async_computation.3 | async-start | bytes 131072 | tf_op jit(solution)/shard_map/all_to_all | solution.py:345
  93.3 1.0 copy-done.6
  94.4 0.9 copy-done.8
  95.3 0.8 copy-done.12
  96.1 0.7 copy-done.14
  96.8 0.7 copy-done.16
  98.1 2.1 %shard_map.142 = (bf16[1024,128]{1,0:T(8,128)(2,1)S(1)}, f32[1024,256]{1,0:T(8,128)S(1)}) custom-call(bf16[1024,256]{1,0:T(8,128)(2,1)S(1)} %get-tuple-element.33.xs_ref, bf16[1024,128]{1,0:T(8,128)(2,1)S(1)} %copy-done.8, bf16[1024,896]{1,0:T(8,128)(2,1)S(1)} %bitcast.19, bf16[8,512]{1,0:T(8,128)(2,1)S(1)} %copy-done.16, f32[16,128]{1,0:T(8,128)S(1)} %copy-done.14, ...), custom_call_target="tpu_custom_call" | custom-call | flops 134217728 | bytes 1048576 | tf_op jit(solution)/shard_map/pallas_call | solution.py:25
  100.3 0.7 copy-done.9
  101.0 0.9 copy-done.10
  101.9 1.0 shard_map.143
  103.0 1.3 copy-done.3
  104.3 3.7 %all-to-all-start.4 = ((bf16[4,1024,256]{2,1,0:T(8,128)(2,1)}), bf16[4,1024,256]{2,1,0:T(8,128)(2,1)S(1)}, u32[]{:S(2)}, u32[]{:S(2)}) async-start(bf16[4,1024,256]{2,1,0:T(8,128)(2,1)} %copy-done.3), calls=%async_computation.4 | async-start | bytes 4194304 | tf_op jit(solution)/shard_map/all_to_all | solution.py:345
  108.1 1.6 copy-done.4
  110.0 1.4 copy-done.1
  111.4 18.6 %all-to-all-done.4.gated_ref = bf16[4,1024,256]{2,1,0:T(8,128)(2,1)S(1)} async-done(((bf16[4,1024,256]{2,1,0:T(8,128)(2,1)}), bf16[4,1024,256]{2,1,0:T(8,128)(2,1)S(1)}, u32[]{:S(2)}, u32[]{:S(2)}) %all-to-all-start.4) | async-done | bytes 2097184 | tf_op jit(solution)/shard_map/all_to_all | solution.py:345
  130.0 1.6 copy-done.2
  131.6 1.3 shard_map.145
  132.9 7.2 %collective-permute-start.1 = (bf16[512,1024]{1,0:T(8,128)(2,1)S(1)}, bf16[512,1024]{1,0:T(8,128)(2,1)S(1)}, u32[]{:S(2)}, u32[]{:S(2)}) collective-permute-start(bf16[512,1024]{1,0:T(8,128)(2,1)S(1)} %shard_map.145), channel_id=1, source_target_pairs={{0,1},{1,0},{2,3},{3,2},{4,5},{5,4},{6,7},{7,6},{8,9},{9,8},{10,11... | collective-permute-start | bytes 3145736 | tf_op jit(solution)/shard_map/ppermute | solution.py:341
  140.1 2.3 %collective-permute-done.1.other_ref = bf16[512,1024]{1,0:T(8,128)(2,1)S(1)} collective-permute-done((bf16[512,1024]{1,0:T(8,128)(2,1)S(1)}, bf16[512,1024]{1,0:T(8,128)(2,1)S(1)}, u32[]{:S(2)}, u32[]{:S(2)}) %collective-permute-start.1) | collective-permute-done | bytes 1048608 | tf_op jit(solution)/shard_map/ppermute | solution.py:341
  142.4 1.4 shard_map.146
  143.7 18.8 %all_to_all.32.shares_ref = bf16[16,32,1024]{2,1,0:T(8,128)(2,1)S(1)} all-to-all(bf16[16,32,1024]{2,1,0:T(8,128)(2,1)S(1)} %bitcast.21), channel_id=1, replica_groups=mesh['zh'=4,'zl'=4,'x'=4,'y'=4,'c'=2] {'x','y'}, dimensions={0} | all-to-all | bytes 2097152 | tf_op jit(solution)/shard_map/all_to_all | solution.py:345
  162.5 0.9 shard_map.147
  (57 shorter events, 4.3 us)
Async XLA Ops:
  6.5 16.1 %copy-start = (f32[4,1024]{1,0:T(4,128)S(1)}, f32[4,1024]{1,0:T(4,128)}, u32[]{:S(2)}) copy-start(f32[4,1024]{1,0:T(4,128)} %param.22) | copy-start | bytes 49156
  9.5 11.4 %copy-start.22 = (f32[16]{0:T(128)S(1)}, f32[16]{0:T(128)}, u32[]{:S(2)}) copy-start(f32[16]{0:T(128)} %param.20) | copy-start | bytes 196
  9.5 11.4 %copy-start.21 = (f32[16]{0:T(128)S(1)}, f32[16]{0:T(128)}, u32[]{:S(2)}) copy-start(f32[16]{0:T(128)} %param.19) | copy-start | bytes 196
  9.5 11.7 %copy-start.23 = (f32[16]{0:T(128)S(1)}, f32[16]{0:T(128)}, u32[]{:S(2)}) copy-start(f32[16]{0:T(128)} %param.21) | copy-start | bytes 196
  9.5 11.8 %copy-start.19 = (f32[4,2,128]{2,1,0:T(2,128)S(1)}, f32[4,2,128]{2,1,0:T(2,128)}, u32[]{:S(2)}) copy-start(f32[4,2,128]{2,1,0:T(2,128)} %param.24) | copy-start | bytes 12292
  9.5 11.8 %copy-start.20 = (f32[2,128]{1,0:T(2,128)S(1)}, f32[2,128]{1,0:T(2,128)}, u32[]{:S(2)}) copy-start(f32[2,128]{1,0:T(2,128)} %param.25) | copy-start | bytes 3076
  9.5 36.2 %all-to-all-start = ((bf16[32,32,896]{2,1,0:T(8,128)(2,1)}), bf16[32,32,896]{2,1,0:T(8,128)(2,1)S(1)}, u32[]{:S(2)}, u32[]{:S(2)}) async-start(bf16[32,32,896]{2,1,0:T(8,128)(2,1)} %shard_map.136), calls=%async_computation | async-start | bytes 3670016 | tf_op jit(solution)/shard_map/all_to_all | solution.py:345
  20.2 87.9 %all-gather.2.cloned.1.call-start = ((), (), s32[]{:S(2)}) async-start(), calls=%async_computation.6 | async-start | bytes 2228224 | tf_op jit(solution)/shard_map/all_gather | solution.py:365
  22.7 29.2 %copy-start.13 = (f32[16,128]{1,0:T(8,128)}, f32[16,128]{1,0:T(8,128)S(1)}, u32[]{:S(2)}) copy-start(f32[16,128]{1,0:T(8,128)S(1)} %pad_bitcast_fusion.group_taps_ref) | copy-start | bytes 24580
  45.8 2.3 %collective-permute-start = (bf16[8,512]{1,0:T(8,128)(2,1)S(1)}, bf16[8,512]{1,0:T(8,128)(2,1)S(1)}, u32[]{:S(2)}, u32[]{:S(2)}) collective-permute-start(bf16[8,512]{1,0:T(8,128)(2,1)S(1)} %shard_map.137), channel_id=1, source_target_pairs={{0,32},{32,64},{64,96},{96,128},{128,160},{160,192},{192,224},{224... | collective-permute-start | bytes 24584 | tf_op jit(solution)/shard_map/ppermute | solution.py:341
  48.0 42.0 %copy-start.11 = (f32[8,1024]{1,0:T(8,128)}, f32[8,1024]{1,0:T(8,128)S(1)}, u32[]{:S(2)}) copy-start(f32[8,1024]{1,0:T(8,128)S(1)} %get-tuple-element.27.cum_ref) | copy-start | bytes 98308
  48.1 41.9 %copy-start.15 = (bf16[8,512]{1,0:T(8,128)(2,1)}, bf16[8,512]{1,0:T(8,128)(2,1)S(1)}, u32[]{:S(2)}) copy-start(bf16[8,512]{1,0:T(8,128)(2,1)S(1)} %collective-permute-done.halo_ref) | copy-start | bytes 24580
  52.0 0.8 copy-start.5
  52.8 0.7 copy-start.7
  90.0 10.9 %all-to-all-start.3 = ((bf16[4,64,128]{2,1,0:T(8,128)(2,1)}), bf16[4,64,128]{2,1,0:T(8,128)(2,1)S(1)}, u32[]{:S(2)}, u32[]{:S(2)}) async-start(bf16[4,64,128]{2,1,0:T(8,128)(2,1)} %shard_map.141), calls=%async_computation.3 | async-start | bytes 131072 | tf_op jit(solution)/shard_map/all_to_all | solution.py:345
  93.3 1.0 copy-start.6
  94.4 0.9 copy-start.8
  95.3 0.8 copy-start.12
  96.1 0.7 copy-start.14
  96.8 0.7 copy-start.16
  97.5 0.7 copy-start.18
  100.2 0.7 copy-start.9
  101.0 1.0 copy-start.10
  103.0 1.3 copy-start.3
  104.3 3.8 %copy-start.17 = (f32[1024]{0:T(1024)S(1)}, f32[1024]{0:T(1024)}, u32[]{:S(2)}) copy-start(f32[1024]{0:T(1024)} %param.26) | copy-start | bytes 12292
  104.3 25.7 %all-to-all-start.4 = ((bf16[4,1024,256]{2,1,0:T(8,128)(2,1)}), bf16[4,1024,256]{2,1,0:T(8,128)(2,1)S(1)}, u32[]{:S(2)}, u32[]{:S(2)}) async-start(bf16[4,1024,256]{2,1,0:T(8,128)(2,1)} %copy-done.3), calls=%async_computation.4 | async-start | bytes 4194304 | tf_op jit(solution)/shard_map/all_to_all | solution.py:345
  108.1 1.6 copy-start.4
  110.0 1.4 copy-start.1
  130.0 1.6 copy-start.2
  132.9 9.5 %collective-permute-start.1 = (bf16[512,1024]{1,0:T(8,128)(2,1)S(1)}, bf16[512,1024]{1,0:T(8,128)(2,1)S(1)}, u32[]{:S(2)}, u32[]{:S(2)}) collective-permute-start(bf16[512,1024]{1,0:T(8,128)(2,1)S(1)} %shard_map.145), channel_id=1, source_target_pairs={{0,1},{1,0},{2,3},{3,2},{4,5},{5,4},{6,7},{7,6},{8,9},{9,8},{10,11... | collective-permute-start | bytes 3145736 | tf_op jit(solution)/shard_map/ppermute | solution.py:341
Sparse Core Ops, SparseCore 0:
  23.0 66.8 all-gather.1

commit v4 on v3

--- a/solution.py
+++ b/solution.py
@@ -13,10 +13,11 @@
 F32 = jnp.float32
 BF16 = jnp.bfloat16
 Z = ("zh", "zl")
-SEQ = ("zh", "zl", "x")
+X = ("xh", "xl")
+SEQ = ("zh", "zl", "xh", "xl")
 HEAD = ("y", "c")
-PLANE = ("x", "y", "c")
-ALL = ("zh", "zl", "x", "y", "c")
+PLANE = ("xh", "xl", "y", "c")
+ALL = ("zh", "zl", "xh", "xl", "y", "c")
 VMEM = pl.BlockSpec(memory_space=pltpu.VMEM)
 HBM = pl.BlockSpec(memory_space=pltpu.HBM)
 
@@ -97,8 +98,10 @@
         store.wait()
 
 
-def steps(packed_ref, heads_ref, dt_ref, cum_ref, sum_ref):
+def steps(packed_ref, heads_ref, dt_ref, cum_ref, sum_ref, late_ref):
     rows, tokens = dt_ref.shape
+    width = late_ref.shape[1]
+    late_ref[...] = packed_ref[:, packed_ref.shape[1] - LANES - width : packed_ref.shape[1] - LANES]
     before = lax.broadcasted_iota(jnp.int32, (SPAN, SPAN), 0)
     after = lax.broadcasted_iota(jnp.int32, (SPAN, SPAN), 1)
     ones = (before <= after).astype(F32)
@@ -211,12 +214,12 @@
 
 
 def local(
-    xs_ref, b_ref, packed_ref, halo_ref, group_taps_ref, dt_ref, cum_ref, held_ref, skip_ref,
+    xs_ref, b_ref, late_ref, halo_ref, group_taps_ref, dt_ref, cum_ref, held_ref, skip_ref,
     c_ref, y_ref, padded,
 ):
     tokens, cols = xs_ref.shape
     padded[:8] = halo_ref[:, cols + LANES : cols + 2 * LANES].astype(F32)
-    padded[8:] = packed_ref[:, cols + LANES : cols + 2 * LANES].astype(F32)
+    padded[8:] = late_ref[:, :LANES].astype(F32)
     rows = lax.broadcasted_iota(jnp.int32, (SPAN, SPAN), 0)
     lanes = lax.broadcasted_iota(jnp.int32, (SPAN, SPAN), 1)
     causal = rows >= lanes
@@ -248,10 +251,10 @@
             y_ref[part, lo : lo + LANES] = y
 
 
-def finish(start_ref, c_ref, sum_ref, y_ref, packed_ref, out_ref):
+def finish(start_ref, c_ref, sum_ref, y_ref, late_ref, out_ref, *, ys):
     tokens, cols = y_ref.shape
-    copies = out_ref.shape[0]
     rows = tokens // 32
+    half = out_ref.shape[1] // 2
     left = left_half()
     first = lax.axis_index("c") == 0
     for k in range(tokens // SPAN):
@@ -260,52 +263,60 @@
         for chunk in range(cols // LANES):
             lo = chunk * LANES
             carry = nt(c_ref[part], start_ref[lo : lo + LANES]) * by_head(grown, chunk, left)
-            at = cols + 2 * LANES + lo
-            z = packed_ref[part, at : at + LANES].astype(F32)
+            z = late_ref[part, LANES + lo : 2 * LANES + lo].astype(F32)
             gated = ((y_ref[part, lo : lo + LANES] + carry) * silu(z)).astype(BF16)
             for i in range(SPAN // (2 * rows)):
                 even = gated[2 * i * rows : (2 * i + 1) * rows]
                 odd = gated[(2 * i + 1) * rows : (2 * i + 2) * rows]
                 theirs = jnp.where(first, odd, even)
                 ours = jnp.where(first, even, odd)
-                at = k * (SPAN // 2) + i * rows
-                for d in range(copies):
+                x, y = divmod(k * (SPAN // (2 * rows)) + i, ys)
+                at = (x // 2 * ys + y) * rows
+                for d in range(x % 2, out_ref.shape[0], 2):
                     out_ref[d, at : at + rows, lo : lo + LANES] = theirs
-                    out_ref[d, tokens // 2 + at : tokens // 2 + at + rows, lo : lo + LANES] = ours
-
-
-def multiply(gated_ref, first, weights_ref, out_ref, other_ref):
+                    out_ref[d, half + at : half + at + rows, lo : lo + LANES] = ours
+
+
+def rescale(weights_ref, gain_ref, out_ref):
+    for lo in range(0, out_ref.shape[0], SPAN):
+        part = slice(lo, lo + SPAN)
+        out_ref[part] = (weights_ref[part].astype(F32) * gain_ref[...]).astype(BF16)
+
+
+def multiply(first, gated_ref, weights_far, out_ref, weights_ref, sems):
     parts, _, cols = gated_ref.shape
     rows, width = out_ref.shape
+    step = width // sems.shape[0]
+    loads = []
+    for j in range(sems.shape[0]):
+        span = pl.ds(j * step, step)
+        loads.append(pltpu.make_async_copy(weights_far.at[span], weights_ref.at[span], sems.at[j]))
+        loads[-1].start()
     squares = jnp.zeros((rows, 1), F32)
     for i in range(parts):
         value = gated_ref[i, first : first + rows].astype(F32)
         squares = squares + jnp.sum(value * value, axis=1, keepdims=True)
     scale = 1.0 / jnp.sqrt(squares / weights_ref.shape[1] + 1.0)
-    step = 2 * LANES
-    for lo in range(0, width, step):
+    for j, load in enumerate(loads):
+        lo = j * step
+        load.wait()
         total = jnp.zeros((rows, step), F32)
         for i in range(parts):
             weights = weights_ref[lo : lo + step, i * cols : (i + 1) * cols]
             total = total + nt(gated_ref[i, first : first + rows], weights)
-        total = total * scale
-        if other_ref is not None:
-            total = total + other_ref[:, lo : lo + step].astype(F32)
-        out_ref[:, lo : lo + step] = total.astype(BF16)
-
-
-def rescale(weights_ref, gain_ref, out_ref):
-    for lo in range(0, out_ref.shape[0], SPAN):
-        part = slice(lo, lo + SPAN)
-        out_ref[part] = (weights_ref[part].astype(F32) * gain_ref[...]).astype(BF16)
-
-
-def project(gated_ref, weights_ref, out_ref):
-    multiply(gated_ref, 0, weights_ref, out_ref, None)
-
-
-def project_add(gated_ref, weights_ref, other_ref, out_ref):
-    multiply(gated_ref, out_ref.shape[0], weights_ref, out_ref, other_ref)
+        out_ref[:, lo : lo + step] = (total * scale).astype(BF16)
+
+
+def project_theirs(*refs):
+    multiply(0, *refs)
+
+
+def project_ours(gated_ref, weights_far, out_ref, *refs):
+    multiply(out_ref.shape[0], gated_ref, weights_far, out_ref, *refs)
+
+
+def add(ours_ref, other_ref, out_ref):
+    out_ref[...] = (ours_ref[...].astype(F32) + other_ref[...].astype(F32)).astype(BF16)
 
 
 def tail(array_ref, out_ref):
@@ -314,25 +325,14 @@
 
 def collect(shares_ref, out_ref, *, ys):
     count, _, width = shares_ref.shape
-    xs = count // ys
-    left = left_half()
-    for pair in range(width // LANES):
-        lo = pair * LANES
-        sums = []
-        for i in range(xs):
-            total = shares_ref[i * ys, :, lo : lo + LANES].astype(F32)
+    halves = count // ys
+    for k in range(width // LANES):
+        for i in range(halves):
+            total = shares_ref[i * ys, :, k * LANES : (k + 1) * LANES].astype(F32)
             for j in range(1, ys):
-                total = total + shares_ref[i * ys + j, :, lo : lo + LANES].astype(F32)
-            sums.append(total)
-        rolled = [pltpu.roll(total, HEAD_DIM, 1) for total in sums]
-        for side in range(2):
-            for i in range(0, xs, 2):
-                if side == 0:
-                    value = jnp.where(left, sums[i], rolled[i + 1])
-                else:
-                    value = jnp.where(left, rolled[i], sums[i + 1])
-                at = (2 * pair + side) * (xs * HEAD_DIM) + i * HEAD_DIM
-                out_ref[:, at : at + LANES] = value.astype(BF16)
+                total = total + shares_ref[i * ys + j, :, k * LANES : (k + 1) * LANES].astype(F32)
+            at = (k * halves + i) * LANES
+            out_ref[:, at : at + LANES] = total.astype(BF16)
 
 
 def shift(array, axis, by, wrap=True):
@@ -349,20 +349,25 @@
     x_proj, z_proj, b_proj, c_proj, dt_raw, dt_bias, a_log, d_skip,
     conv_x, conv_bias_x, conv_bc, conv_bias_bc, norm_weight, out_weight,
 ):
-    xs, ys, cs = (lax.axis_size(a) for a in PLANE)
+    xh, xl, ys, cs = (lax.axis_size(a) for a in PLANE)
+    xs = xh * xl
     zh, zl = (lax.axis_size(a) for a in Z)
     plane = xs * ys * cs
     rows, inner = x_proj.shape
     cols = inner // plane
     tokens = rows * plane
-    part = lax.axis_index("x")
+    part = lax.axis_index("xh") * xl + lax.axis_index("xl")
     heads = dt_bias.shape[0] // xs
 
     def own(values, axis):
         size = values.shape[axis] // xs
         return lax.dynamic_slice_in_dim(values, part * size, size, axis)
 
-    weights = lax.all_gather(out_weight.T, Z, axis=0, tiled=True)
+    mine = out_weight.T
+    other = shift(mine, "xl", 1)
+    even = lax.axis_index("xl") == 0
+    pair = jnp.concatenate([jnp.where(even, mine, other), jnp.where(even, other, mine)])
+    weights = lax.all_gather(pair, Z, axis=0, tiled=True)
     out = call(
         pack,
         shape((plane, rows, 2 * cols + 3 * LANES), BF16),
@@ -392,7 +397,8 @@
     halo = call(tail, shape((8, cols + 2 * LANES), BF16), (packed,), (), 1 << 16, 4)
     halo = shift(halo, Z, 1, wrap=False)
     by_token = shape((8, tokens), F32)
-    dt, cum, sums = call(steps, (by_token, by_token, by_token), (packed, per_head))
+    late = shape((tokens, cols + LANES), BF16)
+    dt, cum, sums, late = call(steps, (by_token, by_token, by_token, late), (packed, per_head))
     x_conv, b_conv, held, states_out = call(
         scan_in,
         (
@@ -412,35 +418,44 @@
         (shape(near, F32), shape((8 * zl, LANES), F32), shape((zh, cols // zl + 8, STATE), BF16)),
         (near_in,),
     )
-    far_in = sent(far_out, "zh")
-    starts = call(scan_far, shape(near, BF16), (far_in, inner, before))
-    start = sent(starts, "zl").reshape(cols, STATE)
     c_conv, y = call(
         local,
         (shape((tokens, LANES), BF16), shape((tokens, cols), F32)),
-        (x_conv, b_conv, packed, halo, group_taps, dt, cum, held, skip),
+        (x_conv, b_conv, late, halo, group_taps, dt, cum, held, skip),
         [pltpu.VMEM((tokens + 8, LANES), F32)],
         1 << 27,
     )
+    far_in, c_conv, y = lax.optimization_barrier((sent(far_out, "zh"), c_conv, y))
+    starts = call(scan_far, shape(near, BF16), (far_in, inner, before))
+    start = sent(starts, "zl").reshape(cols, STATE)
+
+    def finish_all(*refs):
+        finish(*refs, ys=ys)
+
+    def collect_all(*refs):
+        collect(*refs, ys=ys)
+
     copies = call(
-        finish, shape((xs, tokens, cols), BF16), (start, c_conv, sums, y, packed), (), 1 << 25
-    )
-    gated = sent(copies, "x")
-    weights = call(rescale, shape(weights.shape, BF16), (weights, norm_weight[None]))
-    product = shape((tokens // 2, weights.shape[0]), BF16)
-    away = call(project, product, (gated, weights), (), 1 << 29, 24)
-    other = shift(away, "c", 1)
-    both = call(project_add, product, (gated, weights, other), (), 1 << 29, 24)
-    shares = sent(both.reshape(xs * ys, rows, weights.shape[0]), ("x", "y"))
-
-    def collect_all(shares_ref, out_ref):
-        collect(shares_ref, out_ref, ys=ys)
-
-    return call(collect_all, shape((rows, xs * weights.shape[0]), BF16), (shares,))
+        finish_all,
+        shape((xs, tokens // xl, cols), BF16),
+        (start, c_conv, sums, y, late),
+        (),
+        1 << 25,
+    )
+    gated = sent(copies, X)
+    weights = call(rescale, shape(weights.shape, BF16), (weights, norm_weight[None]), (), 1 << 22, 60)
+    count = tokens // (2 * xl)
+    product = shape((count, weights.shape[0]), BF16)
+    room = [pltpu.VMEM(weights.shape, BF16), pltpu.SemaphoreType.DMA((8,))]
+    theirs = call(project_theirs, product, (gated, weights), room, 1 << 30, 50, (1,))
+    ours = call(project_ours, product, (gated, weights), room, 1 << 30, 50, (1,))
+    both = call(add, product, (ours, shift(theirs, "c", 1)))
+    shares = sent(both.reshape(xh * ys, rows, weights.shape[0]), ("xh", "y"))
+    return call(collect_all, shape((rows, xh * weights.shape[0]), BF16), (shares,))
 
 
 def solution(mesh):
-    split = Mesh(mesh.devices.reshape(4, 4, 4, 4, 2), ALL)
+    split = Mesh(mesh.devices.reshape(4, 4, 2, 2, 4, 2), ALL)
     return jax.shard_map(
         per_device,
         mesh=split,

time: 172 us -> 167 us (0.971)
  blocking collectives: 54.6 us -> 37.6 us
  starting transfers between devices: 26.4 us -> 41.8 us
  Pallas kernels: 15.2 us -> 27.9 us
  local copies, waits for them, and re-layouts: 15.5 us -> 2.99 us
  waiting for transfers between devices: 44.7 us -> 41.1 us
    all_to_all x3, blocking collectives: 54.6 us -> 37.6 us  [sent(): return lax.all_to_all(array, axes, 0, 0, tiled=True)]
    pallas_call x12 -> x13, Pallas kernels: 15.2 us -> 27.9 us  [call(): pl.pallas_call(kernel, out_shape=outs, in_specs=[HBM if i in far else VME...]
    unnamed x49 -> x17, local copies, waits for them, and re-layouts: 13.8 us -> 1.87 us
    all_to_all x3, starting transfers between devices: 17.6 us -> 27 us  [sent(): return lax.all_to_all(array, axes, 0, 0, tiled=True)]
    ppermute x2 -> x3, starting transfers between devices: 8.72 us -> 14.8 us  [shift(): return lax.ppermute(array, axis, pairs)]
    all_to_all x3, waiting for transfers between devices: 41.7 us -> 38.4 us  [sent(): return lax.all_to_all(array, axes, 0, 0, tiled=True)]
  transfers between devices with their start and end apart: 6 -> 7, of which waited for: 4 -> 5; matrix products, arithmetic and copies ran while one was open for 1% -> 1% of each run, Pallas kernels for 5% -> 13%
where the time goes in v4:
time: 167 us
  starting transfers between devices  41.8 us (25%)
  waiting for transfers between devices  41.1 us (25%)
  blocking collectives  37.6 us (23%)
  Pallas kernels  27.9 us (17%)
  between operations  13.6 us (8%)
  local copies, waits for them, and re-layouts  2.99 us (2%)
  other arithmetic  1.74 us (1%)
    all_to_all x3, waiting for transfers between devices, sent(): return lax.all_to_all(array, axes, 0, 0, tiled=True)  38.4 us
    all_to_all x3, blocking collectives, sent(): return lax.all_to_all(array, axes, 0, 0, tiled=True)  37.6 us
    pallas_call x13, Pallas kernels, call(): pl.pallas_call(kernel, out_shape=outs, in_specs=[HBM if i in far else VME...  27.9 us
    all_to_all x3, starting transfers between devices, sent(): return lax.all_to_all(array, axes, 0, 0, tiled=True)  27 us
    ppermute x3, starting transfers between devices, shift(): return lax.ppermute(array, axis, pairs)  14.8 us
  transfers between devices with their start and end apart: 7, of which 5 were waited for; matrix products, arithmetic and copies ran while one was open for 1% of the time, Pallas kernels for 13%

profile of v4, /device:TPU:1, one launch (start us, length us, event | category | flops | bytes accessed | tf_op | source)
XLA Modules:
  0.0 166.7 jit_solution(6465459796940692877)
XLA Ops:
  6.6 4.1 %collective-permute-start.1 = (bf16[64,1024]{1,0:T(8,128)(2,1)}, bf16[64,1024]{1,0:T(8,128)(2,1)S(1)}, u32[]{:S(2)}, u32[]{:S(2)}) collective-permute-start(bf16[64,1024]{1,0:T(8,128)(2,1)} %bitcast.23), channel_id=1, source_target_pairs={{0,8},{8,0},{1,9},{9,1},{2,10},{10,2},{3,11},{11,3},{4,12},{12,4},... | collective-permute-start | bytes 393224 | tf_op jit(solution)/shard_map/ppermute | solution.py:341
  10.7 2.5 %collective-permute-done.1 = bf16[64,1024]{1,0:T(8,128)(2,1)S(1)} collective-permute-done((bf16[64,1024]{1,0:T(8,128)(2,1)}, bf16[64,1024]{1,0:T(8,128)(2,1)S(1)}, u32[]{:S(2)}, u32[]{:S(2)}) %collective-permute-start.1) | collective-permute-done | bytes 131104 | tf_op jit(solution)/shard_map/ppermute | solution.py:341
  13.2 0.9 broadcast_select_fusion.1
  14.2 0.7 pad_maximum_fusion
  14.9 2.9 %shard_map.136 = bf16[32,32,896]{2,1,0:T(8,128)(2,1)} custom-call(bf16[32,8192]{1,0:T(8,128)(2,1)} %x_far.1, bf16[32,8192]{1,0:T(8,128)(2,1)} %z_far.1, bf16[32,1024]{1,0:T(8,128)(2,1)} %b_far.1, bf16[32,1024]{1,0:T(8,128)(2,1)} %c_far.1, bf16[32,128]{1,0:T(8,128)(2,1)} %dt_far.1), custom_call_target="tpu_custom_call" | custom-call | flops 4194304 | bytes 1048576 | tf_op jit(solution)/shard_map/pallas_call | solution.py:26
  17.9 11.1 %all-to-all-start = ((bf16[32,32,896]{2,1,0:T(8,128)(2,1)}), bf16[32,32,896]{2,1,0:T(8,128)(2,1)S(1)}, u32[]{:S(2)}, u32[]{:S(2)}) async-start(bf16[32,32,896]{2,1,0:T(8,128)(2,1)} %shard_map.136), calls=%async_computation | async-start | bytes 3670016 | tf_op jit(solution)/shard_map/all_to_all | solution.py:345
  29.1 0.1 copy.16
  29.2 0.1 copy.15
  29.3 0.8 dynamic_slice.19
  30.2 24.3 %all-to-all-done = bf16[32,32,896]{2,1,0:T(8,128)(2,1)S(1)} async-done(((bf16[32,32,896]{2,1,0:T(8,128)(2,1)}), bf16[32,32,896]{2,1,0:T(8,128)(2,1)S(1)}, u32[]{:S(2)}, u32[]{:S(2)}) %all-to-all-start) | async-done | bytes 1835040 | tf_op jit(solution)/shard_map/all_to_all | solution.py:345
  54.5 1.8 %collective-permute-start = (bf16[8,512]{1,0:T(8,128)(2,1)S(1)}, bf16[8,512]{1,0:T(8,128)(2,1)S(1)}, u32[]{:S(2)}, u32[]{:S(2)}) collective-permute-start(bf16[8,512]{1,0:T(8,128)(2,1)S(1)} %shard_map.137), channel_id=1, source_target_pairs={{0,32},{32,64},{64,96},{96,128},{128,160},{160,192},{192,224},{224... | collective-permute-start | bytes 24584 | tf_op jit(solution)/shard_map/ppermute | solution.py:341
  56.4 0.7 shard_map.138
  57.0 0.1 collective-permute-done.halo_ref
  57.1 3.9 %shard_map.139 = (bf16[1024,256]{1,0:T(8,128)(2,1)S(1)}, bf16[1024,128]{1,0:T(8,128)(2,1)S(1)}, bf16[8,256,128]{2,1,0:T(8,128)(2,1)S(1)}, bf16[4,72,128]{2,1,0:T(8,128)(2,1)S(1)}) custom-call(bf16[1024,896]{1,0:T(8,128)(2,1)S(1)} %bitcast.20, bf16[8,512]{1,0:T(8,128)(2,1)S(1)} %collective-permute-done.halo_ref, f32[8,256]{1,0:T(8,128)S(1)} %select_maximum_fusion.taps_ref, ...), custom_call_target="tpu_custom_call" | custom-call | flops 33554432 | bytes 1048576 | tf_op jit(solution)/shard_map/pallas_call | solution.py:26
  61.0 0.8 copy-done.1
  61.8 11.6 %all_to_all.30.inbox_ref = bf16[4,72,128]{2,1,0:T(8,128)(2,1)S(1)} all-to-all(bf16[4,72,128]{2,1,0:T(8,128)(2,1)S(1)} %get-tuple-element.33), channel_id=1, replica_groups=mesh['zh'=4,'zl'=4,'xh'=2,'xl'=2,'y'=4,'c'=2] {'zl'}, dimensions={0} | all-to-all | bytes 147456 | tf_op jit(solution)/shard_map/all_to_all | solution.py:345
  73.4 0.7 shard_map.140
  74.1 12.4 %all-to-all-start.2 = ((bf16[4,72,128]{2,1,0:T(8,128)(2,1)}), bf16[4,72,128]{2,1,0:T(8,128)(2,1)S(1)}, u32[]{:S(2)}, u32[]{:S(2)}) async-start(bf16[4,72,128]{2,1,0:T(8,128)(2,1)} %get-tuple-element.34), calls=%async_computation.2 | async-start | bytes 147456 | tf_op jit(solution)/shard_map/all_to_all | solution.py:345
  86.5 1.0 copy-done.2
  87.6 2.1 %shard_map.141 = (bf16[1024,128]{1,0:T(8,128)(2,1)S(1)}, f32[1024,256]{1,0:T(8,128)S(1)}) custom-call(bf16[1024,256]{1,0:T(8,128)(2,1)S(1)} %get-tuple-element.35.xs_ref, bf16[1024,128]{1,0:T(8,128)(2,1)S(1)} %get-tuple-element.36.b_ref, bf16[1024,384]{1,0:T(8,128)(2,1)S(1)} %get-tuple-element.37.late_ref.refs_4_, ...), custom_call_target="tpu_custom_call" | custom-call | flops 134217728 | bytes 1048576 | tf_op jit(solution)/shard_map/pallas_call | solution.py:26
  89.7 9.3 %all-to-all-done.2.inbox_ref = bf16[4,72,128]{2,1,0:T(8,128)(2,1)S(1)} async-done(((bf16[4,72,128]{2,1,0:T(8,128)(2,1)}), bf16[4,72,128]{2,1,0:T(8,128)(2,1)S(1)}, u32[]{:S(2)}, u32[]{:S(2)}) %all-to-all-start.2) | async-done | bytes 73760 | tf_op jit(solution)/shard_map/all_to_all | solution.py:345
  99.0 7.0 %all_to_all.31 = bf16[4,64,128]{2,1,0:T(8,128)(2,1)S(1)} all-to-all(bf16[4,64,128]{2,1,0:T(8,128)(2,1)S(1)} %shard_map.142), channel_id=1, replica_groups=mesh['zh'=4,'zl'=4,'xh'=2,'xl'=2,'y'=4,'c'=2] {'zl'}, dimensions={0} | all-to-all | bytes 131072 | tf_op jit(solution)/shard_map/all_to_all | solution.py:345
  106.0 2.1 %shard_map.143 = bf16[4,512,256]{2,1,0:T(8,128)(2,1)} custom-call(bf16[256,128]{1,0:T(8,128)(2,1)S(1)} %bitcast.22, bf16[1024,128]{1,0:T(8,128)(2,1)S(1)} %get-tuple-element.45.refs_1_, f32[8,1024]{1,0:T(8,128)S(1)} %get-tuple-element.32.sum_ref.refs_2_, f32[1024,256]{1,0:T(8,128)S(1)} %get-tuple-element.46.refs_3_, ...), custom_call_target="tpu_custom_call" | custom-call | flops 33554432 | bytes 1048576 | tf_op jit(solution)/shard_map/pallas_call | solution.py:26
  108.0 3.5 %all-to-all-start.4 = ((bf16[4,512,256]{2,1,0:T(8,128)(2,1)}), bf16[4,512,256]{2,1,0:T(8,128)(2,1)S(1)}, u32[]{:S(2)}, u32[]{:S(2)}) async-start(bf16[4,512,256]{2,1,0:T(8,128)(2,1)} %shard_map.143), calls=%async_computation.4 | async-start | bytes 2097152 | tf_op jit(solution)/shard_map/all_to_all | solution.py:345
  111.6 4.9 %shard_map.144.weights_far.refs_1_ = bf16[2048,1024]{1,0:T(8,128)(2,1)} custom-call(bf16[2048,1024]{1,0:T(8,128)(2,1)} %all-gather.2.cloned.1.call-done.weights_ref, f32[1,1024]{1,0:T(1,128)} %bitcast.24), custom_call_target="tpu_custom_call" | custom-call | flops 4194304 | bytes 1048576 | tf_op jit(solution)/shard_map/pallas_call | solution.py:26
  116.5 4.8 %all-to-all-done.4.gated_ref.refs_0_ = bf16[4,512,256]{2,1,0:T(8,128)(2,1)S(1)} async-done(((bf16[4,512,256]{2,1,0:T(8,128)(2,1)}), bf16[4,512,256]{2,1,0:T(8,128)(2,1)S(1)}, u32[]{:S(2)}, u32[]{:S(2)}) %all-to-all-start.4) | async-done | bytes 1048608 | tf_op jit(solution)/shard_map/all_to_all | solution.py:345
  121.3 4.8 %shard_map.146 = bf16[256,2048]{1,0:T(8,128)(2,1)S(1)} custom-call(bf16[4,512,256]{2,1,0:T(8,128)(2,1)S(1)} %all-to-all-done.4.gated_ref.refs_0_, bf16[2048,1024]{1,0:T(8,128)(2,1)} %shard_map.144.weights_far.refs_1_), custom_call_target="tpu_custom_call" | custom-call | flops 1073741824 | bytes 1048576 | tf_op jit(solution)/shard_map/pallas_call | solution.py:26
  126.0 8.9 %collective-permute-start.2 = (bf16[256,2048]{1,0:T(8,128)(2,1)S(1)}, bf16[256,2048]{1,0:T(8,128)(2,1)S(1)}, u32[]{:S(2)}, u32[]{:S(2)}) collective-permute-start(bf16[256,2048]{1,0:T(8,128)(2,1)S(1)} %shard_map.146), channel_id=1, source_target_pairs={{0,1},{1,0},{2,3},{3,2},{4,5},{5,4},{6,7},{7,6},{8,9},{9,8},{10,11... | collective-permute-start | bytes 3145736 | tf_op jit(solution)/shard_map/ppermute | solution.py:341
  135.0 4.8 %shard_map.145.ours_ref = bf16[256,2048]{1,0:T(8,128)(2,1)S(1)} custom-call(bf16[4,512,256]{2,1,0:T(8,128)(2,1)S(1)} %all-to-all-done.4.gated_ref.refs_0_, bf16[2048,1024]{1,0:T(8,128)(2,1)} %shard_map.144.weights_far.refs_1_), custom_call_target="tpu_custom_call" | custom-call | flops 1073741824 | bytes 1048576 | tf_op jit(solution)/shard_map/pallas_call | solution.py:26
  139.7 0.2 shard_map.147
  140.0 19.0 %all_to_all.32.refs_0_ = bf16[8,32,2048]{2,1,0:T(8,128)(2,1)S(1)} all-to-all(bf16[8,32,2048]{2,1,0:T(8,128)(2,1)S(1)} %bitcast.21), channel_id=1, replica_groups=mesh['zh'=4,'zl'=4,'xh'=2,'xl'=2,'y'=4,'c'=2] {'xh','y'}, dimensions={0} | all-to-all | bytes 2097152 | tf_op jit(solution)/shard_map/all_to_all | solution.py:345
  159.0 0.8 shard_map.148
  (30 shorter events, 0.4 us)
Async XLA Ops:
  6.5 23.6 %copy-start = (f32[4,1024]{1,0:T(4,128)S(1)}, f32[4,1024]{1,0:T(4,128)}, u32[]{:S(2)}) copy-start(f32[4,1024]{1,0:T(4,128)} %param.22) | copy-start | bytes 49156
  6.5 22.4 %copy-start.6 = (f32[16]{0:T(128)S(1)}, f32[16]{0:T(128)}, u32[]{:S(2)}) copy-start(f32[16]{0:T(128)} %param.21) | copy-start | bytes 196
  6.5 22.5 %copy-start.7 = (f32[16]{0:T(128)S(1)}, f32[16]{0:T(128)}, u32[]{:S(2)}) copy-start(f32[16]{0:T(128)} %param.20) | copy-start | bytes 196
  6.5 22.5 %copy-start.5 = (f32[16]{0:T(128)S(1)}, f32[16]{0:T(128)}, u32[]{:S(2)}) copy-start(f32[16]{0:T(128)} %param.19) | copy-start | bytes 196
  6.5 22.8 %copy-start.4 = (f32[2,128]{1,0:T(2,128)S(1)}, f32[2,128]{1,0:T(2,128)}, u32[]{:S(2)}) copy-start(f32[2,128]{1,0:T(2,128)} %param.25) | copy-start | bytes 3076
  6.5 22.8 %copy-start.3 = (f32[4,2,128]{2,1,0:T(2,128)S(1)}, f32[4,2,128]{2,1,0:T(2,128)}, u32[]{:S(2)}) copy-start(f32[4,2,128]{2,1,0:T(2,128)} %param.24) | copy-start | bytes 12292
  6.6 105.0 %all-gather.2.cloned.1.call-start = ((), (), s32[]{:S(2)}) async-start(), calls=%async_computation.6 | async-start | bytes 4456448 | tf_op jit(solution)/shard_map/all_gather | solution.py:370
  6.6 6.6 %collective-permute-start.1 = (bf16[64,1024]{1,0:T(8,128)(2,1)}, bf16[64,1024]{1,0:T(8,128)(2,1)S(1)}, u32[]{:S(2)}, u32[]{:S(2)}) collective-permute-start(bf16[64,1024]{1,0:T(8,128)(2,1)} %bitcast.23), channel_id=1, source_target_pairs={{0,8},{8,0},{1,9},{9,1},{2,10},{10,2},{3,11},{11,3},{4,12},{12,4},... | collective-permute-start | bytes 393224 | tf_op jit(solution)/shard_map/ppermute | solution.py:341
  17.9 36.7 %all-to-all-start = ((bf16[32,32,896]{2,1,0:T(8,128)(2,1)}), bf16[32,32,896]{2,1,0:T(8,128)(2,1)S(1)}, u32[]{:S(2)}, u32[]{:S(2)}) async-start(bf16[32,32,896]{2,1,0:T(8,128)(2,1)} %shard_map.136), calls=%async_computation | async-start | bytes 3670016 | tf_op jit(solution)/shard_map/all_to_all | solution.py:345
  54.5 2.6 %collective-permute-start = (bf16[8,512]{1,0:T(8,128)(2,1)S(1)}, bf16[8,512]{1,0:T(8,128)(2,1)S(1)}, u32[]{:S(2)}, u32[]{:S(2)}) collective-permute-start(bf16[8,512]{1,0:T(8,128)(2,1)S(1)} %shard_map.137), channel_id=1, source_target_pairs={{0,32},{32,64},{64,96},{96,128},{128,160},{160,192},{192,224},{224... | collective-permute-start | bytes 24584 | tf_op jit(solution)/shard_map/ppermute | solution.py:341
  61.0 0.8 copy-start.1
  74.1 24.9 %all-to-all-start.2 = ((bf16[4,72,128]{2,1,0:T(8,128)(2,1)}), bf16[4,72,128]{2,1,0:T(8,128)(2,1)S(1)}, u32[]{:S(2)}, u32[]{:S(2)}) async-start(bf16[4,72,128]{2,1,0:T(8,128)(2,1)} %get-tuple-element.34), calls=%async_computation.2 | async-start | bytes 147456 | tf_op jit(solution)/shard_map/all_to_all | solution.py:345
  86.5 1.1 copy-start.2
  108.0 13.2 %all-to-all-start.4 = ((bf16[4,512,256]{2,1,0:T(8,128)(2,1)}), bf16[4,512,256]{2,1,0:T(8,128)(2,1)S(1)}, u32[]{:S(2)}, u32[]{:S(2)}) async-start(bf16[4,512,256]{2,1,0:T(8,128)(2,1)} %shard_map.143), calls=%async_computation.4 | async-start | bytes 2097152 | tf_op jit(solution)/shard_map/all_to_all | solution.py:345
  126.0 13.7 %collective-permute-start.2 = (bf16[256,2048]{1,0:T(8,128)(2,1)S(1)}, bf16[256,2048]{1,0:T(8,128)(2,1)S(1)}, u32[]{:S(2)}, u32[]{:S(2)}) collective-permute-start(bf16[256,2048]{1,0:T(8,128)(2,1)S(1)} %shard_map.146), channel_id=1, source_target_pairs={{0,1},{1,0},{2,3},{3,2},{4,5},{5,4},{6,7},{7,6},{8,9},{9,8},{10,11... | collective-permute-start | bytes 3145736 | tf_op jit(solution)/shard_map/ppermute | solution.py:341
Sparse Core Ops, SparseCore 0:
  15.0 76.1 all-gather.1

commit v5 on v4

--- a/solution.py
+++ b/solution.py
@@ -186,7 +186,7 @@
     return terms[0:1] + terms[1:2] + terms[2:3]
 
 
-def scan_near(inbox_ref, inner_ref, before_ref, sent_ref):
+def scan_near(inbox_ref, inner_ref, before_ref, group_ref, sent_ref):
     count, rows, _ = inner_ref.shape
     state = jnp.zeros((rows, STATE), F32)
     log = jnp.zeros((1, LANES), F32)
@@ -196,19 +196,22 @@
         mine = from_terms(inbox_ref[i, rows:])
         state = jnp.exp(mine) * state + inbox_ref[i, :rows].astype(F32)
         log = log + mine
-    for d in range(sent_ref.shape[0]):
-        sent_ref[d, :rows] = state.astype(BF16)
-        sent_ref[d, rows:] = in_terms(log)
-
-
-def scan_far(inbox_ref, inner_ref, before_ref, starts_ref):
-    count, rows, _ = inner_ref.shape
-    me = lax.axis_index("zh")
-    state = jnp.zeros((rows, STATE), F32)
-    for j in range(inbox_ref.shape[0]):
-        later = jnp.exp(from_terms(inbox_ref[j, rows:])) * state + inbox_ref[j, :rows].astype(F32)
-        state = jnp.where(j < me, later, state)
-    for i in range(count):
+    before_ref[8 * count :] = jnp.broadcast_to(log, (8, LANES))
+    group_ref[...] = state
+    sent_ref[...] = state.astype(BF16)
+
+
+def extend(inbox_ref, before_ref, group_ref, sent_ref):
+    grown = jnp.exp(before_ref[before_ref.shape[0] - 1 :])
+    sent_ref[...] = (grown * inbox_ref[...].astype(F32) + group_ref[...]).astype(BF16)
+
+
+def scan_far(inner_ref, before_ref, *refs):
+    starts_ref = refs[-1]
+    state = refs[0][...].astype(F32)
+    for ref in refs[1:-1]:
+        state = state + ref[...].astype(F32)
+    for i in range(inner_ref.shape[0]):
         grown = jnp.exp(before_ref[8 * i : 8 * i + 1])
         starts_ref[i] = (grown * state + inner_ref[i]).astype(BF16)
 
@@ -277,15 +280,9 @@
                     out_ref[d, half + at : half + at + rows, lo : lo + LANES] = ours
 
 
-def rescale(weights_ref, gain_ref, out_ref):
-    for lo in range(0, out_ref.shape[0], SPAN):
-        part = slice(lo, lo + SPAN)
-        out_ref[part] = (weights_ref[part].astype(F32) * gain_ref[...]).astype(BF16)
-
-
-def multiply(first, gated_ref, weights_far, out_ref, weights_ref, sems):
-    parts, _, cols = gated_ref.shape
-    rows, width = out_ref.shape
+def project(gated_ref, weights_far, theirs_ref, ours_ref, weights_ref, sems):
+    parts, rows, cols = gated_ref.shape
+    half, width = ours_ref.shape
     step = width // sems.shape[0]
     loads = []
     for j in range(sems.shape[0]):
@@ -294,7 +291,7 @@
         loads[-1].start()
     squares = jnp.zeros((rows, 1), F32)
     for i in range(parts):
-        value = gated_ref[i, first : first + rows].astype(F32)
+        value = gated_ref[i].astype(F32)
         squares = squares + jnp.sum(value * value, axis=1, keepdims=True)
     scale = 1.0 / jnp.sqrt(squares / weights_ref.shape[1] + 1.0)
     for j, load in enumerate(loads):
@@ -303,16 +300,10 @@
         total = jnp.zeros((rows, step), F32)
         for i in range(parts):
             weights = weights_ref[lo : lo + step, i * cols : (i + 1) * cols]
-            total = total + nt(gated_ref[i, first : first + rows], weights)
-        out_ref[:, lo : lo + step] = (total * scale).astype(BF16)
-
-
-def project_theirs(*refs):
-    multiply(0, *refs)
-
-
-def project_ours(gated_ref, weights_far, out_ref, *refs):
-    multiply(out_ref.shape[0], gated_ref, weights_far, out_ref, *refs)
+            total = total + nt(gated_ref[i], weights)
+        total = (total * scale).astype(BF16)
+        theirs_ref[:, lo : lo + step] = total[:half]
+        ours_ref[:, lo : lo + step] = total[half:]
 
 
 def add(ours_ref, other_ref, out_ref):
@@ -363,11 +354,8 @@
         size = values.shape[axis] // xs
         return lax.dynamic_slice_in_dim(values, part * size, size, axis)
 
-    mine = out_weight.T
-    other = shift(mine, "xl", 1)
-    even = lax.axis_index("xl") == 0
-    pair = jnp.concatenate([jnp.where(even, mine, other), jnp.where(even, other, mine)])
-    weights = lax.all_gather(pair, Z, axis=0, tiled=True)
+    scaled = (out_weight.T.astype(F32) * norm_weight[None]).astype(BF16)
+    weights = lax.all_gather(scaled, (*Z, "xl"), axis=0, tiled=True)
     out = call(
         pack,
         shape((plane, rows, 2 * cols + 3 * LANES), BF16),
@@ -411,13 +399,6 @@
         [pltpu.VMEM((tokens + 8, cols + LANES), F32)],
         1 << 25,
     )
-    near_in = sent(states_out, "zl")
-    near = zl, cols // zl, STATE
-    inner, before, far_out = call(
-        scan_near,
-        (shape(near, F32), shape((8 * zl, LANES), F32), shape((zh, cols // zl + 8, STATE), BF16)),
-        (near_in,),
-    )
     c_conv, y = call(
         local,
         (shape((tokens, LANES), BF16), shape((tokens, cols), F32)),
@@ -425,8 +406,24 @@
         [pltpu.VMEM((tokens + 8, LANES), F32)],
         1 << 27,
     )
-    far_in, c_conv, y = lax.optimization_barrier((sent(far_out, "zh"), c_conv, y))
-    starts = call(scan_far, shape(near, BF16), (far_in, inner, before))
+    near_in, c_conv, y = lax.optimization_barrier((sent(states_out, "zl"), c_conv, y))
+    near = zl, cols // zl, STATE
+    inner, before, group, ahead = call(
+        scan_near,
+        (
+            shape(near, F32),
+            shape((8 * zl + 8, LANES), F32),
+            shape(near[1:], F32),
+            shape(near[1:], BF16),
+        ),
+        (near_in,),
+    )
+    inboxes = []
+    for hop in range(zh - 1):
+        if hop:
+            ahead = call(extend, shape(near[1:], BF16), (inboxes[-1], before, group))
+        inboxes.append(lax.ppermute(ahead, "zh", [(hop, hop + 1)]))
+    starts = call(scan_far, shape(near, BF16), (inner, before, *inboxes))
     start = sent(starts, "zl").reshape(cols, STATE)
 
     def finish_all(*refs):
@@ -443,12 +440,10 @@
         1 << 25,
     )
     gated = sent(copies, X)
-    weights = call(rescale, shape(weights.shape, BF16), (weights, norm_weight[None]), (), 1 << 22, 60)
     count = tokens // (2 * xl)
     product = shape((count, weights.shape[0]), BF16)
     room = [pltpu.VMEM(weights.shape, BF16), pltpu.SemaphoreType.DMA((8,))]
-    theirs = call(project_theirs, product, (gated, weights), room, 1 << 30, 50, (1,))
-    ours = call(project_ours, product, (gated, weights), room, 1 << 30, 50, (1,))
+    theirs, ours = call(project, (product, product), (gated, weights), room, 1 << 30, 50, (1,))
     both = call(add, product, (ours, shift(theirs, "c", 1)))
     shares = sent(both.reshape(xh * ys, rows, weights.shape[0]), ("xh", "y"))
     return call(collect_all, shape((rows, xh * weights.shape[0]), BF16), (shares,))

time: 167 us -> 204 us (1.22)
  blocking collectives: 37.6 us -> 67.6 us
  waiting for transfers between devices: 41.1 us -> 50.7 us
  Pallas kernels: 27.9 us -> 18.6 us
  starting transfers between devices: 41.8 us -> 47.3 us
    all_to_all x3, blocking collectives: 37.6 us -> 67.6 us  [sent(): return lax.all_to_all(array, axes, 0, 0, tiled=True)]
    ppermute x0 -> x3, starting transfers between devices: none -> 12.3 us  [per_device(): inboxes.append(lax.ppermute(ahead, 'zh', [(hop, hop + 1)]))]
    pallas_call x13, Pallas kernels: 27.9 us -> 18.6 us  [call(): pl.pallas_call(kernel, out_shape=outs, in_specs=[HBM if i in far else VME...]
    all_to_all x3 -> x2, starting transfers between devices: 27 us -> 20.6 us  [sent(): return lax.all_to_all(array, axes, 0, 0, tiled=True)]
    all_gather x1, waiting for transfers between devices: 0.02 us -> 5.15 us  [per_device(): weights = lax.all_gather(scaled, (*Z, 'xl'), axis=0, tiled=True)]
    all_to_all x3 -> x2, waiting for transfers between devices: 38.4 us -> 42.3 us  [sent(): return lax.all_to_all(array, axes, 0, 0, tiled=True)]
    ppermute x3 -> x2, starting transfers between devices: 14.8 us -> 14.4 us  [shift(): return lax.ppermute(array, axis, pairs)]
  transfers between devices with their start and end apart: 7 -> 8, of which waited for: 5 -> 6; matrix products, arithmetic and copies ran while one was open for 1% -> 1% of each run, Pallas kernels for 13% -> 5%
where the time goes in v5:
time: 204 us; the launch traced here: 203 us
  blocking collectives  67.6 us (33%)
  waiting for transfers between devices  50.7 us (25%)
  starting transfers between devices  47.3 us (23%)
  Pallas kernels  18.6 us (9%)
  between operations  13.6 us (7%)
  local copies, waits for them, and re-layouts  3.62 us (2%)
    all_to_all x3, blocking collectives, sent(): return lax.all_to_all(array, axes, 0, 0, tiled=True)  67.6 us
    all_to_all x2, waiting for transfers between devices, sent(): return lax.all_to_all(array, axes, 0, 0, tiled=True)  42.3 us
    all_to_all x2, starting transfers between devices, sent(): return lax.all_to_all(array, axes, 0, 0, tiled=True)  20.6 us
    pallas_call x13, Pallas kernels, call(): pl.pallas_call(kernel, out_shape=outs, in_specs=[HBM if i in far else VME...  18.6 us
    ppermute x2, starting transfers between devices, shift(): return lax.ppermute(array, axis, pairs)  14.4 us
    ppermute x3, starting transfers between devices, per_device(): inboxes.append(lax.ppermute(ahead, 'zh', [(hop, hop + 1)]))  12.3 us
    all_gather x1, waiting for transfers between devices, per_device(): weights = lax.all_gather(scaled, (*Z, 'xl'), axis=0, tiled=True)  5.15 us
  transfers between devices with their start and end apart: 8, of which 6 were waited for; matrix products, arithmetic and copies ran while one was open for 1% of the time, Pallas kernels for 5%

profile of v5, /device:TPU:1, one launch (start us, length us, event | category | flops | bytes accessed | tf_op | source)
XLA Modules:
  0.0 203.2 jit_solution(17976173550147466256)
XLA Ops:
  6.5 1.6 fusion
  8.2 3.0 %shard_map.136 = bf16[32,32,896]{2,1,0:T(8,128)(2,1)} custom-call(bf16[32,8192]{1,0:T(8,128)(2,1)} %x_far.1, bf16[32,8192]{1,0:T(8,128)(2,1)} %z_far.1, bf16[32,1024]{1,0:T(8,128)(2,1)} %b_far.1, bf16[32,1024]{1,0:T(8,128)(2,1)} %c_far.1, bf16[32,128]{1,0:T(8,128)(2,1)} %dt_far.1), custom_call_target="tpu_custom_call" | custom-call | flops 4194304 | bytes 1048576 | tf_op jit(solution)/shard_map/pallas_call | solution.py:26
  11.2 10.6 %all-to-all-start = ((bf16[32,32,896]{2,1,0:T(8,128)(2,1)}), bf16[32,32,896]{2,1,0:T(8,128)(2,1)S(1)}, u32[]{:S(2)}, u32[]{:S(2)}) async-start(bf16[32,32,896]{2,1,0:T(8,128)(2,1)} %shard_map.136), calls=%async_computation | async-start | bytes 3670016 | tf_op jit(solution)/shard_map/all_to_all | solution.py:336
  21.9 0.1 dynamic-slice_bitcast_fusion
  21.9 0.1 copy.15
  22.0 0.1 copy.16
  22.2 0.8 dynamic_slice.19
  23.1 40.3 %all-to-all-done = bf16[32,32,896]{2,1,0:T(8,128)(2,1)S(1)} async-done(((bf16[32,32,896]{2,1,0:T(8,128)(2,1)}), bf16[32,32,896]{2,1,0:T(8,128)(2,1)S(1)}, u32[]{:S(2)}, u32[]{:S(2)}) %all-to-all-start) | async-done | bytes 1835040 | tf_op jit(solution)/shard_map/all_to_all | solution.py:336
  63.4 1.3 collective-permute-start
  64.7 0.7 shard_map.138
  65.4 0.1 collective-permute-done.halo_ref
  65.4 3.9 %shard_map.139 = (bf16[1024,256]{1,0:T(8,128)(2,1)S(1)}, bf16[1024,128]{1,0:T(8,128)(2,1)S(1)}, bf16[8,256,128]{2,1,0:T(8,128)(2,1)S(1)}, bf16[4,72,128]{2,1,0:T(8,128)(2,1)S(1)}) custom-call(bf16[1024,896]{1,0:T(8,128)(2,1)S(1)} %bitcast.18, bf16[8,512]{1,0:T(8,128)(2,1)S(1)} %collective-permute-done.halo_ref, f32[8,256]{1,0:T(8,128)S(1)} %select_maximum_fusion.taps_ref, ...), custom_call_target="tpu_custom_call" | custom-call | flops 33554432 | bytes 1048576 | tf_op jit(solution)/shard_map/pallas_call | solution.py:26
  69.3 0.8 copy-done.1
  70.1 0.6 copy-done.3
  70.8 10.0 %all-to-all-start.1 = ((bf16[4,72,128]{2,1,0:T(8,128)(2,1)}), bf16[4,72,128]{2,1,0:T(8,128)(2,1)S(1)}, u32[]{:S(2)}, u32[]{:S(2)}) async-start(bf16[4,72,128]{2,1,0:T(8,128)(2,1)} %copy-done.3), calls=%async_computation.1 | async-start | bytes 147456 | tf_op jit(solution)/shard_map/all_to_all | solution.py:336
  80.7 1.0 copy-done.2
  81.8 2.1 %shard_map.140 = (bf16[1024,128]{1,0:T(8,128)(2,1)S(1)}, f32[1024,256]{1,0:T(8,128)S(1)}) custom-call(bf16[1024,256]{1,0:T(8,128)(2,1)S(1)} %get-tuple-element.37.xs_ref, bf16[1024,128]{1,0:T(8,128)(2,1)S(1)} %get-tuple-element.38.b_ref, bf16[1024,384]{1,0:T(8,128)(2,1)S(1)} %get-tuple-element.39.late_ref.refs_4_, ...), custom_call_target="tpu_custom_call" | custom-call | flops 134217728 | bytes 1048576 | tf_op jit(solution)/shard_map/pallas_call | solution.py:26
  83.9 2.1 %all-to-all-done.1.inbox_ref = bf16[4,72,128]{2,1,0:T(8,128)(2,1)S(1)} async-done(((bf16[4,72,128]{2,1,0:T(8,128)(2,1)}), bf16[4,72,128]{2,1,0:T(8,128)(2,1)S(1)}, u32[]{:S(2)}, u32[]{:S(2)}) %all-to-all-start.1) | async-done | bytes 73760 | tf_op jit(solution)/shard_map/all_to_all | solution.py:336
  86.0 11.0 %collective-permute-start.1 = (bf16[64,128]{1,0:T(8,128)(2,1)S(1)}, bf16[64,128]{1,0:T(8,128)(2,1)S(1)}, u32[]{:S(2)}, u32[]{:S(2)}) collective-permute-start(bf16[64,128]{1,0:T(8,128)(2,1)S(1)} %get-tuple-element.47), channel_id=1, source_target_pairs={{0,128},{1,129},{2,130},{3,131},{4,132},{5,133},{6,134},{7,135},{8... | collective-permute-start | bytes 49160 | tf_op jit(solution)/shard_map/ppermute | solution.py:425
  97.0 0.9 collective-permute-done.1.inbox_ref.refs_0_
  97.8 0.7 collective-permute-start.2
  98.5 0.7 collective-permute-start.3
  99.2 7.7 %all_to_all.25 = bf16[4,64,128]{2,1,0:T(8,128)(2,1)S(1)} all-to-all(bf16[4,64,128]{2,1,0:T(8,128)(2,1)S(1)} %shard_map.144), channel_id=1, replica_groups=mesh['zh'=4,'zl'=4,'xh'=2,'xl'=2,'y'=4,'c'=2] {'zl'}, dimensions={0} | all-to-all | bytes 131072 | tf_op jit(solution)/shard_map/all_to_all | solution.py:336
  107.0 0.9 shard_map.145
  107.9 37.8 %all_to_all.26.gated_ref = bf16[4,512,256]{2,1,0:T(8,128)(2,1)S(1)} all-to-all(bf16[4,512,256]{2,1,0:T(8,128)(2,1)S(1)} %shard_map.145), channel_id=1, replica_groups=mesh['zh'=4,'zl'=4,'xh'=2,'xl'=2,'y'=4,'c'=2] {'xh','xl'}, dimensions={0} | all-to-all | bytes 2097152 | tf_op jit(solution)/shard_map/all_to_all | solution.py:336
  145.7 5.1 %all-gather.2.cloned.1.call-done.weights_far = bf16[2048,1024]{1,0:T(8,128)(2,1)} async-done(((bf16[64,1024]{1,0:T(8,128)(2,1)}), bf16[2048,1024]{1,0:T(8,128)(2,1)}) %all-gather.2.cloned.1.call-update) | async-done | bytes 4194320 | tf_op jit(solution)/shard_map/all_gather | solution.py:358
  150.8 6.9 %shard_map.146 = (bf16[256,2048]{1,0:T(8,128)(2,1)S(1)}, bf16[256,2048]{1,0:T(8,128)(2,1)S(1)}) custom-call(bf16[4,512,256]{2,1,0:T(8,128)(2,1)S(1)} %all_to_all.26.gated_ref, bf16[2048,1024]{1,0:T(8,128)(2,1)} %all-gather.2.cloned.1.call-done.weights_far), custom_call_target="tpu_custom_call" | custom-call | flops 1073741824 | bytes 1048576 | tf_op jit(solution)/shard_map/pallas_call | solution.py:26
  157.7 13.1 %collective-permute-start.4 = (bf16[256,2048]{1,0:T(8,128)(2,1)S(1)}, bf16[256,2048]{1,0:T(8,128)(2,1)S(1)}, u32[]{:S(2)}, u32[]{:S(2)}) collective-permute-start(bf16[256,2048]{1,0:T(8,128)(2,1)S(1)} %get-tuple-element.52), channel_id=1, source_target_pairs={{0,1},{1,0},{2,3},{3,2},{4,5},{5,4},{6,7},{7,6},{8,9},{9,8},{10,11... | collective-permute-start | bytes 3145736 | tf_op jit(solution)/shard_map/ppermute | solution.py:332
  170.9 2.3 %collective-permute-done.4.other_ref = bf16[256,2048]{1,0:T(8,128)(2,1)S(1)} collective-permute-done((bf16[256,2048]{1,0:T(8,128)(2,1)S(1)}, bf16[256,2048]{1,0:T(8,128)(2,1)S(1)}, u32[]{:S(2)}, u32[]{:S(2)}) %collective-permute-start.4) | collective-permute-done | bytes 1048608 | tf_op jit(solution)/shard_map/ppermute | solution.py:332
  173.1 0.2 shard_map.147
  173.4 22.1 %all_to_all.27.refs_0_ = bf16[8,32,2048]{2,1,0:T(8,128)(2,1)S(1)} all-to-all(bf16[8,32,2048]{2,1,0:T(8,128)(2,1)S(1)} %bitcast.19), channel_id=1, replica_groups=mesh['zh'=4,'zl'=4,'xh'=2,'xl'=2,'y'=4,'c'=2] {'xh','y'}, dimensions={0} | all-to-all | bytes 2097152 | tf_op jit(solution)/shard_map/all_to_all | solution.py:336
  195.5 0.8 shard_map.148
  (33 shorter events, 0.3 us)
Async XLA Ops:
  6.5 16.5 %copy-start = (f32[4,1024]{1,0:T(4,128)S(1)}, f32[4,1024]{1,0:T(4,128)}, u32[]{:S(2)}) copy-start(f32[4,1024]{1,0:T(4,128)} %param.22) | copy-start | bytes 49156
  6.5 144.3 %all-gather.2.cloned.1.call-start = ((), (), s32[]{:S(2)}) async-start(), calls=%async_computation.5 | async-start | bytes 4325376 | tf_op jit(solution)/shard_map/all_gather | solution.py:358
  11.1 10.7 %copy-start.7 = (f32[16]{0:T(128)S(1)}, f32[16]{0:T(128)}, u32[]{:S(2)}) copy-start(f32[16]{0:T(128)} %param.20) | copy-start | bytes 196
  11.1 10.7 %copy-start.6 = (f32[16]{0:T(128)S(1)}, f32[16]{0:T(128)}, u32[]{:S(2)}) copy-start(f32[16]{0:T(128)} %param.19) | copy-start | bytes 196
  11.1 11.0 %copy-start.8 = (f32[16]{0:T(128)S(1)}, f32[16]{0:T(128)}, u32[]{:S(2)}) copy-start(f32[16]{0:T(128)} %param.21) | copy-start | bytes 196
  11.2 11.0 %copy-start.4 = (f32[4,2,128]{2,1,0:T(2,128)S(1)}, f32[4,2,128]{2,1,0:T(2,128)}, u32[]{:S(2)}) copy-start(f32[4,2,128]{2,1,0:T(2,128)} %param.24) | copy-start | bytes 12292
  11.2 11.0 %copy-start.5 = (f32[2,128]{1,0:T(2,128)S(1)}, f32[2,128]{1,0:T(2,128)}, u32[]{:S(2)}) copy-start(f32[2,128]{1,0:T(2,128)} %param.25) | copy-start | bytes 3076
  11.2 52.2 %all-to-all-start = ((bf16[32,32,896]{2,1,0:T(8,128)(2,1)}), bf16[32,32,896]{2,1,0:T(8,128)(2,1)S(1)}, u32[]{:S(2)}, u32[]{:S(2)}) async-start(bf16[32,32,896]{2,1,0:T(8,128)(2,1)} %shard_map.136), calls=%async_computation | async-start | bytes 3670016 | tf_op jit(solution)/shard_map/all_to_all | solution.py:336
  63.4 2.1 %collective-permute-start = (bf16[8,512]{1,0:T(8,128)(2,1)S(1)}, bf16[8,512]{1,0:T(8,128)(2,1)S(1)}, u32[]{:S(2)}, u32[]{:S(2)}) collective-permute-start(bf16[8,512]{1,0:T(8,128)(2,1)S(1)} %shard_map.137), channel_id=1, source_target_pairs={{0,32},{32,64},{64,96},{96,128},{128,160},{160,192},{192,224},{224... | collective-permute-start | bytes 24584 | tf_op jit(solution)/shard_map/ppermute | solution.py:332
  69.3 0.8 copy-start.1
  70.1 0.6 copy-start.3
  70.8 15.2 %all-to-all-start.1 = ((bf16[4,72,128]{2,1,0:T(8,128)(2,1)}), bf16[4,72,128]{2,1,0:T(8,128)(2,1)S(1)}, u32[]{:S(2)}, u32[]{:S(2)}) async-start(bf16[4,72,128]{2,1,0:T(8,128)(2,1)} %copy-done.3), calls=%async_computation.1 | async-start | bytes 147456 | tf_op jit(solution)/shard_map/all_to_all | solution.py:336
  80.7 1.0 copy-start.2
  86.0 11.8 %collective-permute-start.1 = (bf16[64,128]{1,0:T(8,128)(2,1)S(1)}, bf16[64,128]{1,0:T(8,128)(2,1)S(1)}, u32[]{:S(2)}, u32[]{:S(2)}) collective-permute-start(bf16[64,128]{1,0:T(8,128)(2,1)S(1)} %get-tuple-element.47), channel_id=1, source_target_pairs={{0,128},{1,129},{2,130},{3,131},{4,132},{5,133},{6,134},{7,135},{8... | collective-permute-start | bytes 49160 | tf_op jit(solution)/shard_map/ppermute | solution.py:425
  97.8 0.7 collective-permute-start.2
  98.5 0.7 collective-permute-start.3
  157.7 15.4 %collective-permute-start.4 = (bf16[256,2048]{1,0:T(8,128)(2,1)S(1)}, bf16[256,2048]{1,0:T(8,128)(2,1)S(1)}, u32[]{:S(2)}, u32[]{:S(2)}) collective-permute-start(bf16[256,2048]{1,0:T(8,128)(2,1)S(1)} %get-tuple-element.52), channel_id=1, source_target_pairs={{0,1},{1,0},{2,3},{3,2},{4,5},{5,4},{6,7},{7,6},{8,9},{9,8},{10,11... | collective-permute-start | bytes 3145736 | tf_op jit(solution)/shard_map/ppermute | solution.py:332
Sparse Core Ops, SparseCore 0:
  9.4 141.3 all-gather.1

commit v6 on v5

--- a/solution.py
+++ b/solution.py
@@ -280,7 +280,16 @@
                     out_ref[d, half + at : half + at + rows, lo : lo + LANES] = ours
 
 
-def project(gated_ref, weights_far, theirs_ref, ours_ref, weights_ref, sems):
+def join(mine_ref, other_ref, gain_ref, out_ref):
+    rows = mine_ref.shape[0]
+    mine = mine_ref[...].astype(F32) * gain_ref[...]
+    other = other_ref[...].astype(F32) * gain_ref[...]
+    even = lax.axis_index("xl") == 0
+    out_ref[:rows] = jnp.where(even, mine, other).astype(BF16)
+    out_ref[rows:] = jnp.where(even, other, mine).astype(BF16)
+
+
+def project(gated_ref, weights_far, theirs_ref, ours_ref, weights_ref, wide_ref, sems):
     parts, rows, cols = gated_ref.shape
     half, width = ours_ref.shape
     step = width // sems.shape[0]
@@ -291,17 +300,14 @@
         loads[-1].start()
     squares = jnp.zeros((rows, 1), F32)
     for i in range(parts):
+        wide_ref[:, i * cols : (i + 1) * cols] = gated_ref[i]
         value = gated_ref[i].astype(F32)
         squares = squares + jnp.sum(value * value, axis=1, keepdims=True)
     scale = 1.0 / jnp.sqrt(squares / weights_ref.shape[1] + 1.0)
     for j, load in enumerate(loads):
         lo = j * step
         load.wait()
-        total = jnp.zeros((rows, step), F32)
-        for i in range(parts):
-            weights = weights_ref[lo : lo + step, i * cols : (i + 1) * cols]
-            total = total + nt(gated_ref[i], weights)
-        total = (total * scale).astype(BF16)
+        total = (nt(wide_ref[...], weights_ref[lo : lo + step]) * scale).astype(BF16)
         theirs_ref[:, lo : lo + step] = total[:half]
         ours_ref[:, lo : lo + step] = total[half:]
 
@@ -354,8 +360,14 @@
         size = values.shape[axis] // xs
         return lax.dynamic_slice_in_dim(values, part * size, size, axis)
 
-    scaled = (out_weight.T.astype(F32) * norm_weight[None]).astype(BF16)
-    weights = lax.all_gather(scaled, (*Z, "xl"), axis=0, tiled=True)
+    mine = out_weight.T
+    other = shift(mine, "xl", 1)
+    pair = call(
+        join,
+        shape((2 * mine.shape[0], mine.shape[1]), BF16),
+        (mine, other, norm_weight[None]),
+    )
+    weights = lax.all_gather(pair, Z, axis=0, tiled=True)
     out = call(
         pack,
         shape((plane, rows, 2 * cols + 3 * LANES), BF16),
@@ -442,7 +454,11 @@
     gated = sent(copies, X)
     count = tokens // (2 * xl)
     product = shape((count, weights.shape[0]), BF16)
-    room = [pltpu.VMEM(weights.shape, BF16), pltpu.SemaphoreType.DMA((8,))]
+    room = [
+        pltpu.VMEM(weights.shape, BF16),
+        pltpu.VMEM((2 * count, weights.shape[1]), BF16),
+        pltpu.SemaphoreType.DMA((8,)),
+    ]
     theirs, ours = call(project, (product, product), (gated, weights), room, 1 << 30, 50, (1,))
     both = call(add, product, (ours, shift(theirs, "c", 1)))
     shares = sent(both.reshape(xh * ys, rows, weights.shape[0]), ("xh", "y"))

time: 204 us -> 158 us (0.77)
  the two profiles are of different devices: /device:TPU:1 before, /device:TPU:384 now
where the time goes in v6:
time: 158 us
  waiting for transfers between devices  55.4 us (35%)
  blocking collectives  42.1 us (27%)
  starting transfers between devices  21.7 us (14%)
  Pallas kernels  19.4 us (12%)
  between operations  13.7 us (9%)
  local copies, waits for them, and re-layouts  5.21 us (3%)
    all_to_all x3, blocking collectives, sent(): return lax.all_to_all(array, axes, 0, 0, tiled=True)  42.1 us
    all_to_all x2, waiting for transfers between devices, sent(): return lax.all_to_all(array, axes, 0, 0, tiled=True)  27.8 us
    pallas_call x14, Pallas kernels, call(): pl.pallas_call(kernel, out_shape=outs, in_specs=[HBM if i in far else VME...  19.4 us
    ppermute x3, waiting for transfers between devices, per_device(): inboxes.append(lax.ppermute(ahead, 'zh', [(hop, hop + 1)]))  17.8 us
    all_to_all x2, starting transfers between devices, sent(): return lax.all_to_all(array, axes, 0, 0, tiled=True)  10.8 us
    ppermute x3, waiting for transfers between devices, shift(): return lax.ppermute(array, axis, pairs)  9.7 us
    ppermute x3, starting transfers between devices, shift(): return lax.ppermute(array, axis, pairs)  8.35 us
    unnamed x23, local copies, waits for them, and re-layouts  4.09 us
  transfers between devices with their start and end apart: 9, of which 6 were waited for; matrix products, arithmetic and copies ran while one was open for 1% of the time, Pallas kernels for 7%

profile of v6, /device:TPU:384, one launch (start us, length us, event | category | flops | bytes accessed | tf_op | source)
XLA Modules:
  0.0 157.6 jit_solution(7477806573999196456)
XLA Ops:
  6.5 3.5 %collective-permute-start.4 = (bf16[64,1024]{1,0:T(8,128)(2,1)}, bf16[64,1024]{1,0:T(8,128)(2,1)S(1)}, u32[]{:S(2)}, u32[]{:S(2)}) collective-permute-start(bf16[64,1024]{1,0:T(8,128)(2,1)} %bitcast.21), channel_id=1, source_target_pairs={{0,8},{8,0},{1,9},{9,1},{2,10},{10,2},{3,11},{11,3},{4,12},{12,4},... | collective-permute-start | bytes 393224 | tf_op jit(solution)/shard_map/ppermute | solution.py:338
  10.1 3.9 %collective-permute-done.4.other_ref = bf16[64,1024]{1,0:T(8,128)(2,1)S(1)} collective-permute-done((bf16[64,1024]{1,0:T(8,128)(2,1)}, bf16[64,1024]{1,0:T(8,128)(2,1)S(1)}, u32[]{:S(2)}, u32[]{:S(2)}) %collective-permute-start.4) | collective-permute-done | bytes 131104 | tf_op jit(solution)/shard_map/ppermute | solution.py:338
  14.0 0.9 copy-done.3
  14.9 0.7 copy-done.5
  15.6 0.8 shard_map.146
  16.4 3.0 %shard_map.136 = bf16[32,32,896]{2,1,0:T(8,128)(2,1)} custom-call(bf16[32,8192]{1,0:T(8,128)(2,1)} %x_far.1, bf16[32,8192]{1,0:T(8,128)(2,1)} %z_far.1, bf16[32,1024]{1,0:T(8,128)(2,1)} %b_far.1, bf16[32,1024]{1,0:T(8,128)(2,1)} %c_far.1, bf16[32,128]{1,0:T(8,128)(2,1)} %dt_far.1), custom_call_target="tpu_custom_call" | custom-call | flops 4194304 | bytes 1048576 | tf_op jit(solution)/shard_map/pallas_call | solution.py:26
  19.4 7.5 %all-to-all-start = ((bf16[32,32,896]{2,1,0:T(8,128)(2,1)}), bf16[32,32,896]{2,1,0:T(8,128)(2,1)S(1)}, u32[]{:S(2)}, u32[]{:S(2)}) async-start(bf16[32,32,896]{2,1,0:T(8,128)(2,1)} %shard_map.136), calls=%async_computation | async-start | bytes 3670016 | tf_op jit(solution)/shard_map/all_to_all | solution.py:342
  27.3 0.8 dynamic_slice.19
  28.2 24.7 %all-to-all-done = bf16[32,32,896]{2,1,0:T(8,128)(2,1)S(1)} async-done(((bf16[32,32,896]{2,1,0:T(8,128)(2,1)}), bf16[32,32,896]{2,1,0:T(8,128)(2,1)S(1)}, u32[]{:S(2)}, u32[]{:S(2)}) %all-to-all-start) | async-done | bytes 1835040 | tf_op jit(solution)/shard_map/all_to_all | solution.py:342
  52.9 2.9 %collective-permute-start = (bf16[8,512]{1,0:T(8,128)(2,1)S(1)}, bf16[8,512]{1,0:T(8,128)(2,1)S(1)}, u32[]{:S(2)}, u32[]{:S(2)}) collective-permute-start(bf16[8,512]{1,0:T(8,128)(2,1)S(1)} %shard_map.137), channel_id=1, source_target_pairs={{0,32},{32,64},{64,96},{96,128},{128,160},{160,192},{192,224},{224... | collective-permute-start | bytes 24584 | tf_op jit(solution)/shard_map/ppermute | solution.py:338
  55.8 0.7 shard_map.138
  56.5 3.1 %collective-permute-done.halo_ref = bf16[8,512]{1,0:T(8,128)(2,1)S(1)} collective-permute-done((bf16[8,512]{1,0:T(8,128)(2,1)S(1)}, bf16[8,512]{1,0:T(8,128)(2,1)S(1)}, u32[]{:S(2)}, u32[]{:S(2)}) %collective-permute-start) | collective-permute-done | bytes 8224 | tf_op jit(solution)/shard_map/ppermute | solution.py:338
  59.6 3.9 %shard_map.139 = (bf16[1024,256]{1,0:T(8,128)(2,1)S(1)}, bf16[1024,128]{1,0:T(8,128)(2,1)S(1)}, bf16[8,256,128]{2,1,0:T(8,128)(2,1)S(1)}, bf16[4,72,128]{2,1,0:T(8,128)(2,1)S(1)}) custom-call(bf16[1024,896]{1,0:T(8,128)(2,1)S(1)} %bitcast.18, bf16[8,512]{1,0:T(8,128)(2,1)S(1)} %collective-permute-done.halo_ref, f32[8,256]{1,0:T(8,128)S(1)} %select_maximum_fusion.taps_ref, ...), custom_call_target="tpu_custom_call" | custom-call | flops 33554432 | bytes 1048576 | tf_op jit(solution)/shard_map/pallas_call | solution.py:26
  63.5 0.8 copy-done.1
  64.3 0.6 copy-done.4
  65.0 3.3 %all-to-all-start.1 = ((bf16[4,72,128]{2,1,0:T(8,128)(2,1)}), bf16[4,72,128]{2,1,0:T(8,128)(2,1)S(1)}, u32[]{:S(2)}, u32[]{:S(2)}) async-start(bf16[4,72,128]{2,1,0:T(8,128)(2,1)} %copy-done.4), calls=%async_computation.1 | async-start | bytes 147456 | tf_op jit(solution)/shard_map/all_to_all | solution.py:342
  68.3 1.0 copy-done.2
  69.3 2.1 %shard_map.140 = (bf16[1024,128]{1,0:T(8,128)(2,1)S(1)}, f32[1024,256]{1,0:T(8,128)S(1)}) custom-call(bf16[1024,256]{1,0:T(8,128)(2,1)S(1)} %get-tuple-element.37.xs_ref, bf16[1024,128]{1,0:T(8,128)(2,1)S(1)} %get-tuple-element.38.b_ref, bf16[1024,384]{1,0:T(8,128)(2,1)S(1)} %get-tuple-element.39.late_ref.refs_4_, ...), custom_call_target="tpu_custom_call" | custom-call | flops 134217728 | bytes 1048576 | tf_op jit(solution)/shard_map/pallas_call | solution.py:26
  71.4 3.1 %all-to-all-done.1.inbox_ref = bf16[4,72,128]{2,1,0:T(8,128)(2,1)S(1)} async-done(((bf16[4,72,128]{2,1,0:T(8,128)(2,1)}), bf16[4,72,128]{2,1,0:T(8,128)(2,1)S(1)}, u32[]{:S(2)}, u32[]{:S(2)}) %all-to-all-start.1) | async-done | bytes 73760 | tf_op jit(solution)/shard_map/all_to_all | solution.py:342
  74.5 0.7 collective-permute-start.1
  75.2 0.7 collective-permute-start.2
  75.9 1.3 collective-permute-start.3
  77.2 17.8 %collective-permute-done.3.refs_2_ = bf16[64,128]{1,0:T(8,128)(2,1)S(1)} collective-permute-done((bf16[64,128]{1,0:T(8,128)(2,1)S(1)}, bf16[64,128]{1,0:T(8,128)(2,1)S(1)}, u32[]{:S(2)}, u32[]{:S(2)}) %collective-permute-start.3) | collective-permute-done | bytes 16416 | tf_op jit(solution)/shard_map/ppermute | solution.py:437
  95.1 8.7 %all_to_all.25 = bf16[4,64,128]{2,1,0:T(8,128)(2,1)S(1)} all-to-all(bf16[4,64,128]{2,1,0:T(8,128)(2,1)S(1)} %shard_map.144), channel_id=1, replica_groups=mesh['zh'=4,'zl'=4,'xh'=2,'xl'=2,'y'=4,'c'=2] {'zl'}, dimensions={0} | all-to-all | bytes 131072 | tf_op jit(solution)/shard_map/all_to_all | solution.py:342
  103.8 0.9 shard_map.145
  104.7 13.3 %all_to_all.26.gated_ref = bf16[4,512,256]{2,1,0:T(8,128)(2,1)S(1)} all-to-all(bf16[4,512,256]{2,1,0:T(8,128)(2,1)S(1)} %shard_map.145), channel_id=1, replica_groups=mesh['zh'=4,'zl'=4,'xh'=2,'xl'=2,'y'=4,'c'=2] {'xh','xl'}, dimensions={0} | all-to-all | bytes 2097152 | tf_op jit(solution)/shard_map/all_to_all | solution.py:342
  118.0 6.9 %shard_map.147 = (bf16[256,2048]{1,0:T(8,128)(2,1)S(1)}, bf16[256,2048]{1,0:T(8,128)(2,1)S(1)}) custom-call(bf16[4,512,256]{2,1,0:T(8,128)(2,1)S(1)} %all_to_all.26.gated_ref, bf16[2048,1024]{1,0:T(8,128)(2,1)} %all-gather.2.cloned.1.call-done.weights_far), custom_call_target="tpu_custom_call" | custom-call | flops 1073741824 | bytes 1048576 | tf_op jit(solution)/shard_map/pallas_call | solution.py:26
  125.0 1.9 %collective-permute-start.5 = (bf16[256,2048]{1,0:T(8,128)(2,1)S(1)}, bf16[256,2048]{1,0:T(8,128)(2,1)S(1)}, u32[]{:S(2)}, u32[]{:S(2)}) collective-permute-start(bf16[256,2048]{1,0:T(8,128)(2,1)S(1)} %get-tuple-element.52), channel_id=1, source_target_pairs={{0,1},{1,0},{2,3},{3,2},{4,5},{5,4},{6,7},{7,6},{8,9},{9,8},{10,11... | collective-permute-start | bytes 3145736 | tf_op jit(solution)/shard_map/ppermute | solution.py:338
  126.9 2.6 %collective-permute-done.5.other_ref = bf16[256,2048]{1,0:T(8,128)(2,1)S(1)} collective-permute-done((bf16[256,2048]{1,0:T(8,128)(2,1)S(1)}, bf16[256,2048]{1,0:T(8,128)(2,1)S(1)}, u32[]{:S(2)}, u32[]{:S(2)}) %collective-permute-start.5) | collective-permute-done | bytes 1048608 | tf_op jit(solution)/shard_map/ppermute | solution.py:338
  129.5 0.2 shard_map.148
  129.8 20.1 %all_to_all.27.refs_0_ = bf16[8,32,2048]{2,1,0:T(8,128)(2,1)S(1)} all-to-all(bf16[8,32,2048]{2,1,0:T(8,128)(2,1)S(1)} %bitcast.19), channel_id=1, replica_groups=mesh['zh'=4,'zl'=4,'xh'=2,'xl'=2,'y'=4,'c'=2] {'xh','y'}, dimensions={0} | all-to-all | bytes 2097152 | tf_op jit(solution)/shard_map/all_to_all | solution.py:342
  149.9 0.8 shard_map.149
  (39 shorter events, 0.6 us)
Async XLA Ops:
  6.5 21.5 %copy-start = (f32[4,1024]{1,0:T(4,128)S(1)}, f32[4,1024]{1,0:T(4,128)}, u32[]{:S(2)}) copy-start(f32[4,1024]{1,0:T(4,128)} %param.22) | copy-start | bytes 49156
  6.5 111.5 %all-gather.2.cloned.1.call-start = ((), (), s32[]{:S(2)}) async-start(), calls=%async_computation.5 | async-start | bytes 4456448 | tf_op jit(solution)/shard_map/all_gather | solution.py:370
  6.5 7.5 %collective-permute-start.4 = (bf16[64,1024]{1,0:T(8,128)(2,1)}, bf16[64,1024]{1,0:T(8,128)(2,1)S(1)}, u32[]{:S(2)}, u32[]{:S(2)}) collective-permute-start(bf16[64,1024]{1,0:T(8,128)(2,1)} %bitcast.21), channel_id=1, source_target_pairs={{0,8},{8,0},{1,9},{9,1},{2,10},{10,2},{3,11},{11,3},{4,12},{12,4},... | collective-permute-start | bytes 393224 | tf_op jit(solution)/shard_map/ppermute | solution.py:338
  14.0 0.9 copy-start.3
  14.9 0.7 copy-start.5
  19.3 7.5 %copy-start.9 = (f32[16]{0:T(128)S(1)}, f32[16]{0:T(128)}, u32[]{:S(2)}) copy-start(f32[16]{0:T(128)} %param.20) | copy-start | bytes 196
  19.4 7.6 %copy-start.8 = (f32[16]{0:T(128)S(1)}, f32[16]{0:T(128)}, u32[]{:S(2)}) copy-start(f32[16]{0:T(128)} %param.19) | copy-start | bytes 196
  19.4 7.8 %copy-start.10 = (f32[16]{0:T(128)S(1)}, f32[16]{0:T(128)}, u32[]{:S(2)}) copy-start(f32[16]{0:T(128)} %param.21) | copy-start | bytes 196
  19.4 7.9 %copy-start.6 = (f32[4,2,128]{2,1,0:T(2,128)S(1)}, f32[4,2,128]{2,1,0:T(2,128)}, u32[]{:S(2)}) copy-start(f32[4,2,128]{2,1,0:T(2,128)} %param.24) | copy-start | bytes 12292
  19.4 7.9 %copy-start.7 = (f32[2,128]{1,0:T(2,128)S(1)}, f32[2,128]{1,0:T(2,128)}, u32[]{:S(2)}) copy-start(f32[2,128]{1,0:T(2,128)} %param.25) | copy-start | bytes 3076
  19.4 33.5 %all-to-all-start = ((bf16[32,32,896]{2,1,0:T(8,128)(2,1)}), bf16[32,32,896]{2,1,0:T(8,128)(2,1)S(1)}, u32[]{:S(2)}, u32[]{:S(2)}) async-start(bf16[32,32,896]{2,1,0:T(8,128)(2,1)} %shard_map.136), calls=%async_computation | async-start | bytes 3670016 | tf_op jit(solution)/shard_map/all_to_all | solution.py:342
  52.9 6.7 %collective-permute-start = (bf16[8,512]{1,0:T(8,128)(2,1)S(1)}, bf16[8,512]{1,0:T(8,128)(2,1)S(1)}, u32[]{:S(2)}, u32[]{:S(2)}) collective-permute-start(bf16[8,512]{1,0:T(8,128)(2,1)S(1)} %shard_map.137), channel_id=1, source_target_pairs={{0,32},{32,64},{64,96},{96,128},{128,160},{160,192},{192,224},{224... | collective-permute-start | bytes 24584 | tf_op jit(solution)/shard_map/ppermute | solution.py:338
  63.5 0.8 copy-start.1
  64.3 0.6 copy-start.4
  65.0 9.6 %all-to-all-start.1 = ((bf16[4,72,128]{2,1,0:T(8,128)(2,1)}), bf16[4,72,128]{2,1,0:T(8,128)(2,1)S(1)}, u32[]{:S(2)}, u32[]{:S(2)}) async-start(bf16[4,72,128]{2,1,0:T(8,128)(2,1)} %copy-done.4), calls=%async_computation.1 | async-start | bytes 147456 | tf_op jit(solution)/shard_map/all_to_all | solution.py:342
  68.3 1.0 copy-start.2
  74.5 0.7 collective-permute-start.1
  75.2 0.7 collective-permute-start.2
  75.9 19.1 %collective-permute-start.3 = (bf16[64,128]{1,0:T(8,128)(2,1)S(1)}, bf16[64,128]{1,0:T(8,128)(2,1)S(1)}, u32[]{:S(2)}, u32[]{:S(2)}) collective-permute-start(bf16[64,128]{1,0:T(8,128)(2,1)S(1)} %shard_map.143), channel_id=1, source_target_pairs={{256,384},{257,385},{258,386},{259,387},{260,388},{261,389},{262,3... | collective-permute-start | bytes 49160 | tf_op jit(solution)/shard_map/ppermute | solution.py:437
  125.0 4.6 %collective-permute-start.5 = (bf16[256,2048]{1,0:T(8,128)(2,1)S(1)}, bf16[256,2048]{1,0:T(8,128)(2,1)S(1)}, u32[]{:S(2)}, u32[]{:S(2)}) collective-permute-start(bf16[256,2048]{1,0:T(8,128)(2,1)S(1)} %get-tuple-element.52), channel_id=1, source_target_pairs={{0,1},{1,0},{2,3},{3,2},{4,5},{5,4},{6,7},{7,6},{8,9},{9,8},{10,11... | collective-permute-start | bytes 3145736 | tf_op jit(solution)/shard_map/ppermute | solution.py:338
Sparse Core Ops, SparseCore 0:
  16.5 74.9 all-gather.1

commit v7 on v6

--- a/solution.py
+++ b/solution.py
@@ -98,10 +98,12 @@
         store.wait()
 
 
-def steps(packed_ref, heads_ref, dt_ref, cum_ref, sum_ref, late_ref):
+def steps(packed_ref, heads_ref, dt_ref, cum_ref, sum_ref, c_ref, z_ref):
     rows, tokens = dt_ref.shape
-    width = late_ref.shape[1]
-    late_ref[...] = packed_ref[:, packed_ref.shape[1] - LANES - width : packed_ref.shape[1] - LANES]
+    last = packed_ref.shape[1] - LANES
+    first = last - z_ref.shape[1]
+    c_ref[...] = packed_ref[:, first - LANES : first]
+    z_ref[...] = packed_ref[:, first:last]
     before = lax.broadcasted_iota(jnp.int32, (SPAN, SPAN), 0)
     after = lax.broadcasted_iota(jnp.int32, (SPAN, SPAN), 1)
     ones = (before <= after).astype(F32)
@@ -217,12 +219,12 @@
 
 
 def local(
-    xs_ref, b_ref, late_ref, halo_ref, group_taps_ref, dt_ref, cum_ref, held_ref, skip_ref,
+    xs_ref, b_ref, raw_ref, halo_ref, group_taps_ref, dt_ref, cum_ref, held_ref, skip_ref,
     c_ref, y_ref, padded,
 ):
     tokens, cols = xs_ref.shape
     padded[:8] = halo_ref[:, cols + LANES : cols + 2 * LANES].astype(F32)
-    padded[8:] = late_ref[:, :LANES].astype(F32)
+    padded[8:] = raw_ref[...].astype(F32)
     rows = lax.broadcasted_iota(jnp.int32, (SPAN, SPAN), 0)
     lanes = lax.broadcasted_iota(jnp.int32, (SPAN, SPAN), 1)
     causal = rows >= lanes
@@ -251,10 +253,10 @@
             y = jnp.where(left, y0, y1) + by_head(skip_ref[...], chunk, left) * xs.astype(F32)
             if k > 0:
                 y = y + nt(c, held_ref[k, lo : lo + LANES]) * by_head(grown, chunk, left)
-            y_ref[part, lo : lo + LANES] = y
-
-
-def finish(start_ref, c_ref, sum_ref, y_ref, late_ref, out_ref, *, ys):
+            y_ref[part, lo : lo + LANES] = y.astype(BF16)
+
+
+def finish(start_ref, c_ref, sum_ref, y_ref, z_ref, out_ref, *, ys):
     tokens, cols = y_ref.shape
     rows = tokens // 32
     half = out_ref.shape[1] // 2
@@ -266,8 +268,8 @@
         for chunk in range(cols // LANES):
             lo = chunk * LANES
             carry = nt(c_ref[part], start_ref[lo : lo + LANES]) * by_head(grown, chunk, left)
-            z = late_ref[part, LANES + lo : 2 * LANES + lo].astype(F32)
-            gated = ((y_ref[part, lo : lo + LANES] + carry) * silu(z)).astype(BF16)
+            z = z_ref[part, lo : lo + LANES].astype(F32)
+            gated = ((y_ref[part, lo : lo + LANES].astype(F32) + carry) * silu(z)).astype(BF16)
             for i in range(SPAN // (2 * rows)):
                 even = gated[2 * i * rows : (2 * i + 1) * rows]
                 odd = gated[(2 * i + 1) * rows : (2 * i + 2) * rows]
@@ -397,8 +399,11 @@
     halo = call(tail, shape((8, cols + 2 * LANES), BF16), (packed,), (), 1 << 16, 4)
     halo = shift(halo, Z, 1, wrap=False)
     by_token = shape((8, tokens), F32)
-    late = shape((tokens, cols + LANES), BF16)
-    dt, cum, sums, late = call(steps, (by_token, by_token, by_token, late), (packed, per_head))
+    dt, cum, sums, c_raw, z_raw = call(
+        steps,
+        (by_token, by_token, by_token, shape((tokens, LANES), BF16), shape((tokens, cols), BF16)),
+        (packed, per_head),
+    )
     x_conv, b_conv, held, states_out = call(
         scan_in,
         (
@@ -413,8 +418,8 @@
     )
     c_conv, y = call(
         local,
-        (shape((tokens, LANES), BF16), shape((tokens, cols), F32)),
-        (x_conv, b_conv, late, halo, group_taps, dt, cum, held, skip),
+        (shape((tokens, LANES), BF16), shape((tokens, cols), BF16)),
+        (x_conv, b_conv, c_raw, halo, group_taps, dt, cum, held, skip),
         [pltpu.VMEM((tokens + 8, LANES), F32)],
         1 << 27,
     )
@@ -447,7 +452,7 @@
     copies = call(
         finish_all,
         shape((xs, tokens // xl, cols), BF16),
-        (start, c_conv, sums, y, late),
+        (start, c_conv, sums, y, z_raw),
         (),
         1 << 25,
     )
@@ -457,7 +462,7 @@
     room = [
         pltpu.VMEM(weights.shape, BF16),
         pltpu.VMEM((2 * count, weights.shape[1]), BF16),
-        pltpu.SemaphoreType.DMA((8,)),
+        pltpu.SemaphoreType.DMA((4,)),
     ]
     theirs, ours = call(project, (product, product), (gated, weights), room, 1 << 30, 50, (1,))
     both = call(add, product, (ours, shift(theirs, "c", 1)))

time: 158 us -> 156 us (0.987)
  Pallas kernels: 19.4 us -> 16.7 us
    pallas_call x14, Pallas kernels: 19.4 us -> 16.7 us  [call(): pl.pallas_call(kernel, out_shape=outs, in_specs=[HBM if i in far else VME...]
    unnamed x23 -> x27, local copies, waits for them, and re-layouts: 4.09 us -> 4.86 us
where the time goes in v7:
time: 156 us; the launch traced here: 155 us
  waiting for transfers between devices  54.5 us (35%)
  blocking collectives  42.1 us (27%)
  starting transfers between devices  21.7 us (14%)
  Pallas kernels  16.7 us (11%)
  between operations  13.7 us (9%)
  local copies, waits for them, and re-layouts  5.97 us (4%)
    all_to_all x3, blocking collectives, sent(): return lax.all_to_all(array, axes, 0, 0, tiled=True)  42.1 us
    all_to_all x2, waiting for transfers between devices, sent(): return lax.all_to_all(array, axes, 0, 0, tiled=True)  27 us
    ppermute x3, waiting for transfers between devices, per_device(): inboxes.append(lax.ppermute(ahead, 'zh', [(hop, hop + 1)]))  17.9 us
    pallas_call x14, Pallas kernels, call(): pl.pallas_call(kernel, out_shape=outs, in_specs=[HBM if i in far else VME...  16.7 us
    all_to_all x2, starting transfers between devices, sent(): return lax.all_to_all(array, axes, 0, 0, tiled=True)  10.8 us
    ppermute x3, waiting for transfers between devices, shift(): return lax.ppermute(array, axis, pairs)  9.7 us
    ppermute x3, starting transfers between devices, shift(): return lax.ppermute(array, axis, pairs)  8.35 us
    unnamed x27, local copies, waits for them, and re-layouts  4.86 us
  transfers between devices with their start and end apart: 9, of which 6 were waited for; matrix products, arithmetic and copies ran while one was open for 1% of the time, Pallas kernels for 7%

profile of v7, /device:TPU:384, one launch (start us, length us, event | category | flops | bytes accessed | tf_op | source)
XLA Modules:
  0.0 154.8 jit_solution(6041507588256392438)
XLA Ops:
  6.5 3.5 %collective-permute-start.4 = (bf16[64,1024]{1,0:T(8,128)(2,1)}, bf16[64,1024]{1,0:T(8,128)(2,1)S(1)}, u32[]{:S(2)}, u32[]{:S(2)}) collective-permute-start(bf16[64,1024]{1,0:T(8,128)(2,1)} %bitcast.21), channel_id=1, source_target_pairs={{0,8},{8,0},{1,9},{9,1},{2,10},{10,2},{3,11},{11,3},{4,12},{12,4},... | collective-permute-start | bytes 393224 | tf_op jit(solution)/shard_map/ppermute | solution.py:340
  10.1 3.9 %collective-permute-done.4.other_ref = bf16[64,1024]{1,0:T(8,128)(2,1)S(1)} collective-permute-done((bf16[64,1024]{1,0:T(8,128)(2,1)}, bf16[64,1024]{1,0:T(8,128)(2,1)S(1)}, u32[]{:S(2)}, u32[]{:S(2)}) %collective-permute-start.4) | collective-permute-done | bytes 131104 | tf_op jit(solution)/shard_map/ppermute | solution.py:340
  14.0 0.9 copy-done.5
  14.9 0.7 copy-done.7
  15.6 0.8 shard_map.146
  16.4 3.0 %shard_map.136 = bf16[32,32,896]{2,1,0:T(8,128)(2,1)} custom-call(bf16[32,8192]{1,0:T(8,128)(2,1)} %x_far.1, bf16[32,8192]{1,0:T(8,128)(2,1)} %z_far.1, bf16[32,1024]{1,0:T(8,128)(2,1)} %b_far.1, bf16[32,1024]{1,0:T(8,128)(2,1)} %c_far.1, bf16[32,128]{1,0:T(8,128)(2,1)} %dt_far.1), custom_call_target="tpu_custom_call" | custom-call | flops 4194304 | bytes 1048576 | tf_op jit(solution)/shard_map/pallas_call | solution.py:26
  19.4 7.5 %all-to-all-start = ((bf16[32,32,896]{2,1,0:T(8,128)(2,1)}), bf16[32,32,896]{2,1,0:T(8,128)(2,1)S(1)}, u32[]{:S(2)}, u32[]{:S(2)}) async-start(bf16[32,32,896]{2,1,0:T(8,128)(2,1)} %shard_map.136), calls=%async_computation | async-start | bytes 3670016 | tf_op jit(solution)/shard_map/all_to_all | solution.py:344
  27.3 0.8 dynamic_slice.19
  28.2 24.7 %all-to-all-done = bf16[32,32,896]{2,1,0:T(8,128)(2,1)S(1)} async-done(((bf16[32,32,896]{2,1,0:T(8,128)(2,1)}), bf16[32,32,896]{2,1,0:T(8,128)(2,1)S(1)}, u32[]{:S(2)}, u32[]{:S(2)}) %all-to-all-start) | async-done | bytes 1835040 | tf_op jit(solution)/shard_map/all_to_all | solution.py:344
  52.9 2.9 %collective-permute-start = (bf16[8,512]{1,0:T(8,128)(2,1)S(1)}, bf16[8,512]{1,0:T(8,128)(2,1)S(1)}, u32[]{:S(2)}, u32[]{:S(2)}) collective-permute-start(bf16[8,512]{1,0:T(8,128)(2,1)S(1)} %shard_map.137), channel_id=1, source_target_pairs={{0,32},{32,64},{64,96},{96,128},{128,160},{160,192},{192,224},{224... | collective-permute-start | bytes 24584 | tf_op jit(solution)/shard_map/ppermute | solution.py:340
  55.8 0.7 shard_map.138
  56.5 3.1 %collective-permute-done.halo_ref = bf16[8,512]{1,0:T(8,128)(2,1)S(1)} collective-permute-done((bf16[8,512]{1,0:T(8,128)(2,1)S(1)}, bf16[8,512]{1,0:T(8,128)(2,1)S(1)}, u32[]{:S(2)}, u32[]{:S(2)}) %collective-permute-start) | collective-permute-done | bytes 8224 | tf_op jit(solution)/shard_map/ppermute | solution.py:340
  59.7 3.9 %shard_map.139 = (bf16[1024,256]{1,0:T(8,128)(2,1)S(1)}, bf16[1024,128]{1,0:T(8,128)(2,1)S(1)}, bf16[8,256,128]{2,1,0:T(8,128)(2,1)S(1)}, bf16[4,72,128]{2,1,0:T(8,128)(2,1)S(1)}) custom-call(bf16[1024,896]{1,0:T(8,128)(2,1)S(1)} %bitcast.18, bf16[8,512]{1,0:T(8,128)(2,1)S(1)} %collective-permute-done.halo_ref, f32[8,256]{1,0:T(8,128)S(1)} %select_maximum_fusion.taps_ref, ...), custom_call_target="tpu_custom_call" | custom-call | flops 33554432 | bytes 1048576 | tf_op jit(solution)/shard_map/pallas_call | solution.py:26
  63.6 0.7 copy-done.3
  64.3 0.6 copy-done.6
  64.9 3.3 %all-to-all-start.1 = ((bf16[4,72,128]{2,1,0:T(8,128)(2,1)}), bf16[4,72,128]{2,1,0:T(8,128)(2,1)S(1)}, u32[]{:S(2)}, u32[]{:S(2)}) async-start(bf16[4,72,128]{2,1,0:T(8,128)(2,1)} %copy-done.6), calls=%async_computation.1 | async-start | bytes 147456 | tf_op jit(solution)/shard_map/all_to_all | solution.py:344
  68.2 0.9 copy-done.2
  69.1 0.9 copy-done.4
  70.1 2.1 %shard_map.140 = (bf16[1024,128]{1,0:T(8,128)(2,1)S(1)}, bf16[1024,256]{1,0:T(8,128)(2,1)S(1)}) custom-call(bf16[1024,256]{1,0:T(8,128)(2,1)S(1)} %get-tuple-element.38.xs_ref, bf16[1024,128]{1,0:T(8,128)(2,1)S(1)} %copy-done.4, bf16[1024,128]{1,0:T(8,128)(2,1)S(1)} %copy-done.2, bf16[8,512]{1,0:T(8,128)(2,1)S(1)} %collective-permute-done.halo_ref, ...), custom_call_target="tpu_custom_call" | custom-call | flops 134217728 | bytes 1048576 | tf_op jit(solution)/shard_map/pallas_call | solution.py:26
  72.2 2.2 %all-to-all-done.1.inbox_ref = bf16[4,72,128]{2,1,0:T(8,128)(2,1)S(1)} async-done(((bf16[4,72,128]{2,1,0:T(8,128)(2,1)}), bf16[4,72,128]{2,1,0:T(8,128)(2,1)S(1)}, u32[]{:S(2)}, u32[]{:S(2)}) %all-to-all-start.1) | async-done | bytes 73760 | tf_op jit(solution)/shard_map/all_to_all | solution.py:344
  74.5 0.7 collective-permute-start.1
  75.2 0.7 collective-permute-start.2
  75.9 1.3 collective-permute-start.3
  77.2 17.9 %collective-permute-done.3.refs_2_ = bf16[64,128]{1,0:T(8,128)(2,1)S(1)} collective-permute-done((bf16[64,128]{1,0:T(8,128)(2,1)S(1)}, bf16[64,128]{1,0:T(8,128)(2,1)S(1)}, u32[]{:S(2)}, u32[]{:S(2)}) %collective-permute-start.3) | collective-permute-done | bytes 16416 | tf_op jit(solution)/shard_map/ppermute | solution.py:442
  95.1 8.6 %all_to_all.25 = bf16[4,64,128]{2,1,0:T(8,128)(2,1)S(1)} all-to-all(bf16[4,64,128]{2,1,0:T(8,128)(2,1)S(1)} %shard_map.144), channel_id=1, replica_groups=mesh['zh'=4,'zl'=4,'xh'=2,'xl'=2,'y'=4,'c'=2] {'zl'}, dimensions={0} | all-to-all | bytes 131072 | tf_op jit(solution)/shard_map/all_to_all | solution.py:344
  103.7 1.0 shard_map.145
  104.6 13.3 %all_to_all.26.gated_ref = bf16[4,512,256]{2,1,0:T(8,128)(2,1)S(1)} all-to-all(bf16[4,512,256]{2,1,0:T(8,128)(2,1)S(1)} %shard_map.145), channel_id=1, replica_groups=mesh['zh'=4,'zl'=4,'xh'=2,'xl'=2,'y'=4,'c'=2] {'xh','xl'}, dimensions={0} | all-to-all | bytes 2097152 | tf_op jit(solution)/shard_map/all_to_all | solution.py:344
  118.0 4.2 %shard_map.147 = (bf16[256,2048]{1,0:T(8,128)(2,1)S(1)}, bf16[256,2048]{1,0:T(8,128)(2,1)S(1)}) custom-call(bf16[4,512,256]{2,1,0:T(8,128)(2,1)S(1)} %all_to_all.26.gated_ref, bf16[2048,1024]{1,0:T(8,128)(2,1)} %all-gather.2.cloned.1.call-done.weights_far), custom_call_target="tpu_custom_call" | custom-call | flops 1073741824 | bytes 1048576 | tf_op jit(solution)/shard_map/pallas_call | solution.py:26
  122.2 1.9 %collective-permute-start.5 = (bf16[256,2048]{1,0:T(8,128)(2,1)S(1)}, bf16[256,2048]{1,0:T(8,128)(2,1)S(1)}, u32[]{:S(2)}, u32[]{:S(2)}) collective-permute-start(bf16[256,2048]{1,0:T(8,128)(2,1)S(1)} %get-tuple-element.54), channel_id=1, source_target_pairs={{0,1},{1,0},{2,3},{3,2},{4,5},{5,4},{6,7},{7,6},{8,9},{9,8},{10,11... | collective-permute-start | bytes 3145736 | tf_op jit(solution)/shard_map/ppermute | solution.py:340
  124.1 2.6 %collective-permute-done.5.other_ref = bf16[256,2048]{1,0:T(8,128)(2,1)S(1)} collective-permute-done((bf16[256,2048]{1,0:T(8,128)(2,1)S(1)}, bf16[256,2048]{1,0:T(8,128)(2,1)S(1)}, u32[]{:S(2)}, u32[]{:S(2)}) %collective-permute-start.5) | collective-permute-done | bytes 1048608 | tf_op jit(solution)/shard_map/ppermute | solution.py:340
  127.0 20.1 %all_to_all.27.refs_0_ = bf16[8,32,2048]{2,1,0:T(8,128)(2,1)S(1)} all-to-all(bf16[8,32,2048]{2,1,0:T(8,128)(2,1)S(1)} %bitcast.19), channel_id=1, replica_groups=mesh['zh'=4,'zl'=4,'xh'=2,'xl'=2,'y'=4,'c'=2] {'xh','y'}, dimensions={0} | all-to-all | bytes 2097152 | tf_op jit(solution)/shard_map/all_to_all | solution.py:344
  147.1 0.8 shard_map.149
  (43 shorter events, 0.8 us)
Async XLA Ops:
  6.5 21.5 %copy-start = (f32[4,1024]{1,0:T(4,128)S(1)}, f32[4,1024]{1,0:T(4,128)}, u32[]{:S(2)}) copy-start(f32[4,1024]{1,0:T(4,128)} %param.22) | copy-start | bytes 49156
  6.5 111.4 %all-gather.2.cloned.1.call-start = ((), (), s32[]{:S(2)}) async-start(), calls=%async_computation.5 | async-start | bytes 4456448 | tf_op jit(solution)/shard_map/all_gather | solution.py:372
  6.5 7.5 %collective-permute-start.4 = (bf16[64,1024]{1,0:T(8,128)(2,1)}, bf16[64,1024]{1,0:T(8,128)(2,1)S(1)}, u32[]{:S(2)}, u32[]{:S(2)}) collective-permute-start(bf16[64,1024]{1,0:T(8,128)(2,1)} %bitcast.21), channel_id=1, source_target_pairs={{0,8},{8,0},{1,9},{9,1},{2,10},{10,2},{3,11},{11,3},{4,12},{12,4},... | collective-permute-start | bytes 393224 | tf_op jit(solution)/shard_map/ppermute | solution.py:340
  14.0 0.9 copy-start.5
  14.9 0.7 copy-start.7
  19.4 7.5 %copy-start.11 = (f32[16]{0:T(128)S(1)}, f32[16]{0:T(128)}, u32[]{:S(2)}) copy-start(f32[16]{0:T(128)} %param.20) | copy-start | bytes 196
  19.4 7.5 %copy-start.10 = (f32[16]{0:T(128)S(1)}, f32[16]{0:T(128)}, u32[]{:S(2)}) copy-start(f32[16]{0:T(128)} %param.19) | copy-start | bytes 196
  19.4 7.8 %copy-start.12 = (f32[16]{0:T(128)S(1)}, f32[16]{0:T(128)}, u32[]{:S(2)}) copy-start(f32[16]{0:T(128)} %param.21) | copy-start | bytes 196
  19.4 7.9 %copy-start.8 = (f32[4,2,128]{2,1,0:T(2,128)S(1)}, f32[4,2,128]{2,1,0:T(2,128)}, u32[]{:S(2)}) copy-start(f32[4,2,128]{2,1,0:T(2,128)} %param.24) | copy-start | bytes 12292
  19.4 7.9 %copy-start.9 = (f32[2,128]{1,0:T(2,128)S(1)}, f32[2,128]{1,0:T(2,128)}, u32[]{:S(2)}) copy-start(f32[2,128]{1,0:T(2,128)} %param.25) | copy-start | bytes 3076
  19.4 33.5 %all-to-all-start = ((bf16[32,32,896]{2,1,0:T(8,128)(2,1)}), bf16[32,32,896]{2,1,0:T(8,128)(2,1)S(1)}, u32[]{:S(2)}, u32[]{:S(2)}) async-start(bf16[32,32,896]{2,1,0:T(8,128)(2,1)} %shard_map.136), calls=%async_computation | async-start | bytes 3670016 | tf_op jit(solution)/shard_map/all_to_all | solution.py:344
  52.9 6.7 %collective-permute-start = (bf16[8,512]{1,0:T(8,128)(2,1)S(1)}, bf16[8,512]{1,0:T(8,128)(2,1)S(1)}, u32[]{:S(2)}, u32[]{:S(2)}) collective-permute-start(bf16[8,512]{1,0:T(8,128)(2,1)S(1)} %shard_map.137), channel_id=1, source_target_pairs={{0,32},{32,64},{64,96},{96,128},{128,160},{160,192},{192,224},{224... | collective-permute-start | bytes 24584 | tf_op jit(solution)/shard_map/ppermute | solution.py:340
  56.5 7.0 %copy-start.1 = (bf16[1024,128]{1,0:T(8,128)(2,1)}, bf16[1024,128]{1,0:T(8,128)(2,1)S(1)}, u32[]{:S(2)}) copy-start(bf16[1024,128]{1,0:T(8,128)(2,1)S(1)} %get-tuple-element.40.raw_ref) | copy-start | bytes 786436
  63.5 0.7 copy-start.3
  64.2 0.6 copy-start.6
  64.9 9.5 %all-to-all-start.1 = ((bf16[4,72,128]{2,1,0:T(8,128)(2,1)}), bf16[4,72,128]{2,1,0:T(8,128)(2,1)S(1)}, u32[]{:S(2)}, u32[]{:S(2)}) async-start(bf16[4,72,128]{2,1,0:T(8,128)(2,1)} %copy-done.6), calls=%async_computation.1 | async-start | bytes 147456 | tf_op jit(solution)/shard_map/all_to_all | solution.py:344
  68.2 1.0 copy-start.2
  69.1 0.9 copy-start.4
  74.5 0.7 collective-permute-start.1
  75.2 0.7 collective-permute-start.2
  75.9 19.2 %collective-permute-start.3 = (bf16[64,128]{1,0:T(8,128)(2,1)S(1)}, bf16[64,128]{1,0:T(8,128)(2,1)S(1)}, u32[]{:S(2)}, u32[]{:S(2)}) collective-permute-start(bf16[64,128]{1,0:T(8,128)(2,1)S(1)} %shard_map.143), channel_id=1, source_target_pairs={{256,384},{257,385},{258,386},{259,387},{260,388},{261,389},{262,3... | collective-permute-start | bytes 49160 | tf_op jit(solution)/shard_map/ppermute | solution.py:442
  122.2 4.6 %collective-permute-start.5 = (bf16[256,2048]{1,0:T(8,128)(2,1)S(1)}, bf16[256,2048]{1,0:T(8,128)(2,1)S(1)}, u32[]{:S(2)}, u32[]{:S(2)}) collective-permute-start(bf16[256,2048]{1,0:T(8,128)(2,1)S(1)} %get-tuple-element.54), channel_id=1, source_target_pairs={{0,1},{1,0},{2,3},{3,2},{4,5},{5,4},{6,7},{7,6},{8,9},{9,8},{10,11... | collective-permute-start | bytes 3145736 | tf_op jit(solution)/shard_map/ppermute | solution.py:340
Sparse Core Ops, SparseCore 0:
  16.5 75.0 all-gather.1

commit v8 on v7

--- a/solution.py
+++ b/solution.py
@@ -200,19 +200,20 @@
         log = log + mine
     before_ref[8 * count :] = jnp.broadcast_to(log, (8, LANES))
     group_ref[...] = state
-    sent_ref[...] = state.astype(BF16)
+    sent_ref[:rows] = state.astype(BF16)
+    sent_ref[rows:] = in_terms(log)
 
 
 def extend(inbox_ref, before_ref, group_ref, sent_ref):
     grown = jnp.exp(before_ref[before_ref.shape[0] - 1 :])
-    sent_ref[...] = (grown * inbox_ref[...].astype(F32) + group_ref[...]).astype(BF16)
-
-
-def scan_far(inner_ref, before_ref, *refs):
-    starts_ref = refs[-1]
-    state = refs[0][...].astype(F32)
-    for ref in refs[1:-1]:
-        state = state + ref[...].astype(F32)
+    last = inbox_ref[: sent_ref.shape[0]].astype(F32)
+    sent_ref[...] = (grown * last + group_ref[...]).astype(BF16)
+
+
+def scan_far(last_ref, earlier_ref, inner_ref, before_ref, starts_ref):
+    rows = earlier_ref.shape[0]
+    grown = jnp.exp(from_terms(last_ref[rows:]))
+    state = last_ref[:rows].astype(F32) + grown * earlier_ref[...].astype(F32)
     for i in range(inner_ref.shape[0]):
         grown = jnp.exp(before_ref[8 * i : 8 * i + 1])
         starts_ref[i] = (grown * state + inner_ref[i]).astype(BF16)
@@ -350,7 +351,7 @@
 ):
     xh, xl, ys, cs = (lax.axis_size(a) for a in PLANE)
     xs = xh * xl
-    zh, zl = (lax.axis_size(a) for a in Z)
+    _, zl = (lax.axis_size(a) for a in Z)
     plane = xs * ys * cs
     rows, inner = x_proj.shape
     cols = inner // plane
@@ -431,16 +432,14 @@
             shape(near, F32),
             shape((8 * zl + 8, LANES), F32),
             shape(near[1:], F32),
-            shape(near[1:], BF16),
+            shape((near[1] + 8, STATE), BF16),
         ),
         (near_in,),
     )
-    inboxes = []
-    for hop in range(zh - 1):
-        if hop:
-            ahead = call(extend, shape(near[1:], BF16), (inboxes[-1], before, group))
-        inboxes.append(lax.ppermute(ahead, "zh", [(hop, hop + 1)]))
-    starts = call(scan_far, shape(near, BF16), (inner, before, *inboxes))
+    last = shift(ahead, "zh", 1, wrap=False)
+    two = call(extend, shape(near[1:], BF16), (last, before, group))
+    earlier = shift(two, "zh", 2, wrap=False)
+    starts = call(scan_far, shape(near, BF16), (last, earlier, inner, before))
     start = sent(starts, "zl").reshape(cols, STATE)
 
     def finish_all(*refs):

time: 156 us -> 161 us (1.032)
  the two profiles are of different devices: /device:TPU:384 before, /device:TPU:1 now
where the time goes in v8:
time: 161 us
  starting transfers between devices  53.7 us (33%)
  blocking collectives  38.6 us (24%)
  waiting for transfers between devices  31.9 us (20%)
  Pallas kernels  16.7 us (10%)
  between operations  13.6 us (8%)
  local copies, waits for them, and re-layouts  5.98 us (4%)
    all_to_all x3, blocking collectives, sent(): return lax.all_to_all(array, axes, 0, 0, tiled=True)  38.6 us
    ppermute x5, starting transfers between devices, shift(): return lax.ppermute(array, axis, pairs)  35.6 us
    all_to_all x2, waiting for transfers between devices, sent(): return lax.all_to_all(array, axes, 0, 0, tiled=True)  25.3 us
    all_to_all x2, starting transfers between devices, sent(): return lax.all_to_all(array, axes, 0, 0, tiled=True)  18 us
    pallas_call x13, Pallas kernels, call(): pl.pallas_call(kernel, out_shape=outs, in_specs=[HBM if i in far else VME...  16.7 us
    ppermute x5, waiting for transfers between devices, shift(): return lax.ppermute(array, axis, pairs)  6.63 us
    unnamed x27, local copies, waits for them, and re-layouts  4.86 us
  transfers between devices with their start and end apart: 8, of which 7 were waited for; matrix products, arithmetic and copies ran while one was open for 1% of the time, Pallas kernels for 7%

profile of v8, /device:TPU:1, one launch (start us, length us, event | category | flops | bytes accessed | tf_op | source)
XLA Modules:
  0.0 160.6 jit_solution(1158198075805638865)
XLA Ops:
  6.5 4.1 %collective-permute-start.3 = (bf16[64,1024]{1,0:T(8,128)(2,1)}, bf16[64,1024]{1,0:T(8,128)(2,1)S(1)}, u32[]{:S(2)}, u32[]{:S(2)}) collective-permute-start(bf16[64,1024]{1,0:T(8,128)(2,1)} %bitcast.21), channel_id=1, source_target_pairs={{0,8},{8,0},{1,9},{9,1},{2,10},{10,2},{3,11},{11,3},{4,12},{12,4},... | collective-permute-start | bytes 393224 | tf_op jit(solution)/shard_map/ppermute | solution.py:341
  10.6 2.6 %collective-permute-done.3.other_ref = bf16[64,1024]{1,0:T(8,128)(2,1)S(1)} collective-permute-done((bf16[64,1024]{1,0:T(8,128)(2,1)}, bf16[64,1024]{1,0:T(8,128)(2,1)S(1)}, u32[]{:S(2)}, u32[]{:S(2)}) %collective-permute-start.3) | collective-permute-done | bytes 131104 | tf_op jit(solution)/shard_map/ppermute | solution.py:341
  13.2 0.9 copy-done.5
  14.1 0.7 copy-done.7
  14.8 0.8 shard_map.145
  15.5 3.0 %shard_map.136 = bf16[32,32,896]{2,1,0:T(8,128)(2,1)} custom-call(bf16[32,8192]{1,0:T(8,128)(2,1)} %x_far.1, bf16[32,8192]{1,0:T(8,128)(2,1)} %z_far.1, bf16[32,1024]{1,0:T(8,128)(2,1)} %b_far.1, bf16[32,1024]{1,0:T(8,128)(2,1)} %c_far.1, bf16[32,128]{1,0:T(8,128)(2,1)} %dt_far.1), custom_call_target="tpu_custom_call" | custom-call | flops 4194304 | bytes 1048576 | tf_op jit(solution)/shard_map/pallas_call | solution.py:26
  18.6 11.2 %all-to-all-start = ((bf16[32,32,896]{2,1,0:T(8,128)(2,1)}), bf16[32,32,896]{2,1,0:T(8,128)(2,1)S(1)}, u32[]{:S(2)}, u32[]{:S(2)}) async-start(bf16[32,32,896]{2,1,0:T(8,128)(2,1)} %shard_map.136), calls=%async_computation | async-start | bytes 3670016 | tf_op jit(solution)/shard_map/all_to_all | solution.py:345
  30.2 0.8 dynamic_slice.19
  31.1 24.3 %all-to-all-done = bf16[32,32,896]{2,1,0:T(8,128)(2,1)S(1)} async-done(((bf16[32,32,896]{2,1,0:T(8,128)(2,1)}), bf16[32,32,896]{2,1,0:T(8,128)(2,1)S(1)}, u32[]{:S(2)}, u32[]{:S(2)}) %all-to-all-start) | async-done | bytes 1835040 | tf_op jit(solution)/shard_map/all_to_all | solution.py:345
  55.4 1.8 %collective-permute-start = (bf16[8,512]{1,0:T(8,128)(2,1)S(1)}, bf16[8,512]{1,0:T(8,128)(2,1)S(1)}, u32[]{:S(2)}, u32[]{:S(2)}) collective-permute-start(bf16[8,512]{1,0:T(8,128)(2,1)S(1)} %shard_map.137), channel_id=1, source_target_pairs={{0,32},{32,64},{64,96},{96,128},{128,160},{160,192},{192,224},{224... | collective-permute-start | bytes 24584 | tf_op jit(solution)/shard_map/ppermute | solution.py:341
  57.2 0.7 shard_map.138
  58.0 3.9 %shard_map.139 = (bf16[1024,256]{1,0:T(8,128)(2,1)S(1)}, bf16[1024,128]{1,0:T(8,128)(2,1)S(1)}, bf16[8,256,128]{2,1,0:T(8,128)(2,1)S(1)}, bf16[4,72,128]{2,1,0:T(8,128)(2,1)S(1)}) custom-call(bf16[1024,896]{1,0:T(8,128)(2,1)S(1)} %bitcast.18, bf16[8,512]{1,0:T(8,128)(2,1)S(1)} %collective-permute-done.halo_ref, f32[8,256]{1,0:T(8,128)S(1)} %select_maximum_fusion.taps_ref, ...), custom_call_target="tpu_custom_call" | custom-call | flops 33554432 | bytes 1048576 | tf_op jit(solution)/shard_map/pallas_call | solution.py:26
  61.9 0.7 copy-done.3
  62.6 0.6 copy-done.6
  63.2 6.8 %all-to-all-start.1 = ((bf16[4,72,128]{2,1,0:T(8,128)(2,1)}), bf16[4,72,128]{2,1,0:T(8,128)(2,1)S(1)}, u32[]{:S(2)}, u32[]{:S(2)}) async-start(bf16[4,72,128]{2,1,0:T(8,128)(2,1)} %copy-done.6), calls=%async_computation.1 | async-start | bytes 147456 | tf_op jit(solution)/shard_map/all_to_all | solution.py:345
  70.0 1.0 copy-done.2
  71.0 0.9 copy-done.4
  71.9 2.1 %shard_map.140 = (bf16[1024,128]{1,0:T(8,128)(2,1)S(1)}, bf16[1024,256]{1,0:T(8,128)(2,1)S(1)}) custom-call(bf16[1024,256]{1,0:T(8,128)(2,1)S(1)} %get-tuple-element.38.xs_ref, bf16[1024,128]{1,0:T(8,128)(2,1)S(1)} %copy-done.4, bf16[1024,128]{1,0:T(8,128)(2,1)S(1)} %copy-done.2, bf16[8,512]{1,0:T(8,128)(2,1)S(1)} %collective-permute-done.halo_ref, ...), custom_call_target="tpu_custom_call" | custom-call | flops 134217728 | bytes 1048576 | tf_op jit(solution)/shard_map/pallas_call | solution.py:26
  74.1 0.9 all-to-all-done.1.inbox_ref
  75.0 8.6 %collective-permute-start.1 = (bf16[72,128]{1,0:T(8,128)(2,1)S(1)}, bf16[72,128]{1,0:T(8,128)(2,1)S(1)}, u32[]{:S(2)}, u32[]{:S(2)}) collective-permute-start(bf16[72,128]{1,0:T(8,128)(2,1)S(1)} %get-tuple-element.46), channel_id=1, source_target_pairs={{0,128},{128,256},{256,384},{1,129},{129,257},{257,385},{2,130},{1... | collective-permute-start | bytes 55304 | tf_op jit(solution)/shard_map/ppermute | solution.py:341
  83.7 0.9 collective-permute-done.1.inbox_ref.last_ref
  84.6 12.9 %collective-permute-start.2 = (bf16[64,128]{1,0:T(8,128)(2,1)S(1)}, bf16[64,128]{1,0:T(8,128)(2,1)S(1)}, u32[]{:S(2)}, u32[]{:S(2)}) collective-permute-start(bf16[64,128]{1,0:T(8,128)(2,1)S(1)} %shard_map.142), channel_id=1, source_target_pairs={{0,256},{128,384},{1,257},{129,385},{2,258},{130,386},{3,259},{131... | collective-permute-start | bytes 49160 | tf_op jit(solution)/shard_map/ppermute | solution.py:341
  97.4 0.9 collective-permute-done.2.earlier_ref
  98.3 8.1 %all_to_all.25 = bf16[4,64,128]{2,1,0:T(8,128)(2,1)S(1)} all-to-all(bf16[4,64,128]{2,1,0:T(8,128)(2,1)S(1)} %shard_map.143), channel_id=1, replica_groups=mesh['zh'=4,'zl'=4,'xh'=2,'xl'=2,'y'=4,'c'=2] {'zl'}, dimensions={0} | all-to-all | bytes 131072 | tf_op jit(solution)/shard_map/all_to_all | solution.py:345
  106.4 1.0 shard_map.144
  107.4 12.2 %all_to_all.26.gated_ref = bf16[4,512,256]{2,1,0:T(8,128)(2,1)S(1)} all-to-all(bf16[4,512,256]{2,1,0:T(8,128)(2,1)S(1)} %shard_map.144), channel_id=1, replica_groups=mesh['zh'=4,'zl'=4,'xh'=2,'xl'=2,'y'=4,'c'=2] {'xh','xl'}, dimensions={0} | all-to-all | bytes 2097152 | tf_op jit(solution)/shard_map/all_to_all | solution.py:345
  119.5 4.2 %shard_map.146 = (bf16[256,2048]{1,0:T(8,128)(2,1)S(1)}, bf16[256,2048]{1,0:T(8,128)(2,1)S(1)}) custom-call(bf16[4,512,256]{2,1,0:T(8,128)(2,1)S(1)} %all_to_all.26.gated_ref, bf16[2048,1024]{1,0:T(8,128)(2,1)} %all-gather.2.cloned.1.call-done.weights_far), custom_call_target="tpu_custom_call" | custom-call | flops 1073741824 | bytes 1048576 | tf_op jit(solution)/shard_map/pallas_call | solution.py:26
  123.8 8.3 %collective-permute-start.4 = (bf16[256,2048]{1,0:T(8,128)(2,1)S(1)}, bf16[256,2048]{1,0:T(8,128)(2,1)S(1)}, u32[]{:S(2)}, u32[]{:S(2)}) collective-permute-start(bf16[256,2048]{1,0:T(8,128)(2,1)S(1)} %get-tuple-element.54), channel_id=1, source_target_pairs={{0,1},{1,0},{2,3},{3,2},{4,5},{5,4},{6,7},{7,6},{8,9},{9,8},{10,11... | collective-permute-start | bytes 3145736 | tf_op jit(solution)/shard_map/ppermute | solution.py:341
  132.0 2.3 %collective-permute-done.4.other_ref = bf16[256,2048]{1,0:T(8,128)(2,1)S(1)} collective-permute-done((bf16[256,2048]{1,0:T(8,128)(2,1)S(1)}, bf16[256,2048]{1,0:T(8,128)(2,1)S(1)}, u32[]{:S(2)}, u32[]{:S(2)}) %collective-permute-start.4) | collective-permute-done | bytes 1048608 | tf_op jit(solution)/shard_map/ppermute | solution.py:341
  134.3 0.2 shard_map.147
  134.5 18.4 %all_to_all.27.refs_0_ = bf16[8,32,2048]{2,1,0:T(8,128)(2,1)S(1)} all-to-all(bf16[8,32,2048]{2,1,0:T(8,128)(2,1)S(1)} %bitcast.19), channel_id=1, replica_groups=mesh['zh'=4,'zl'=4,'xh'=2,'xl'=2,'y'=4,'c'=2] {'xh','y'}, dimensions={0} | all-to-all | bytes 2097152 | tf_op jit(solution)/shard_map/all_to_all | solution.py:345
  152.9 0.8 shard_map.148
  (40 shorter events, 0.7 us)
Async XLA Ops:
  6.5 24.4 %copy-start = (f32[4,1024]{1,0:T(4,128)S(1)}, f32[4,1024]{1,0:T(4,128)}, u32[]{:S(2)}) copy-start(f32[4,1024]{1,0:T(4,128)} %param.22) | copy-start | bytes 49156
  6.5 113.0 %all-gather.2.cloned.1.call-start = ((), (), s32[]{:S(2)}) async-start(), calls=%async_computation.5 | async-start | bytes 4456448 | tf_op jit(solution)/shard_map/all_gather | solution.py:373
  6.5 6.6 %collective-permute-start.3 = (bf16[64,1024]{1,0:T(8,128)(2,1)}, bf16[64,1024]{1,0:T(8,128)(2,1)S(1)}, u32[]{:S(2)}, u32[]{:S(2)}) collective-permute-start(bf16[64,1024]{1,0:T(8,128)(2,1)} %bitcast.21), channel_id=1, source_target_pairs={{0,8},{8,0},{1,9},{9,1},{2,10},{10,2},{3,11},{11,3},{4,12},{12,4},... | collective-permute-start | bytes 393224 | tf_op jit(solution)/shard_map/ppermute | solution.py:341
  13.2 0.9 copy-start.5
  14.1 0.7 copy-start.7
  18.5 11.3 %copy-start.11 = (f32[16]{0:T(128)S(1)}, f32[16]{0:T(128)}, u32[]{:S(2)}) copy-start(f32[16]{0:T(128)} %param.20) | copy-start | bytes 196
  18.5 11.3 %copy-start.10 = (f32[16]{0:T(128)S(1)}, f32[16]{0:T(128)}, u32[]{:S(2)}) copy-start(f32[16]{0:T(128)} %param.19) | copy-start | bytes 196
  18.5 11.6 %copy-start.12 = (f32[16]{0:T(128)S(1)}, f32[16]{0:T(128)}, u32[]{:S(2)}) copy-start(f32[16]{0:T(128)} %param.21) | copy-start | bytes 196
  18.5 11.6 %copy-start.8 = (f32[4,2,128]{2,1,0:T(2,128)S(1)}, f32[4,2,128]{2,1,0:T(2,128)}, u32[]{:S(2)}) copy-start(f32[4,2,128]{2,1,0:T(2,128)} %param.24) | copy-start | bytes 12292
  18.6 11.6 %copy-start.9 = (f32[2,128]{1,0:T(2,128)S(1)}, f32[2,128]{1,0:T(2,128)}, u32[]{:S(2)}) copy-start(f32[2,128]{1,0:T(2,128)} %param.25) | copy-start | bytes 3076
  18.6 36.8 %all-to-all-start = ((bf16[32,32,896]{2,1,0:T(8,128)(2,1)}), bf16[32,32,896]{2,1,0:T(8,128)(2,1)S(1)}, u32[]{:S(2)}, u32[]{:S(2)}) async-start(bf16[32,32,896]{2,1,0:T(8,128)(2,1)} %shard_map.136), calls=%async_computation | async-start | bytes 3670016 | tf_op jit(solution)/shard_map/all_to_all | solution.py:345
  55.4 2.6 %collective-permute-start = (bf16[8,512]{1,0:T(8,128)(2,1)S(1)}, bf16[8,512]{1,0:T(8,128)(2,1)S(1)}, u32[]{:S(2)}, u32[]{:S(2)}) collective-permute-start(bf16[8,512]{1,0:T(8,128)(2,1)S(1)} %shard_map.137), channel_id=1, source_target_pairs={{0,32},{32,64},{64,96},{96,128},{128,160},{160,192},{192,224},{224... | collective-permute-start | bytes 24584 | tf_op jit(solution)/shard_map/ppermute | solution.py:341
  57.9 4.0 %copy-start.1 = (bf16[1024,128]{1,0:T(8,128)(2,1)}, bf16[1024,128]{1,0:T(8,128)(2,1)S(1)}, u32[]{:S(2)}) copy-start(bf16[1024,128]{1,0:T(8,128)(2,1)S(1)} %get-tuple-element.40.raw_ref) | copy-start | bytes 786436
  61.9 0.7 copy-start.3
  62.6 0.6 copy-start.6
  63.2 11.8 %all-to-all-start.1 = ((bf16[4,72,128]{2,1,0:T(8,128)(2,1)}), bf16[4,72,128]{2,1,0:T(8,128)(2,1)S(1)}, u32[]{:S(2)}, u32[]{:S(2)}) async-start(bf16[4,72,128]{2,1,0:T(8,128)(2,1)} %copy-done.6), calls=%async_computation.1 | async-start | bytes 147456 | tf_op jit(solution)/shard_map/all_to_all | solution.py:345
  70.0 1.0 copy-start.2
  71.0 0.9 copy-start.4
  75.0 9.5 %collective-permute-start.1 = (bf16[72,128]{1,0:T(8,128)(2,1)S(1)}, bf16[72,128]{1,0:T(8,128)(2,1)S(1)}, u32[]{:S(2)}, u32[]{:S(2)}) collective-permute-start(bf16[72,128]{1,0:T(8,128)(2,1)S(1)} %get-tuple-element.46), channel_id=1, source_target_pairs={{0,128},{128,256},{256,384},{1,129},{129,257},{257,385},{2,130},{1... | collective-permute-start | bytes 55304 | tf_op jit(solution)/shard_map/ppermute | solution.py:341
  84.6 13.7 %collective-permute-start.2 = (bf16[64,128]{1,0:T(8,128)(2,1)S(1)}, bf16[64,128]{1,0:T(8,128)(2,1)S(1)}, u32[]{:S(2)}, u32[]{:S(2)}) collective-permute-start(bf16[64,128]{1,0:T(8,128)(2,1)S(1)} %shard_map.142), channel_id=1, source_target_pairs={{0,256},{128,384},{1,257},{129,385},{2,258},{130,386},{3,259},{131... | collective-permute-start | bytes 49160 | tf_op jit(solution)/shard_map/ppermute | solution.py:341
  123.8 10.5 %collective-permute-start.4 = (bf16[256,2048]{1,0:T(8,128)(2,1)S(1)}, bf16[256,2048]{1,0:T(8,128)(2,1)S(1)}, u32[]{:S(2)}, u32[]{:S(2)}) collective-permute-start(bf16[256,2048]{1,0:T(8,128)(2,1)S(1)} %get-tuple-element.54), channel_id=1, source_target_pairs={{0,1},{1,0},{2,3},{3,2},{4,5},{5,4},{6,7},{7,6},{8,9},{9,8},{10,11... | collective-permute-start | bytes 3145736 | tf_op jit(solution)/shard_map/ppermute | solution.py:341
Sparse Core Ops, SparseCore 0:
  15.7 76.0 all-gather.1

commit v9 on v7

--- a/solution.py
+++ b/solution.py
@@ -72,25 +72,28 @@
         load.start()
     for load in loads:
         load.wait()
-    count, _, width = out_ref.shape
+    count = out_ref.shape[0]
     groups = b_ref.shape[1] // LANES
     parts = count // groups
     cols = x_ref.shape[1] // count
     heads = dt_ref.shape[1] // count
-    dt = dt_ref[...].astype(F32)
+    tokens = dt_ref.shape[0]
+    dt = jnp.concatenate([dt_ref[...].astype(F32), jnp.zeros((LANES - tokens, LANES), F32)]).T
     stores = [
         pltpu.make_async_copy(out_ref.at[d], out_far.at[d], out_sems.at[d]) for d in range(count)
     ]
     for d in range(count):
         part, group = divmod(d, groups)
         at = group * parts + part
-        mine = dt if at == 0 else pltpu.roll(dt, LANES - at * heads, 1)
         side = slice(group * LANES, (group + 1) * LANES)
-        out_ref[d, :, :cols] = x_ref[:, at * cols : (at + 1) * cols]
-        out_ref[d, :, cols : cols + LANES] = b_ref[:, side]
-        out_ref[d, :, cols + LANES : cols + 2 * LANES] = c_ref[:, side]
-        out_ref[d, :, cols + 2 * LANES : width - LANES] = z_ref[:, at * cols : (at + 1) * cols]
-        out_ref[d, :, width - LANES :] = mine.astype(BF16)
+        spans = [slice(at * cols + lo, at * cols + lo + LANES) for lo in range(0, cols, LANES)]
+        pieces = [x_ref[:, span] for span in spans] + [b_ref[:, side], c_ref[:, side]]
+        pieces += [z_ref[:, span] for span in spans]
+        for i, piece in enumerate(pieces):
+            out_ref[d, i * tokens : (i + 1) * tokens] = piece
+        mine = dt[at * heads : (at + 1) * heads]
+        mine = jnp.concatenate([mine, jnp.zeros((8 - heads, LANES), F32)])
+        out_ref[d, len(pieces) * tokens :] = mine.astype(BF16)
         if d > 0:
             stores[d - 1].start()
     stores[-1].start()
@@ -98,12 +101,15 @@
         store.wait()
 
 
+def piece_of(packed_ref, i, first, last):
+    tokens = (packed_ref.shape[1] - 8) // 6
+    sources = packed_ref[first // tokens : last // tokens, i * tokens : (i + 1) * tokens]
+    return sources.reshape(last - first, LANES)
+
+
 def steps(packed_ref, heads_ref, dt_ref, cum_ref, sum_ref, c_ref, z_ref):
     rows, tokens = dt_ref.shape
-    last = packed_ref.shape[1] - LANES
-    first = last - z_ref.shape[1]
-    c_ref[...] = packed_ref[:, first - LANES : first]
-    z_ref[...] = packed_ref[:, first:last]
+    own = (packed_ref.shape[1] - 8) // 6
     before = lax.broadcasted_iota(jnp.int32, (SPAN, SPAN), 0)
     after = lax.broadcasted_iota(jnp.int32, (SPAN, SPAN), 1)
     ones = (before <= after).astype(F32)
@@ -111,7 +117,13 @@
     total = jnp.zeros((rows, 1), F32)
     for k in range(tokens // SPAN):
         part = slice(k * SPAN, (k + 1) * SPAN)
-        raw = packed_ref[part, packed_ref.shape[1] - LANES :].astype(F32).T[:rows] + bias
+        c_ref[part] = piece_of(packed_ref, 3, k * SPAN, (k + 1) * SPAN)
+        for i in range(2):
+            z = piece_of(packed_ref, 4 + i, k * SPAN, (k + 1) * SPAN)
+            z_ref[part, i * LANES : (i + 1) * LANES] = z
+        first = k * SPAN // own
+        raw = [packed_ref[first + i, 6 * own :, :own].astype(F32) for i in range(SPAN // own)]
+        raw = jnp.concatenate(raw, axis=1) + bias
         dt = jnp.maximum(raw, 0.0) + jnp.log1p(jnp.exp(-jnp.abs(raw)))
         dt_ref[:, part] = dt
         cum = lax.dot(
@@ -127,11 +139,6 @@
     return filled.T
 
 
-def fill_padded(padded, halo_ref, packed_ref, width):
-    padded[:8] = halo_ref[:, :width].astype(F32)
-    padded[8:] = packed_ref[:, :width].astype(F32)
-
-
 def conv(padded, taps, bias, k, lo):
     first = 8 + k * SPAN - 3
     total = bias + taps[0] * padded[first : first + SPAN, lo : lo + LANES]
@@ -146,7 +153,10 @@
 ):
     tokens, cols = xs_ref.shape
     blocks = tokens // SPAN
-    fill_padded(padded, halo_ref, packed_ref, cols + LANES)
+    padded[:8] = halo_ref[:, : cols + LANES].astype(F32)
+    for i in range(3):
+        side = slice(i * LANES, (i + 1) * LANES)
+        padded[8:, side] = piece_of(packed_ref, i, 0, tokens).astype(F32)
     left, top = left_half(), top_half()
     group_taps = [group_taps_ref[j : j + 1] for j in range(4)]
     states = [jnp.zeros((LANES, STATE), F32) for _ in range(cols // LANES)]
@@ -318,8 +328,12 @@
     out_ref[...] = (ours_ref[...].astype(F32) + other_ref[...].astype(F32)).astype(BF16)
 
 
-def tail(array_ref, out_ref):
-    out_ref[...] = array_ref[array_ref.shape[0] - out_ref.shape[0] :, : out_ref.shape[1]]
+def tail(packed_ref, out_ref):
+    own = (packed_ref.shape[1] - 8) // 6
+    last = packed_ref.shape[0] - 1
+    for i in range(out_ref.shape[1] // LANES):
+        side = slice(i * LANES, (i + 1) * LANES)
+        out_ref[:, side] = packed_ref[last, (i + 1) * own - 8 : (i + 1) * own]
 
 
 def collect(shares_ref, out_ref, *, ys):
@@ -372,11 +386,11 @@
     weights = lax.all_gather(pair, Z, axis=0, tiled=True)
     out = call(
         pack,
-        shape((plane, rows, 2 * cols + 3 * LANES), BF16),
+        shape((plane, 6 * rows + 8, LANES), BF16),
         (x_proj, z_proj, b_proj, c_proj, dt_raw),
         [pltpu.VMEM(a.shape, BF16) for a in (x_proj, z_proj, b_proj, c_proj, dt_raw)]
         + [
-            pltpu.VMEM((plane, rows, 2 * cols + 3 * LANES), BF16),
+            pltpu.VMEM((plane, 6 * rows + 8, LANES), BF16),
             pltpu.SemaphoreType.DMA((5,)),
             pltpu.SemaphoreType.DMA((plane,)),
         ],
@@ -395,7 +409,6 @@
     packed, per_head, skip, taps, group_taps = lax.optimization_barrier(
         (sent(out, PLANE), per_head, skip, taps, group_taps)
     )
-    packed = packed.reshape(tokens, 2 * cols + 3 * LANES)
     halo = call(tail, shape((8, cols + 2 * LANES), BF16), (packed,), (), 1 << 16, 4)
     halo = shift(halo, Z, 1, wrap=False)
     by_token = shape((8, tokens), F32)

time: 156 us -> 156 us (level)
  waiting for transfers between devices: 54.5 us -> 48.6 us
  local copies, waits for them, and re-layouts: 5.97 us -> 9.02 us
  blocking collectives: 42.1 us -> 44.3 us
    all_to_all x2, waiting for transfers between devices: 27 us -> 21 us  [sent(): return lax.all_to_all(array, axes, 0, 0, tiled=True)]
    all_to_all x3, blocking collectives: 42.1 us -> 44.3 us  [sent(): return lax.all_to_all(array, axes, 0, 0, tiled=True)]
    unnamed x27 -> x39, local copies, waits for them, and re-layouts: 4.86 us -> 6.74 us
  transfers between devices with their start and end apart: 9 -> 9, of which waited for: 6 -> 6; matrix products, arithmetic and copies ran while one was open for 1% -> 2% of each run, Pallas kernels for 7% -> 7%
where the time goes in v9:
time: 156 us; the launch traced here: 155 us
  waiting for transfers between devices  48.6 us (31%)
  blocking collectives  44.3 us (28%)
  starting transfers between devices  21.9 us (14%)
  Pallas kernels  16.6 us (11%)
  between operations  13.7 us (9%)
  local copies, waits for them, and re-layouts  9.02 us (6%)
    all_to_all x3, blocking collectives, sent(): return lax.all_to_all(array, axes, 0, 0, tiled=True)  44.3 us
    all_to_all x2, waiting for transfers between devices, sent(): return lax.all_to_all(array, axes, 0, 0, tiled=True)  21 us
    ppermute x3, waiting for transfers between devices, per_device(): inboxes.append(lax.ppermute(ahead, 'zh', [(hop, hop + 1)]))  17.9 us
    pallas_call x14, Pallas kernels, call(): pl.pallas_call(kernel, out_shape=outs, in_specs=[HBM if i in far else VME...  16.6 us
    all_to_all x2, starting transfers between devices, sent(): return lax.all_to_all(array, axes, 0, 0, tiled=True)  10.8 us
    ppermute x3, waiting for transfers between devices, shift(): return lax.ppermute(array, axis, pairs)  9.71 us
    ppermute x3, starting transfers between devices, shift(): return lax.ppermute(array, axis, pairs)  8.49 us
    unnamed x39, local copies, waits for them, and re-layouts  6.74 us
  transfers between devices with their start and end apart: 9, of which 6 were waited for; matrix products, arithmetic and copies ran while one was open for 2% of the time, Pallas kernels for 7%

profile of v9, /device:TPU:384, one launch (start us, length us, event | category | flops | bytes accessed | tf_op | source)
XLA Modules:
  0.0 154.8 jit_solution(16618648281871399241)
XLA Ops:
  6.5 3.5 %collective-permute-start.4 = (bf16[64,1024]{1,0:T(8,128)(2,1)}, bf16[64,1024]{1,0:T(8,128)(2,1)S(1)}, u32[]{:S(2)}, u32[]{:S(2)}) collective-permute-start(bf16[64,1024]{1,0:T(8,128)(2,1)} %bitcast.17), channel_id=1, source_target_pairs={{0,8},{8,0},{1,9},{9,1},{2,10},{10,2},{3,11},{11,3},{4,12},{12,4},... | collective-permute-start | bytes 393224 | tf_op jit(solution)/shard_map/ppermute | solution.py:354
  10.1 3.9 %collective-permute-done.4.other_ref = bf16[64,1024]{1,0:T(8,128)(2,1)S(1)} collective-permute-done((bf16[64,1024]{1,0:T(8,128)(2,1)}, bf16[64,1024]{1,0:T(8,128)(2,1)S(1)}, u32[]{:S(2)}, u32[]{:S(2)}) %collective-permute-start.4) | collective-permute-done | bytes 131104 | tf_op jit(solution)/shard_map/ppermute | solution.py:354
  14.0 0.9 copy-done.5
  14.9 0.7 copy-done.12
  15.6 0.8 shard_map.146
  16.4 2.9 %shard_map.136 = bf16[32,200,128]{2,1,0:T(8,128)(2,1)} custom-call(bf16[32,8192]{1,0:T(8,128)(2,1)} %x_far.1, bf16[32,8192]{1,0:T(8,128)(2,1)} %z_far.1, bf16[32,1024]{1,0:T(8,128)(2,1)} %b_far.1, bf16[32,1024]{1,0:T(8,128)(2,1)} %c_far.1, bf16[32,128]{1,0:T(8,128)(2,1)} %dt_far.1), custom_call_target="tpu_custom_call" | custom-call | flops 4194304 | bytes 1048576 | tf_op jit(solution)/shard_map/pallas_call | solution.py:26
  19.3 7.5 %all-to-all-start = ((bf16[32,200,128]{2,1,0:T(8,128)(2,1)}), bf16[32,200,128]{2,1,0:T(8,128)(2,1)S(1)}, u32[]{:S(2)}, u32[]{:S(2)}) async-start(bf16[32,200,128]{2,1,0:T(8,128)(2,1)} %shard_map.136), calls=%async_computation | async-start | bytes 3276800 | tf_op jit(solution)/shard_map/all_to_all | solution.py:358
  27.2 0.8 dynamic_slice.19
  29.8 20.8 %all-to-all-done.packed_ref = bf16[32,200,128]{2,1,0:T(8,128)(2,1)S(1)} async-done(((bf16[32,200,128]{2,1,0:T(8,128)(2,1)}), bf16[32,200,128]{2,1,0:T(8,128)(2,1)S(1)}, u32[]{:S(2)}, u32[]{:S(2)}) %all-to-all-start) | async-done | bytes 1638432 | tf_op jit(solution)/shard_map/all_to_all | solution.py:358
  50.6 3.1 %collective-permute-start = (bf16[8,512]{1,0:T(8,128)(2,1)S(1)}, bf16[8,512]{1,0:T(8,128)(2,1)S(1)}, u32[]{:S(2)}, u32[]{:S(2)}) collective-permute-start(bf16[8,512]{1,0:T(8,128)(2,1)S(1)} %shard_map.137), channel_id=1, source_target_pairs={{0,32},{32,64},{64,96},{96,128},{128,160},{160,192},{192,224},{224... | collective-permute-start | bytes 24584 | tf_op jit(solution)/shard_map/ppermute | solution.py:354
  53.7 0.7 shard_map.138
  54.3 3.2 %collective-permute-done.halo_ref = bf16[8,512]{1,0:T(8,128)(2,1)S(1)} collective-permute-done((bf16[8,512]{1,0:T(8,128)(2,1)S(1)}, bf16[8,512]{1,0:T(8,128)(2,1)S(1)}, u32[]{:S(2)}, u32[]{:S(2)}) %collective-permute-start) | collective-permute-done | bytes 8224 | tf_op jit(solution)/shard_map/ppermute | solution.py:354
  57.5 3.9 %shard_map.139 = (bf16[1024,256]{1,0:T(8,128)(2,1)S(1)}, bf16[1024,128]{1,0:T(8,128)(2,1)S(1)}, bf16[8,256,128]{2,1,0:T(8,128)(2,1)S(1)}, bf16[4,72,128]{2,1,0:T(8,128)(2,1)S(1)}) custom-call(bf16[32,200,128]{2,1,0:T(8,128)(2,1)S(1)} %all-to-all-done.packed_ref, bf16[8,512]{1,0:T(8,128)(2,1)S(1)} %collective-permute-done.halo_ref, f32[8,256]{1,0:T(8,128)S(1)} %copy-done.11, ...), custom_call_target="tpu_custom_call" | custom-call | flops 33554432 | bytes 1048576 | tf_op jit(solution)/shard_map/pallas_call | solution.py:26
  61.4 0.7 copy-done.1
  62.7 3.3 %all-to-all-start.1 = ((bf16[4,72,128]{2,1,0:T(8,128)(2,1)}), bf16[4,72,128]{2,1,0:T(8,128)(2,1)S(1)}, u32[]{:S(2)}, u32[]{:S(2)}) async-start(bf16[4,72,128]{2,1,0:T(8,128)(2,1)} %copy-done.8), calls=%async_computation.1 | async-start | bytes 147456 | tf_op jit(solution)/shard_map/all_to_all | solution.py:358
  66.0 0.9 copy-done.2
  67.0 0.8 copy-done.4
  67.7 0.7 copy-done.7
  68.4 0.7 copy-done.10
  69.1 0.7 copy-done.13
  69.8 2.1 %shard_map.140 = (bf16[1024,128]{1,0:T(8,128)(2,1)S(1)}, bf16[1024,256]{1,0:T(8,128)(2,1)S(1)}) custom-call(bf16[1024,256]{1,0:T(8,128)(2,1)S(1)} %get-tuple-element.38.xs_ref, bf16[1024,128]{1,0:T(8,128)(2,1)S(1)} %copy-done.2, bf16[1024,128]{1,0:T(8,128)(2,1)S(1)} %get-tuple-element.40.raw_ref, bf16[8,512]{1,0:T(8,128)(2,1)S(1)} %copy-done.10, ...), custom_call_target="tpu_custom_call" | custom-call | flops 134217728 | bytes 1048576 | tf_op jit(solution)/shard_map/pallas_call | solution.py:26
  72.2 0.7 collective-permute-start.1
  73.6 1.3 collective-permute-start.3
  74.9 17.8 %collective-permute-done.3.refs_2_ = bf16[64,128]{1,0:T(8,128)(2,1)S(1)} collective-permute-done((bf16[64,128]{1,0:T(8,128)(2,1)S(1)}, bf16[64,128]{1,0:T(8,128)(2,1)S(1)}, u32[]{:S(2)}, u32[]{:S(2)}) %collective-permute-start.3) | collective-permute-done | bytes 16416 | tf_op jit(solution)/shard_map/ppermute | solution.py:455
  92.8 10.8 %all_to_all.25 = bf16[4,64,128]{2,1,0:T(8,128)(2,1)S(1)} all-to-all(bf16[4,64,128]{2,1,0:T(8,128)(2,1)S(1)} %shard_map.144), channel_id=1, replica_groups=mesh['zh'=4,'zl'=4,'xh'=2,'xl'=2,'y'=4,'c'=2] {'zl'}, dimensions={0} | all-to-all | bytes 131072 | tf_op jit(solution)/shard_map/all_to_all | solution.py:358
  103.6 1.0 shard_map.145
  104.6 13.3 %all_to_all.26.gated_ref = bf16[4,512,256]{2,1,0:T(8,128)(2,1)S(1)} all-to-all(bf16[4,512,256]{2,1,0:T(8,128)(2,1)S(1)} %shard_map.145), channel_id=1, replica_groups=mesh['zh'=4,'zl'=4,'xh'=2,'xl'=2,'y'=4,'c'=2] {'xh','xl'}, dimensions={0} | all-to-all | bytes 2097152 | tf_op jit(solution)/shard_map/all_to_all | solution.py:358
  117.9 4.2 %shard_map.147 = (bf16[256,2048]{1,0:T(8,128)(2,1)S(1)}, bf16[256,2048]{1,0:T(8,128)(2,1)S(1)}) custom-call(bf16[4,512,256]{2,1,0:T(8,128)(2,1)S(1)} %all_to_all.26.gated_ref, bf16[2048,1024]{1,0:T(8,128)(2,1)} %all-gather.2.cloned.1.call-done.weights_far), custom_call_target="tpu_custom_call" | custom-call | flops 1073741824 | bytes 1048576 | tf_op jit(solution)/shard_map/pallas_call | solution.py:26
  122.1 1.9 %collective-permute-start.5 = (bf16[256,2048]{1,0:T(8,128)(2,1)S(1)}, bf16[256,2048]{1,0:T(8,128)(2,1)S(1)}, u32[]{:S(2)}, u32[]{:S(2)}) collective-permute-start(bf16[256,2048]{1,0:T(8,128)(2,1)S(1)} %get-tuple-element.54), channel_id=1, source_target_pairs={{0,1},{1,0},{2,3},{3,2},{4,5},{5,4},{6,7},{7,6},{8,9},{9,8},{10,11... | collective-permute-start | bytes 3145736 | tf_op jit(solution)/shard_map/ppermute | solution.py:354
  124.0 2.6 %collective-permute-done.5.other_ref = bf16[256,2048]{1,0:T(8,128)(2,1)S(1)} collective-permute-done((bf16[256,2048]{1,0:T(8,128)(2,1)S(1)}, bf16[256,2048]{1,0:T(8,128)(2,1)S(1)}, u32[]{:S(2)}, u32[]{:S(2)}) %collective-permute-start.5) | collective-permute-done | bytes 1048608 | tf_op jit(solution)/shard_map/ppermute | solution.py:354
  126.9 20.1 %all_to_all.27.refs_0_ = bf16[8,32,2048]{2,1,0:T(8,128)(2,1)S(1)} all-to-all(bf16[8,32,2048]{2,1,0:T(8,128)(2,1)S(1)} %bitcast.15), channel_id=1, replica_groups=mesh['zh'=4,'zl'=4,'xh'=2,'xl'=2,'y'=4,'c'=2] {'xh','y'}, dimensions={0} | all-to-all | bytes 2097152 | tf_op jit(solution)/shard_map/all_to_all | solution.py:358
  147.1 0.8 shard_map.149
  (55 shorter events, 4.2 us)
Async XLA Ops:
  6.5 22.0 %copy-start = (f32[4,1024]{1,0:T(4,128)S(1)}, f32[4,1024]{1,0:T(4,128)}, u32[]{:S(2)}) copy-start(f32[4,1024]{1,0:T(4,128)} %param.22) | copy-start | bytes 49156
  6.5 111.3 %all-gather.2.cloned.1.call-start = ((), (), s32[]{:S(2)}) async-start(), calls=%async_computation.5 | async-start | bytes 4456448 | tf_op jit(solution)/shard_map/all_gather | solution.py:386
  6.5 7.5 %collective-permute-start.4 = (bf16[64,1024]{1,0:T(8,128)(2,1)}, bf16[64,1024]{1,0:T(8,128)(2,1)S(1)}, u32[]{:S(2)}, u32[]{:S(2)}) collective-permute-start(bf16[64,1024]{1,0:T(8,128)(2,1)} %bitcast.17), channel_id=1, source_target_pairs={{0,8},{8,0},{1,9},{9,1},{2,10},{10,2},{3,11},{11,3},{4,12},{12,4},... | collective-permute-start | bytes 393224 | tf_op jit(solution)/shard_map/ppermute | solution.py:354
  14.0 0.9 copy-start.5
  14.9 0.7 copy-start.12
  19.3 7.5 %copy-start.17 = (f32[16]{0:T(128)S(1)}, f32[16]{0:T(128)}, u32[]{:S(2)}) copy-start(f32[16]{0:T(128)} %param.20) | copy-start | bytes 196
  19.3 7.5 %copy-start.16 = (f32[16]{0:T(128)S(1)}, f32[16]{0:T(128)}, u32[]{:S(2)}) copy-start(f32[16]{0:T(128)} %param.19) | copy-start | bytes 196
  19.3 7.8 %copy-start.18 = (f32[16]{0:T(128)S(1)}, f32[16]{0:T(128)}, u32[]{:S(2)}) copy-start(f32[16]{0:T(128)} %param.21) | copy-start | bytes 196
  19.3 7.9 %copy-start.14 = (f32[4,2,128]{2,1,0:T(2,128)S(1)}, f32[4,2,128]{2,1,0:T(2,128)}, u32[]{:S(2)}) copy-start(f32[4,2,128]{2,1,0:T(2,128)} %param.24) | copy-start | bytes 12292
  19.3 7.9 %copy-start.15 = (f32[2,128]{1,0:T(2,128)S(1)}, f32[2,128]{1,0:T(2,128)}, u32[]{:S(2)}) copy-start(f32[2,128]{1,0:T(2,128)} %param.25) | copy-start | bytes 3076
  19.3 31.3 %all-to-all-start = ((bf16[32,200,128]{2,1,0:T(8,128)(2,1)}), bf16[32,200,128]{2,1,0:T(8,128)(2,1)S(1)}, u32[]{:S(2)}, u32[]{:S(2)}) async-start(bf16[32,200,128]{2,1,0:T(8,128)(2,1)} %shard_map.136), calls=%async_computation | async-start | bytes 3276800 | tf_op jit(solution)/shard_map/all_to_all | solution.py:358
  50.6 6.9 %copy-start.6 = (f32[16,128]{1,0:T(8,128)S(1)}, f32[16,128]{1,0:T(8,128)}, u32[]{:S(2)}) copy-start(f32[16,128]{1,0:T(8,128)} %pad_bitcast_fusion.group_taps_ref) | copy-start | bytes 24580
  50.6 6.9 %copy-start.11 = (f32[8,256]{1,0:T(8,128)S(1)}, f32[8,256]{1,0:T(8,128)}, u32[]{:S(2)}) copy-start(f32[8,256]{1,0:T(8,128)} %select_maximum_fusion.taps_ref) | copy-start | bytes 24580
  50.6 6.9 %collective-permute-start = (bf16[8,512]{1,0:T(8,128)(2,1)S(1)}, bf16[8,512]{1,0:T(8,128)(2,1)S(1)}, u32[]{:S(2)}, u32[]{:S(2)}) collective-permute-start(bf16[8,512]{1,0:T(8,128)(2,1)S(1)} %shard_map.137), channel_id=1, source_target_pairs={{0,32},{32,64},{64,96},{96,128},{128,160},{160,192},{192,224},{224... | collective-permute-start | bytes 24584 | tf_op jit(solution)/shard_map/ppermute | solution.py:354
  54.3 7.0 %copy-start.3 = (f32[8,1024]{1,0:T(8,128)}, f32[8,1024]{1,0:T(8,128)S(1)}, u32[]{:S(2)}) copy-start(f32[8,1024]{1,0:T(8,128)S(1)} %get-tuple-element.35.cum_ref) | copy-start | bytes 98308
  57.5 3.9 %copy-start.9 = (bf16[8,512]{1,0:T(8,128)(2,1)}, bf16[8,512]{1,0:T(8,128)(2,1)S(1)}, u32[]{:S(2)}) copy-start(bf16[8,512]{1,0:T(8,128)(2,1)S(1)} %collective-permute-done.halo_ref) | copy-start | bytes 24580
  61.4 0.7 copy-start.1
  62.1 0.6 copy-start.8
  62.7 9.5 %all-to-all-start.1 = ((bf16[4,72,128]{2,1,0:T(8,128)(2,1)}), bf16[4,72,128]{2,1,0:T(8,128)(2,1)S(1)}, u32[]{:S(2)}, u32[]{:S(2)}) async-start(bf16[4,72,128]{2,1,0:T(8,128)(2,1)} %copy-done.8), calls=%async_computation.1 | async-start | bytes 147456 | tf_op jit(solution)/shard_map/all_to_all | solution.py:358
  66.0 1.0 copy-start.2
  67.0 0.8 copy-start.4
  67.7 0.7 copy-start.7
  68.4 0.7 copy-start.10
  69.1 0.7 copy-start.13
  72.2 0.7 collective-permute-start.1
  72.9 0.7 collective-permute-start.2
  73.6 19.1 %collective-permute-start.3 = (bf16[64,128]{1,0:T(8,128)(2,1)S(1)}, bf16[64,128]{1,0:T(8,128)(2,1)S(1)}, u32[]{:S(2)}, u32[]{:S(2)}) collective-permute-start(bf16[64,128]{1,0:T(8,128)(2,1)S(1)} %shard_map.143), channel_id=1, source_target_pairs={{256,384},{257,385},{258,386},{259,387},{260,388},{261,389},{262,3... | collective-permute-start | bytes 49160 | tf_op jit(solution)/shard_map/ppermute | solution.py:455
  122.1 4.6 %collective-permute-start.5 = (bf16[256,2048]{1,0:T(8,128)(2,1)S(1)}, bf16[256,2048]{1,0:T(8,128)(2,1)S(1)}, u32[]{:S(2)}, u32[]{:S(2)}) collective-permute-start(bf16[256,2048]{1,0:T(8,128)(2,1)S(1)} %get-tuple-element.54), channel_id=1, source_target_pairs={{0,1},{1,0},{2,3},{3,2},{4,5},{5,4},{6,7},{7,6},{8,9},{9,8},{10,11... | collective-permute-start | bytes 3145736 | tf_op jit(solution)/shard_map/ppermute | solution.py:354
Sparse Core Ops, SparseCore 0:
  16.5 75.3 all-gather.1

commit v10 on v9

--- a/solution.py
+++ b/solution.py
@@ -210,19 +210,21 @@
         log = log + mine
     before_ref[8 * count :] = jnp.broadcast_to(log, (8, LANES))
     group_ref[...] = state
-    sent_ref[...] = state.astype(BF16)
+    sent_ref[:rows] = state.astype(BF16)
+    sent_ref[rows:] = in_terms(log)
 
 
 def extend(inbox_ref, before_ref, group_ref, sent_ref):
     grown = jnp.exp(before_ref[before_ref.shape[0] - 1 :])
-    sent_ref[...] = (grown * inbox_ref[...].astype(F32) + group_ref[...]).astype(BF16)
-
-
-def scan_far(inner_ref, before_ref, *refs):
-    starts_ref = refs[-1]
-    state = refs[0][...].astype(F32)
-    for ref in refs[1:-1]:
-        state = state + ref[...].astype(F32)
+    last = inbox_ref[: sent_ref.shape[0]].astype(F32)
+    sent_ref[...] = (grown * last + group_ref[...]).astype(BF16)
+
+
+def scan_far(last_ref, third_ref, second_ref, inner_ref, before_ref, starts_ref):
+    rows = third_ref.shape[0]
+    grown = jnp.exp(from_terms(last_ref[rows:]))
+    earlier = third_ref[...].astype(F32) + second_ref[...].astype(F32)
+    state = last_ref[:rows].astype(F32) + grown * earlier
     for i in range(inner_ref.shape[0]):
         grown = jnp.exp(before_ref[8 * i : 8 * i + 1])
         starts_ref[i] = (grown * state + inner_ref[i]).astype(BF16)
@@ -364,7 +366,7 @@
 ):
     xh, xl, ys, cs = (lax.axis_size(a) for a in PLANE)
     xs = xh * xl
-    zh, zl = (lax.axis_size(a) for a in Z)
+    _, zl = (lax.axis_size(a) for a in Z)
     plane = xs * ys * cs
     rows, inner = x_proj.shape
     cols = inner // plane
@@ -444,16 +446,15 @@
             shape(near, F32),
             shape((8 * zl + 8, LANES), F32),
             shape(near[1:], F32),
-            shape(near[1:], BF16),
+            shape((near[1] + 8, STATE), BF16),
         ),
         (near_in,),
     )
-    inboxes = []
-    for hop in range(zh - 1):
-        if hop:
-            ahead = call(extend, shape(near[1:], BF16), (inboxes[-1], before, group))
-        inboxes.append(lax.ppermute(ahead, "zh", [(hop, hop + 1)]))
-    starts = call(scan_far, shape(near, BF16), (inner, before, *inboxes))
+    last = lax.ppermute(ahead, "zh", [(0, 1), (2, 3)])
+    two = call(extend, shape(near[1:], BF16), (last, before, group))
+    third = lax.ppermute(two, "zh", [(1, 3)])
+    second = lax.ppermute(two, "zh", [(1, 2)])
+    starts = call(scan_far, shape(near, BF16), (last, third, second, inner, before))
     start = sent(starts, "zl").reshape(cols, STATE)
 
     def finish_all(*refs):

time: 156 us -> 160 us (1.026)
  waiting for transfers between devices: 48.6 us -> 51.8 us
    ppermute x3, waiting for transfers between devices: 17.9 us -> 21.1 us  [the longest x1 12.4 us: per_device(): third = lax.ppermute(two, 'zh', [(1, 3)])]
    pallas_call x14 -> x13, Pallas kernels: 16.6 us -> 16.6 us  [call(): pl.pallas_call(kernel, out_shape=outs, in_specs=[HBM if i in far else VME...]
  transfers between devices with their start and end apart: 9 -> 9, of which waited for: 6 -> 7; matrix products, arithmetic and copies ran while one was open for 2% -> 2% of each run, Pallas kernels for 7% -> 7%
where the time goes in v10:
time: 160 us; the launch traced here: 159 us
  waiting for transfers between devices  51.8 us (32%)
  blocking collectives  44.3 us (28%)
  starting transfers between devices  22.5 us (14%)
  Pallas kernels  16.6 us (10%)
  between operations  13.6 us (8%)
  local copies, waits for them, and re-layouts  9.02 us (6%)
    all_to_all x3, blocking collectives, sent(): return lax.all_to_all(array, axes, 0, 0, tiled=True)  44.3 us
    all_to_all x2, waiting for transfers between devices, sent(): return lax.all_to_all(array, axes, 0, 0, tiled=True)  21 us
    pallas_call x13, Pallas kernels, call(): pl.pallas_call(kernel, out_shape=outs, in_specs=[HBM if i in far else VME...  16.6 us
    ppermute x1, waiting for transfers between devices, per_device(): third = lax.ppermute(two, 'zh', [(1, 3)])  12.4 us
    all_to_all x2, starting transfers between devices, sent(): return lax.all_to_all(array, axes, 0, 0, tiled=True)  10.8 us
    ppermute x3, waiting for transfers between devices, shift(): return lax.ppermute(array, axis, pairs)  9.71 us
    ppermute x1, waiting for transfers between devices, per_device(): last = lax.ppermute(ahead, 'zh', [(0, 1), (2, 3)])  8.69 us
    ppermute x3, starting transfers between devices, shift(): return lax.ppermute(array, axis, pairs)  8.49 us
  transfers between devices with their start and end apart: 9, of which 7 were waited for; matrix products, arithmetic and copies ran while one was open for 2% of the time, Pallas kernels for 7%

profile of v10, /device:TPU:384, one launch (start us, length us, event | category | flops | bytes accessed | tf_op | source)
XLA Modules:
  0.0 158.6 jit_solution(4316807447677842483)
XLA Ops:
  6.5 3.5 %collective-permute-start.4 = (bf16[64,1024]{1,0:T(8,128)(2,1)}, bf16[64,1024]{1,0:T(8,128)(2,1)S(1)}, u32[]{:S(2)}, u32[]{:S(2)}) collective-permute-start(bf16[64,1024]{1,0:T(8,128)(2,1)} %bitcast.17), channel_id=1, source_target_pairs={{0,8},{8,0},{1,9},{9,1},{2,10},{10,2},{3,11},{11,3},{4,12},{12,4},... | collective-permute-start | bytes 393224 | tf_op jit(solution)/shard_map/ppermute | solution.py:356
  10.1 3.9 %collective-permute-done.4.other_ref = bf16[64,1024]{1,0:T(8,128)(2,1)S(1)} collective-permute-done((bf16[64,1024]{1,0:T(8,128)(2,1)}, bf16[64,1024]{1,0:T(8,128)(2,1)S(1)}, u32[]{:S(2)}, u32[]{:S(2)}) %collective-permute-start.4) | collective-permute-done | bytes 131104 | tf_op jit(solution)/shard_map/ppermute | solution.py:356
  14.0 0.9 copy-done.5
  14.9 0.7 copy-done.12
  15.6 0.8 shard_map.145
  16.4 2.9 %shard_map.136 = bf16[32,200,128]{2,1,0:T(8,128)(2,1)} custom-call(bf16[32,8192]{1,0:T(8,128)(2,1)} %x_far.1, bf16[32,8192]{1,0:T(8,128)(2,1)} %z_far.1, bf16[32,1024]{1,0:T(8,128)(2,1)} %b_far.1, bf16[32,1024]{1,0:T(8,128)(2,1)} %c_far.1, bf16[32,128]{1,0:T(8,128)(2,1)} %dt_far.1), custom_call_target="tpu_custom_call" | custom-call | flops 4194304 | bytes 1048576 | tf_op jit(solution)/shard_map/pallas_call | solution.py:26
  19.3 7.5 %all-to-all-start = ((bf16[32,200,128]{2,1,0:T(8,128)(2,1)}), bf16[32,200,128]{2,1,0:T(8,128)(2,1)S(1)}, u32[]{:S(2)}, u32[]{:S(2)}) async-start(bf16[32,200,128]{2,1,0:T(8,128)(2,1)} %shard_map.136), calls=%async_computation | async-start | bytes 3276800 | tf_op jit(solution)/shard_map/all_to_all | solution.py:360
  27.2 0.8 dynamic_slice.19
  29.8 20.8 %all-to-all-done.packed_ref = bf16[32,200,128]{2,1,0:T(8,128)(2,1)S(1)} async-done(((bf16[32,200,128]{2,1,0:T(8,128)(2,1)}), bf16[32,200,128]{2,1,0:T(8,128)(2,1)S(1)}, u32[]{:S(2)}, u32[]{:S(2)}) %all-to-all-start) | async-done | bytes 1638432 | tf_op jit(solution)/shard_map/all_to_all | solution.py:360
  50.6 3.1 %collective-permute-start = (bf16[8,512]{1,0:T(8,128)(2,1)S(1)}, bf16[8,512]{1,0:T(8,128)(2,1)S(1)}, u32[]{:S(2)}, u32[]{:S(2)}) collective-permute-start(bf16[8,512]{1,0:T(8,128)(2,1)S(1)} %shard_map.137), channel_id=1, source_target_pairs={{0,32},{32,64},{64,96},{96,128},{128,160},{160,192},{192,224},{224... | collective-permute-start | bytes 24584 | tf_op jit(solution)/shard_map/ppermute | solution.py:356
  54.3 3.2 %collective-permute-done.halo_ref = bf16[8,512]{1,0:T(8,128)(2,1)S(1)} collective-permute-done((bf16[8,512]{1,0:T(8,128)(2,1)S(1)}, bf16[8,512]{1,0:T(8,128)(2,1)S(1)}, u32[]{:S(2)}, u32[]{:S(2)}) %collective-permute-start) | collective-permute-done | bytes 8224 | tf_op jit(solution)/shard_map/ppermute | solution.py:356
  57.5 3.9 %shard_map.139 = (bf16[1024,256]{1,0:T(8,128)(2,1)S(1)}, bf16[1024,128]{1,0:T(8,128)(2,1)S(1)}, bf16[8,256,128]{2,1,0:T(8,128)(2,1)S(1)}, bf16[4,72,128]{2,1,0:T(8,128)(2,1)S(1)}) custom-call(bf16[32,200,128]{2,1,0:T(8,128)(2,1)S(1)} %all-to-all-done.packed_ref, bf16[8,512]{1,0:T(8,128)(2,1)S(1)} %collective-permute-done.halo_ref, f32[8,256]{1,0:T(8,128)S(1)} %copy-done.11, ...), custom_call_target="tpu_custom_call" | custom-call | flops 33554432 | bytes 1048576 | tf_op jit(solution)/shard_map/pallas_call | solution.py:26
  61.4 0.7 copy-done.1
  62.7 3.3 %all-to-all-start.1 = ((bf16[4,72,128]{2,1,0:T(8,128)(2,1)}), bf16[4,72,128]{2,1,0:T(8,128)(2,1)S(1)}, u32[]{:S(2)}, u32[]{:S(2)}) async-start(bf16[4,72,128]{2,1,0:T(8,128)(2,1)} %copy-done.8), calls=%async_computation.1 | async-start | bytes 147456 | tf_op jit(solution)/shard_map/all_to_all | solution.py:360
  66.0 0.9 copy-done.2
  67.0 0.8 copy-done.4
  67.7 0.7 copy-done.7
  68.4 0.7 copy-done.10
  69.1 0.7 copy-done.13
  69.8 2.1 %shard_map.140 = (bf16[1024,128]{1,0:T(8,128)(2,1)S(1)}, bf16[1024,256]{1,0:T(8,128)(2,1)S(1)}) custom-call(bf16[1024,256]{1,0:T(8,128)(2,1)S(1)} %get-tuple-element.38.xs_ref, bf16[1024,128]{1,0:T(8,128)(2,1)S(1)} %copy-done.2, bf16[1024,128]{1,0:T(8,128)(2,1)S(1)} %get-tuple-element.40.raw_ref, bf16[8,512]{1,0:T(8,128)(2,1)S(1)} %copy-done.10, ...), custom_call_target="tpu_custom_call" | custom-call | flops 134217728 | bytes 1048576 | tf_op jit(solution)/shard_map/pallas_call | solution.py:26
  72.2 1.3 collective-permute-start.1
  73.5 8.7 %collective-permute-done.1.inbox_ref.last_ref = bf16[72,128]{1,0:T(8,128)(2,1)S(1)} collective-permute-done((bf16[72,128]{1,0:T(8,128)(2,1)S(1)}, bf16[72,128]{1,0:T(8,128)(2,1)S(1)}, u32[]{:S(2)}, u32[]{:S(2)}) %collective-permute-start.1) | collective-permute-done | bytes 18464 | tf_op jit(solution)/shard_map/ppermute | solution.py:453
  82.2 1.3 collective-permute-start.2
  84.2 12.4 %collective-permute-done.2.third_ref = bf16[64,128]{1,0:T(8,128)(2,1)S(1)} collective-permute-done((bf16[64,128]{1,0:T(8,128)(2,1)S(1)}, bf16[64,128]{1,0:T(8,128)(2,1)S(1)}, u32[]{:S(2)}, u32[]{:S(2)}) %collective-permute-start.2) | collective-permute-done | bytes 16416 | tf_op jit(solution)/shard_map/ppermute | solution.py:455
  96.6 10.9 %all_to_all.25 = bf16[4,64,128]{2,1,0:T(8,128)(2,1)S(1)} all-to-all(bf16[4,64,128]{2,1,0:T(8,128)(2,1)S(1)} %shard_map.143), channel_id=1, replica_groups=mesh['zh'=4,'zl'=4,'xh'=2,'xl'=2,'y'=4,'c'=2] {'zl'}, dimensions={0} | all-to-all | bytes 131072 | tf_op jit(solution)/shard_map/all_to_all | solution.py:360
  107.5 1.0 shard_map.144
  108.5 13.3 %all_to_all.26.gated_ref = bf16[4,512,256]{2,1,0:T(8,128)(2,1)S(1)} all-to-all(bf16[4,512,256]{2,1,0:T(8,128)(2,1)S(1)} %shard_map.144), channel_id=1, replica_groups=mesh['zh'=4,'zl'=4,'xh'=2,'xl'=2,'y'=4,'c'=2] {'xh','xl'}, dimensions={0} | all-to-all | bytes 2097152 | tf_op jit(solution)/shard_map/all_to_all | solution.py:360
  121.8 4.2 %shard_map.146 = (bf16[256,2048]{1,0:T(8,128)(2,1)S(1)}, bf16[256,2048]{1,0:T(8,128)(2,1)S(1)}) custom-call(bf16[4,512,256]{2,1,0:T(8,128)(2,1)S(1)} %all_to_all.26.gated_ref, bf16[2048,1024]{1,0:T(8,128)(2,1)} %all-gather.2.cloned.1.call-done.weights_far), custom_call_target="tpu_custom_call" | custom-call | flops 1073741824 | bytes 1048576 | tf_op jit(solution)/shard_map/pallas_call | solution.py:26
  126.1 1.9 %collective-permute-start.5 = (bf16[256,2048]{1,0:T(8,128)(2,1)S(1)}, bf16[256,2048]{1,0:T(8,128)(2,1)S(1)}, u32[]{:S(2)}, u32[]{:S(2)}) collective-permute-start(bf16[256,2048]{1,0:T(8,128)(2,1)S(1)} %get-tuple-element.54), channel_id=1, source_target_pairs={{0,1},{1,0},{2,3},{3,2},{4,5},{5,4},{6,7},{7,6},{8,9},{9,8},{10,11... | collective-permute-start | bytes 3145736 | tf_op jit(solution)/shard_map/ppermute | solution.py:356
  128.0 2.6 %collective-permute-done.5.other_ref = bf16[256,2048]{1,0:T(8,128)(2,1)S(1)} collective-permute-done((bf16[256,2048]{1,0:T(8,128)(2,1)S(1)}, bf16[256,2048]{1,0:T(8,128)(2,1)S(1)}, u32[]{:S(2)}, u32[]{:S(2)}) %collective-permute-start.5) | collective-permute-done | bytes 1048608 | tf_op jit(solution)/shard_map/ppermute | solution.py:356
  130.9 20.1 %all_to_all.27.refs_0_ = bf16[8,32,2048]{2,1,0:T(8,128)(2,1)S(1)} all-to-all(bf16[8,32,2048]{2,1,0:T(8,128)(2,1)S(1)} %bitcast.15), channel_id=1, replica_groups=mesh['zh'=4,'zl'=4,'xh'=2,'xl'=2,'y'=4,'c'=2] {'xh','y'}, dimensions={0} | all-to-all | bytes 2097152 | tf_op jit(solution)/shard_map/all_to_all | solution.py:360
  150.9 0.8 shard_map.148
  (54 shorter events, 4.8 us)
Async XLA Ops:
  6.5 22.0 %copy-start = (f32[4,1024]{1,0:T(4,128)S(1)}, f32[4,1024]{1,0:T(4,128)}, u32[]{:S(2)}) copy-start(f32[4,1024]{1,0:T(4,128)} %param.22) | copy-start | bytes 49156
  6.5 115.3 %all-gather.2.cloned.1.call-start = ((), (), s32[]{:S(2)}) async-start(), calls=%async_computation.5 | async-start | bytes 4456448 | tf_op jit(solution)/shard_map/all_gather | solution.py:388
  6.5 7.5 %collective-permute-start.4 = (bf16[64,1024]{1,0:T(8,128)(2,1)}, bf16[64,1024]{1,0:T(8,128)(2,1)S(1)}, u32[]{:S(2)}, u32[]{:S(2)}) collective-permute-start(bf16[64,1024]{1,0:T(8,128)(2,1)} %bitcast.17), channel_id=1, source_target_pairs={{0,8},{8,0},{1,9},{9,1},{2,10},{10,2},{3,11},{11,3},{4,12},{12,4},... | collective-permute-start | bytes 393224 | tf_op jit(solution)/shard_map/ppermute | solution.py:356
  14.0 0.9 copy-start.5
  14.9 0.7 copy-start.12
  19.3 7.5 %copy-start.17 = (f32[16]{0:T(128)S(1)}, f32[16]{0:T(128)}, u32[]{:S(2)}) copy-start(f32[16]{0:T(128)} %param.20) | copy-start | bytes 196
  19.3 7.5 %copy-start.16 = (f32[16]{0:T(128)S(1)}, f32[16]{0:T(128)}, u32[]{:S(2)}) copy-start(f32[16]{0:T(128)} %param.19) | copy-start | bytes 196
  19.3 7.8 %copy-start.18 = (f32[16]{0:T(128)S(1)}, f32[16]{0:T(128)}, u32[]{:S(2)}) copy-start(f32[16]{0:T(128)} %param.21) | copy-start | bytes 196
  19.3 7.9 %copy-start.14 = (f32[4,2,128]{2,1,0:T(2,128)S(1)}, f32[4,2,128]{2,1,0:T(2,128)}, u32[]{:S(2)}) copy-start(f32[4,2,128]{2,1,0:T(2,128)} %param.24) | copy-start | bytes 12292
  19.3 7.9 %copy-start.15 = (f32[2,128]{1,0:T(2,128)S(1)}, f32[2,128]{1,0:T(2,128)}, u32[]{:S(2)}) copy-start(f32[2,128]{1,0:T(2,128)} %param.25) | copy-start | bytes 3076
  19.3 31.3 %all-to-all-start = ((bf16[32,200,128]{2,1,0:T(8,128)(2,1)}), bf16[32,200,128]{2,1,0:T(8,128)(2,1)S(1)}, u32[]{:S(2)}, u32[]{:S(2)}) async-start(bf16[32,200,128]{2,1,0:T(8,128)(2,1)} %shard_map.136), calls=%async_computation | async-start | bytes 3276800 | tf_op jit(solution)/shard_map/all_to_all | solution.py:360
  50.6 6.9 %copy-start.6 = (f32[16,128]{1,0:T(8,128)S(1)}, f32[16,128]{1,0:T(8,128)}, u32[]{:S(2)}) copy-start(f32[16,128]{1,0:T(8,128)} %pad_bitcast_fusion.group_taps_ref) | copy-start | bytes 24580
  50.6 6.9 %copy-start.11 = (f32[8,256]{1,0:T(8,128)S(1)}, f32[8,256]{1,0:T(8,128)}, u32[]{:S(2)}) copy-start(f32[8,256]{1,0:T(8,128)} %select_maximum_fusion.taps_ref) | copy-start | bytes 24580
  50.6 6.9 %collective-permute-start = (bf16[8,512]{1,0:T(8,128)(2,1)S(1)}, bf16[8,512]{1,0:T(8,128)(2,1)S(1)}, u32[]{:S(2)}, u32[]{:S(2)}) collective-permute-start(bf16[8,512]{1,0:T(8,128)(2,1)S(1)} %shard_map.137), channel_id=1, source_target_pairs={{0,32},{32,64},{64,96},{96,128},{128,160},{160,192},{192,224},{224... | collective-permute-start | bytes 24584 | tf_op jit(solution)/shard_map/ppermute | solution.py:356
  54.3 7.0 %copy-start.3 = (f32[8,1024]{1,0:T(8,128)}, f32[8,1024]{1,0:T(8,128)S(1)}, u32[]{:S(2)}) copy-start(f32[8,1024]{1,0:T(8,128)S(1)} %get-tuple-element.35.cum_ref) | copy-start | bytes 98308
  57.5 3.9 %copy-start.9 = (bf16[8,512]{1,0:T(8,128)(2,1)}, bf16[8,512]{1,0:T(8,128)(2,1)S(1)}, u32[]{:S(2)}) copy-start(bf16[8,512]{1,0:T(8,128)(2,1)S(1)} %collective-permute-done.halo_ref) | copy-start | bytes 24580
  61.4 0.7 copy-start.1
  62.1 0.6 copy-start.8
  62.7 9.5 %all-to-all-start.1 = ((bf16[4,72,128]{2,1,0:T(8,128)(2,1)}), bf16[4,72,128]{2,1,0:T(8,128)(2,1)S(1)}, u32[]{:S(2)}, u32[]{:S(2)}) async-start(bf16[4,72,128]{2,1,0:T(8,128)(2,1)} %copy-done.8), calls=%async_computation.1 | async-start | bytes 147456 | tf_op jit(solution)/shard_map/all_to_all | solution.py:360
  66.0 1.0 copy-start.2
  67.0 0.8 copy-start.4
  67.7 0.7 copy-start.7
  68.4 0.7 copy-start.10
  69.1 0.7 copy-start.13
  72.2 10.0 %collective-permute-start.1 = (bf16[72,128]{1,0:T(8,128)(2,1)S(1)}, bf16[72,128]{1,0:T(8,128)(2,1)S(1)}, u32[]{:S(2)}, u32[]{:S(2)}) collective-permute-start(bf16[72,128]{1,0:T(8,128)(2,1)S(1)} %get-tuple-element.46), channel_id=1, source_target_pairs={{0,128},{256,384},{1,129},{257,385},{2,130},{258,386},{3,131},{259... | collective-permute-start | bytes 55304 | tf_op jit(solution)/shard_map/ppermute | solution.py:453
  82.2 14.3 %collective-permute-start.2 = (bf16[64,128]{1,0:T(8,128)(2,1)S(1)}, bf16[64,128]{1,0:T(8,128)(2,1)S(1)}, u32[]{:S(2)}, u32[]{:S(2)}) collective-permute-start(bf16[64,128]{1,0:T(8,128)(2,1)S(1)} %shard_map.142), channel_id=1, source_target_pairs={{128,384},{129,385},{130,386},{131,387},{132,388},{133,389},{134,3... | collective-permute-start | bytes 49160 | tf_op jit(solution)/shard_map/ppermute | solution.py:455
  83.5 13.0 %collective-permute-start.3 = (bf16[64,128]{1,0:T(8,128)(2,1)S(1)}, bf16[64,128]{1,0:T(8,128)(2,1)S(1)}, u32[]{:S(2)}, u32[]{:S(2)}) collective-permute-start(bf16[64,128]{1,0:T(8,128)(2,1)S(1)} %shard_map.142), channel_id=1, source_target_pairs={{128,256},{129,257},{130,258},{131,259},{132,260},{133,261},{134,2... | collective-permute-start | bytes 49160 | tf_op jit(solution)/shard_map/ppermute | solution.py:456
  126.1 4.6 %collective-permute-start.5 = (bf16[256,2048]{1,0:T(8,128)(2,1)S(1)}, bf16[256,2048]{1,0:T(8,128)(2,1)S(1)}, u32[]{:S(2)}, u32[]{:S(2)}) collective-permute-start(bf16[256,2048]{1,0:T(8,128)(2,1)S(1)} %get-tuple-element.54), channel_id=1, source_target_pairs={{0,1},{1,0},{2,3},{3,2},{4,5},{5,4},{6,7},{7,6},{8,9},{9,8},{10,11... | collective-permute-start | bytes 3145736 | tf_op jit(solution)/shard_map/ppermute | solution.py:356
Sparse Core Ops, SparseCore 0:
  16.5 76.2 all-gather.1

commit v11 on v9

--- a/solution.py
+++ b/solution.py
@@ -173,7 +173,8 @@
             xs = conv(padded, taps, taps_ref[4:5, lo : lo + LANES], k, lo)
             xs_ref[part, lo : lo + LANES] = xs
             weighted = (xs.astype(F32) * by_head(scale, chunk, left)).astype(BF16)
-            held_ref[k, lo : lo + LANES] = states[chunk].astype(BF16)
+            if k > 0:
+                held_ref[k - 1, lo : lo + LANES] = states[chunk].astype(BF16)
             states[chunk] = by_head(decay, chunk, top) * states[chunk] + tn(weighted, b)
     count = sent_ref.shape[0]
     rows = cols // count
@@ -262,7 +263,7 @@
             y1 = jnp.dot(mix(2 * chunk + 1), xs, preferred_element_type=F32)
             y = jnp.where(left, y0, y1) + by_head(skip_ref[...], chunk, left) * xs.astype(F32)
             if k > 0:
-                y = y + nt(c, held_ref[k, lo : lo + LANES]) * by_head(grown, chunk, left)
+                y = y + nt(c, held_ref[k - 1, lo : lo + LANES]) * by_head(grown, chunk, left)
             y_ref[part, lo : lo + LANES] = y.astype(BF16)
 
 
@@ -422,7 +423,7 @@
         (
             shape((tokens, cols), BF16),
             shape((tokens, LANES), BF16),
-            shape((tokens // SPAN, cols, STATE), BF16),
+            shape((tokens // SPAN - 1, cols, STATE), BF16),
             shape((zl, cols // zl + 8, STATE), BF16),
         ),
         (packed, halo, taps, group_taps, dt, cum, sums),

time: 156 us -> 153 us (0.981)
  waiting for transfers between devices: 48.6 us -> 53.1 us
  local copies, waits for them, and re-layouts: 9.02 us -> 5.01 us
  blocking collectives: 44.3 us -> 42.5 us
    all_to_all x2, waiting for transfers between devices: 21 us -> 25.7 us  [sent(): return lax.all_to_all(array, axes, 0, 0, tiled=True)]
    unnamed x39 -> x23, local copies, waits for them, and re-layouts: 6.74 us -> 3.9 us
    all_to_all x3, blocking collectives: 44.3 us -> 42.5 us  [sent(): return lax.all_to_all(array, axes, 0, 0, tiled=True)]
  transfers between devices with their start and end apart: 9 -> 9, of which waited for: 6 -> 6; matrix products, arithmetic and copies ran while one was open for 2% -> 1% of each run, Pallas kernels for 7% -> 7%
where the time goes in v11:
time: 153 us
  waiting for transfers between devices  53.1 us (35%)
  blocking collectives  42.5 us (28%)
  starting transfers between devices  21.7 us (14%)
  Pallas kernels  16.7 us (11%)
  between operations  13.7 us (9%)
  local copies, waits for them, and re-layouts  5.01 us (3%)
    all_to_all x3, blocking collectives, sent(): return lax.all_to_all(array, axes, 0, 0, tiled=True)  42.5 us
    all_to_all x2, waiting for transfers between devices, sent(): return lax.all_to_all(array, axes, 0, 0, tiled=True)  25.7 us
    ppermute x3, waiting for transfers between devices, per_device(): inboxes.append(lax.ppermute(ahead, 'zh', [(hop, hop + 1)]))  17.6 us
    pallas_call x14, Pallas kernels, call(): pl.pallas_call(kernel, out_shape=outs, in_specs=[HBM if i in far else VME...  16.7 us
    all_to_all x2, starting transfers between devices, sent(): return lax.all_to_all(array, axes, 0, 0, tiled=True)  10.8 us
    ppermute x3, waiting for transfers between devices, shift(): return lax.ppermute(array, axis, pairs)  9.8 us
    ppermute x3, starting transfers between devices, shift(): return lax.ppermute(array, axis, pairs)  8.35 us
    unnamed x23, local copies, waits for them, and re-layouts  3.9 us
  transfers between devices with their start and end apart: 9, of which 6 were waited for; matrix products, arithmetic and copies ran while one was open for 1% of the time, Pallas kernels for 7%

profile of v11, /device:TPU:384, one launch (start us, length us, event | category | flops | bytes accessed | tf_op | source)
XLA Modules:
  0.0 152.7 jit_solution(8888304671039876665)
XLA Ops:
  6.5 3.5 %collective-permute-start.4 = (bf16[64,1024]{1,0:T(8,128)(2,1)}, bf16[64,1024]{1,0:T(8,128)(2,1)S(1)}, u32[]{:S(2)}, u32[]{:S(2)}) collective-permute-start(bf16[64,1024]{1,0:T(8,128)(2,1)} %bitcast.17), channel_id=1, source_target_pairs={{0,8},{8,0},{1,9},{9,1},{2,10},{10,2},{3,11},{11,3},{4,12},{12,4},... | collective-permute-start | bytes 393224 | tf_op jit(solution)/shard_map/ppermute | solution.py:355
  10.1 3.9 %collective-permute-done.4.other_ref = bf16[64,1024]{1,0:T(8,128)(2,1)S(1)} collective-permute-done((bf16[64,1024]{1,0:T(8,128)(2,1)}, bf16[64,1024]{1,0:T(8,128)(2,1)S(1)}, u32[]{:S(2)}, u32[]{:S(2)}) %collective-permute-start.4) | collective-permute-done | bytes 131104 | tf_op jit(solution)/shard_map/ppermute | solution.py:355
  14.0 0.9 copy-done.3
  14.9 0.7 copy-done.5
  15.6 0.8 shard_map.146
  16.4 2.9 %shard_map.136 = bf16[32,200,128]{2,1,0:T(8,128)(2,1)} custom-call(bf16[32,8192]{1,0:T(8,128)(2,1)} %x_far.1, bf16[32,8192]{1,0:T(8,128)(2,1)} %z_far.1, bf16[32,1024]{1,0:T(8,128)(2,1)} %b_far.1, bf16[32,1024]{1,0:T(8,128)(2,1)} %c_far.1, bf16[32,128]{1,0:T(8,128)(2,1)} %dt_far.1), custom_call_target="tpu_custom_call" | custom-call | flops 4194304 | bytes 1048576 | tf_op jit(solution)/shard_map/pallas_call | solution.py:26
  19.4 7.5 %all-to-all-start = ((bf16[32,200,128]{2,1,0:T(8,128)(2,1)}), bf16[32,200,128]{2,1,0:T(8,128)(2,1)S(1)}, u32[]{:S(2)}, u32[]{:S(2)}) async-start(bf16[32,200,128]{2,1,0:T(8,128)(2,1)} %shard_map.136), calls=%async_computation | async-start | bytes 3276800 | tf_op jit(solution)/shard_map/all_to_all | solution.py:359
  27.2 0.8 dynamic_slice.19
  28.1 22.5 %all-to-all-done.packed_ref = bf16[32,200,128]{2,1,0:T(8,128)(2,1)S(1)} async-done(((bf16[32,200,128]{2,1,0:T(8,128)(2,1)}), bf16[32,200,128]{2,1,0:T(8,128)(2,1)S(1)}, u32[]{:S(2)}, u32[]{:S(2)}) %all-to-all-start) | async-done | bytes 1638432 | tf_op jit(solution)/shard_map/all_to_all | solution.py:359
  50.6 2.9 %collective-permute-start = (bf16[8,512]{1,0:T(8,128)(2,1)S(1)}, bf16[8,512]{1,0:T(8,128)(2,1)S(1)}, u32[]{:S(2)}, u32[]{:S(2)}) collective-permute-start(bf16[8,512]{1,0:T(8,128)(2,1)S(1)} %shard_map.137), channel_id=1, source_target_pairs={{0,32},{32,64},{64,96},{96,128},{128,160},{160,192},{192,224},{224... | collective-permute-start | bytes 24584 | tf_op jit(solution)/shard_map/ppermute | solution.py:355
  53.5 0.7 shard_map.138
  54.2 3.2 %collective-permute-done.halo_ref = bf16[8,512]{1,0:T(8,128)(2,1)S(1)} collective-permute-done((bf16[8,512]{1,0:T(8,128)(2,1)S(1)}, bf16[8,512]{1,0:T(8,128)(2,1)S(1)}, u32[]{:S(2)}, u32[]{:S(2)}) %collective-permute-start) | collective-permute-done | bytes 8224 | tf_op jit(solution)/shard_map/ppermute | solution.py:355
  57.5 3.9 %shard_map.139 = (bf16[1024,256]{1,0:T(8,128)(2,1)S(1)}, bf16[1024,128]{1,0:T(8,128)(2,1)S(1)}, bf16[7,256,128]{2,1,0:T(8,128)(2,1)S(1)}, bf16[4,72,128]{2,1,0:T(8,128)(2,1)S(1)}) custom-call(bf16[32,200,128]{2,1,0:T(8,128)(2,1)S(1)} %all-to-all-done.packed_ref, bf16[8,512]{1,0:T(8,128)(2,1)S(1)} %collective-permute-done.halo_ref, ...), custom_call_target="tpu_custom_call" | custom-call | flops 33554432 | bytes 1048576 | tf_op jit(solution)/shard_map/pallas_call | solution.py:26
  61.3 0.7 copy-done.1
  62.0 0.6 copy-done.4
  62.7 3.3 %all-to-all-start.1 = ((bf16[4,72,128]{2,1,0:T(8,128)(2,1)}), bf16[4,72,128]{2,1,0:T(8,128)(2,1)S(1)}, u32[]{:S(2)}, u32[]{:S(2)}) async-start(bf16[4,72,128]{2,1,0:T(8,128)(2,1)} %copy-done.4), calls=%async_computation.1 | async-start | bytes 147456 | tf_op jit(solution)/shard_map/all_to_all | solution.py:359
  66.0 0.9 copy-done.2
  66.9 2.1 %shard_map.140 = (bf16[1024,128]{1,0:T(8,128)(2,1)S(1)}, bf16[1024,256]{1,0:T(8,128)(2,1)S(1)}) custom-call(bf16[1024,256]{1,0:T(8,128)(2,1)S(1)} %get-tuple-element.38.xs_ref, bf16[1024,128]{1,0:T(8,128)(2,1)S(1)} %copy-done.2, bf16[1024,128]{1,0:T(8,128)(2,1)S(1)} %get-tuple-element.40.raw_ref, bf16[8,512]{1,0:T(8,128)(2,1)S(1)} %collective-permute-done.halo_ref, ...), custom_call_target="tpu_custom_call" | custom-call | flops 134217728 | bytes 1048576 | tf_op jit(solution)/shard_map/pallas_call | solution.py:26
  69.0 3.2 %all-to-all-done.1.inbox_ref = bf16[4,72,128]{2,1,0:T(8,128)(2,1)S(1)} async-done(((bf16[4,72,128]{2,1,0:T(8,128)(2,1)}), bf16[4,72,128]{2,1,0:T(8,128)(2,1)S(1)}, u32[]{:S(2)}, u32[]{:S(2)}) %all-to-all-start.1) | async-done | bytes 73760 | tf_op jit(solution)/shard_map/all_to_all | solution.py:359
  72.2 0.7 collective-permute-start.1
  72.9 0.7 collective-permute-start.2
  73.6 1.3 collective-permute-start.3
  74.9 17.6 %collective-permute-done.3.refs_2_ = bf16[64,128]{1,0:T(8,128)(2,1)S(1)} collective-permute-done((bf16[64,128]{1,0:T(8,128)(2,1)S(1)}, bf16[64,128]{1,0:T(8,128)(2,1)S(1)}, u32[]{:S(2)}, u32[]{:S(2)}) %collective-permute-start.3) | collective-permute-done | bytes 16416 | tf_op jit(solution)/shard_map/ppermute | solution.py:456
  92.5 9.1 %all_to_all.25 = bf16[4,64,128]{2,1,0:T(8,128)(2,1)S(1)} all-to-all(bf16[4,64,128]{2,1,0:T(8,128)(2,1)S(1)} %shard_map.144), channel_id=1, replica_groups=mesh['zh'=4,'zl'=4,'xh'=2,'xl'=2,'y'=4,'c'=2] {'zl'}, dimensions={0} | all-to-all | bytes 131072 | tf_op jit(solution)/shard_map/all_to_all | solution.py:359
  101.6 1.0 shard_map.145
  102.6 13.3 %all_to_all.26.gated_ref = bf16[4,512,256]{2,1,0:T(8,128)(2,1)S(1)} all-to-all(bf16[4,512,256]{2,1,0:T(8,128)(2,1)S(1)} %shard_map.145), channel_id=1, replica_groups=mesh['zh'=4,'zl'=4,'xh'=2,'xl'=2,'y'=4,'c'=2] {'xh','xl'}, dimensions={0} | all-to-all | bytes 2097152 | tf_op jit(solution)/shard_map/all_to_all | solution.py:359
  115.9 4.2 %shard_map.147 = (bf16[256,2048]{1,0:T(8,128)(2,1)S(1)}, bf16[256,2048]{1,0:T(8,128)(2,1)S(1)}) custom-call(bf16[4,512,256]{2,1,0:T(8,128)(2,1)S(1)} %all_to_all.26.gated_ref, bf16[2048,1024]{1,0:T(8,128)(2,1)} %all-gather.2.cloned.1.call-done.weights_far), custom_call_target="tpu_custom_call" | custom-call | flops 1073741824 | bytes 1048576 | tf_op jit(solution)/shard_map/pallas_call | solution.py:26
  120.1 1.9 %collective-permute-start.5 = (bf16[256,2048]{1,0:T(8,128)(2,1)S(1)}, bf16[256,2048]{1,0:T(8,128)(2,1)S(1)}, u32[]{:S(2)}, u32[]{:S(2)}) collective-permute-start(bf16[256,2048]{1,0:T(8,128)(2,1)S(1)} %get-tuple-element.54), channel_id=1, source_target_pairs={{0,1},{1,0},{2,3},{3,2},{4,5},{5,4},{6,7},{7,6},{8,9},{9,8},{10,11... | collective-permute-start | bytes 3145736 | tf_op jit(solution)/shard_map/ppermute | solution.py:355
  122.1 2.6 %collective-permute-done.5.other_ref = bf16[256,2048]{1,0:T(8,128)(2,1)S(1)} collective-permute-done((bf16[256,2048]{1,0:T(8,128)(2,1)S(1)}, bf16[256,2048]{1,0:T(8,128)(2,1)S(1)}, u32[]{:S(2)}, u32[]{:S(2)}) %collective-permute-start.5) | collective-permute-done | bytes 1048608 | tf_op jit(solution)/shard_map/ppermute | solution.py:355
  124.7 0.2 shard_map.148
  124.9 20.1 %all_to_all.27.refs_0_ = bf16[8,32,2048]{2,1,0:T(8,128)(2,1)S(1)} all-to-all(bf16[8,32,2048]{2,1,0:T(8,128)(2,1)S(1)} %bitcast.15), channel_id=1, replica_groups=mesh['zh'=4,'zl'=4,'xh'=2,'xl'=2,'y'=4,'c'=2] {'xh','y'}, dimensions={0} | all-to-all | bytes 2097152 | tf_op jit(solution)/shard_map/all_to_all | solution.py:359
  145.1 0.8 shard_map.149
  (39 shorter events, 0.6 us)
Async XLA Ops:
  6.5 21.5 %copy-start = (f32[4,1024]{1,0:T(4,128)S(1)}, f32[4,1024]{1,0:T(4,128)}, u32[]{:S(2)}) copy-start(f32[4,1024]{1,0:T(4,128)} %param.22) | copy-start | bytes 49156
  6.5 109.4 %all-gather.2.cloned.1.call-start = ((), (), s32[]{:S(2)}) async-start(), calls=%async_computation.5 | async-start | bytes 4456448 | tf_op jit(solution)/shard_map/all_gather | solution.py:387
  6.5 7.5 %collective-permute-start.4 = (bf16[64,1024]{1,0:T(8,128)(2,1)}, bf16[64,1024]{1,0:T(8,128)(2,1)S(1)}, u32[]{:S(2)}, u32[]{:S(2)}) collective-permute-start(bf16[64,1024]{1,0:T(8,128)(2,1)} %bitcast.17), channel_id=1, source_target_pairs={{0,8},{8,0},{1,9},{9,1},{2,10},{10,2},{3,11},{11,3},{4,12},{12,4},... | collective-permute-start | bytes 393224 | tf_op jit(solution)/shard_map/ppermute | solution.py:355
  14.0 0.9 copy-start.3
  14.9 0.7 copy-start.5
  19.3 7.5 %copy-start.9 = (f32[16]{0:T(128)S(1)}, f32[16]{0:T(128)}, u32[]{:S(2)}) copy-start(f32[16]{0:T(128)} %param.20) | copy-start | bytes 196
  19.3 7.5 %copy-start.8 = (f32[16]{0:T(128)S(1)}, f32[16]{0:T(128)}, u32[]{:S(2)}) copy-start(f32[16]{0:T(128)} %param.19) | copy-start | bytes 196
  19.3 7.8 %copy-start.10 = (f32[16]{0:T(128)S(1)}, f32[16]{0:T(128)}, u32[]{:S(2)}) copy-start(f32[16]{0:T(128)} %param.21) | copy-start | bytes 196
  19.3 7.9 %copy-start.6 = (f32[4,2,128]{2,1,0:T(2,128)S(1)}, f32[4,2,128]{2,1,0:T(2,128)}, u32[]{:S(2)}) copy-start(f32[4,2,128]{2,1,0:T(2,128)} %param.24) | copy-start | bytes 12292
  19.3 7.9 %copy-start.7 = (f32[2,128]{1,0:T(2,128)S(1)}, f32[2,128]{1,0:T(2,128)}, u32[]{:S(2)}) copy-start(f32[2,128]{1,0:T(2,128)} %param.25) | copy-start | bytes 3076
  19.4 31.3 %all-to-all-start = ((bf16[32,200,128]{2,1,0:T(8,128)(2,1)}), bf16[32,200,128]{2,1,0:T(8,128)(2,1)S(1)}, u32[]{:S(2)}, u32[]{:S(2)}) async-start(bf16[32,200,128]{2,1,0:T(8,128)(2,1)} %shard_map.136), calls=%async_computation | async-start | bytes 3276800 | tf_op jit(solution)/shard_map/all_to_all | solution.py:359
  50.6 6.8 %collective-permute-start = (bf16[8,512]{1,0:T(8,128)(2,1)S(1)}, bf16[8,512]{1,0:T(8,128)(2,1)S(1)}, u32[]{:S(2)}, u32[]{:S(2)}) collective-permute-start(bf16[8,512]{1,0:T(8,128)(2,1)S(1)} %shard_map.137), channel_id=1, source_target_pairs={{0,32},{32,64},{64,96},{96,128},{128,160},{160,192},{192,224},{224... | collective-permute-start | bytes 24584 | tf_op jit(solution)/shard_map/ppermute | solution.py:355
  61.3 0.7 copy-start.1
  62.0 0.6 copy-start.4
  62.7 9.5 %all-to-all-start.1 = ((bf16[4,72,128]{2,1,0:T(8,128)(2,1)}), bf16[4,72,128]{2,1,0:T(8,128)(2,1)S(1)}, u32[]{:S(2)}, u32[]{:S(2)}) async-start(bf16[4,72,128]{2,1,0:T(8,128)(2,1)} %copy-done.4), calls=%async_computation.1 | async-start | bytes 147456 | tf_op jit(solution)/shard_map/all_to_all | solution.py:359
  65.9 1.0 copy-start.2
  72.2 0.7 collective-permute-start.1
  72.9 0.7 collective-permute-start.2
  73.6 18.9 %collective-permute-start.3 = (bf16[64,128]{1,0:T(8,128)(2,1)S(1)}, bf16[64,128]{1,0:T(8,128)(2,1)S(1)}, u32[]{:S(2)}, u32[]{:S(2)}) collective-permute-start(bf16[64,128]{1,0:T(8,128)(2,1)S(1)} %shard_map.143), channel_id=1, source_target_pairs={{256,384},{257,385},{258,386},{259,387},{260,388},{261,389},{262,3... | collective-permute-start | bytes 49160 | tf_op jit(solution)/shard_map/ppermute | solution.py:456
  120.1 4.6 %collective-permute-start.5 = (bf16[256,2048]{1,0:T(8,128)(2,1)S(1)}, bf16[256,2048]{1,0:T(8,128)(2,1)S(1)}, u32[]{:S(2)}, u32[]{:S(2)}) collective-permute-start(bf16[256,2048]{1,0:T(8,128)(2,1)S(1)} %get-tuple-element.54), channel_id=1, source_target_pairs={{0,1},{1,0},{2,3},{3,2},{4,5},{5,4},{6,7},{7,6},{8,9},{9,8},{10,11... | collective-permute-start | bytes 3145736 | tf_op jit(solution)/shard_map/ppermute | solution.py:355
Sparse Core Ops, SparseCore 0:
  16.5 75.3 all-gather.1
